TPU v7x, 8 devices: a whole 2x2x1 slice. The times are simulated.
8 devices in a mesh: rep: 1 (over z), tp: 2 (over y), sp: 4 (over x, core).
Axes of the slice: x: 2, y: 2, z: 1, core: 2. Of those that a mesh axis runs over, the one named last changes fastest.
Arguments:
- x_in: bfloat16 [4096, 3072], P(('rep', 'sp'))
- positions: int32 [4096], P(('rep', 'sp'))
- segments: int32 [4096], P(('rep', 'sp'))
- gain_attn: float32 [3072], replicated
- w_q: bfloat16 [3072, 3072], P(None, 'tp')
- w_k: bfloat16 [3072, 1024], P(None, 'tp')
- w_v: bfloat16 [3072, 1024], P(None, 'tp')
- w_o: bfloat16 [3072, 3072], P('tp')
- gain_mlp: float32 [3072], replicated
- w_gate: bfloat16 [3072, 8192], P(None, 'tp')
- w_up: bfloat16 [3072, 8192], P(None, 'tp')
- w_down: bfloat16 [8192, 3072], P('tp')
Outputs:
- output 1: bfloat16 [4096, 3072], P(('rep', 'sp'))
- output 2: bfloat16 [4096, 8, 128], P('rep', ('tp', 'sp'))
- output 3: bfloat16 [4096, 8, 128], P('rep', ('tp', 'sp'))
All inputs are finite; a program needn't handle non-finite values.
Results may differ from a plain program's by a relative error of at most 0.00699993.
Values are sent between devices in bfloat16 or wider.
A program may use at most 1 GiB of HBM per device.

v0:
```python
import functools
import jax
import jax.numpy as jnp
from jax import lax
from jax.experimental import pallas as pl
from jax.experimental.pallas import tpu as pltpu
from jax.sharding import PartitionSpec as P


HEAD_DIM = 128
HALF = HEAD_DIM // 2
ROPE_BASE = 500000.0
NORM_EPS = 1e-5
LOG2E = 1.4426950408889634
BF16 = jnp.bfloat16
F32 = jnp.float32

CHUNKS = 4
Q_BLOCK = 256
K_BLOCK = 1024
FF_BLOCK = 512
MASKED = -1e30


def params(semantics, mib):
    return pltpu.CompilerParams(dimension_semantics=semantics, vmem_limit_bytes=mib << 20)


def dot(a, b):
    return jnp.dot(a, b, preferred_element_type=F32)


def normed(x, gain):
    mean_sq = jnp.mean(x * x, axis=-1, keepdims=True)
    return (x * lax.rsqrt(mean_sq + NORM_EPS) * gain).astype(BF16)


def rope_tables(positions):
    inv_freq = jnp.power(jnp.float32(ROPE_BASE), -jnp.arange(HALF, dtype=F32) * (2.0 / HEAD_DIM))
    angles = positions.astype(F32)[:, None] * inv_freq
    cos_t, sin_t = jnp.cos(angles), jnp.sin(angles)
    return jnp.concatenate([cos_t, cos_t], axis=-1), jnp.concatenate([-sin_t, sin_t], axis=-1)


def store_rotated(out_ref, rows, t_f32, cos_t, sin_t):
    for head in range(t_f32.shape[1] // HEAD_DIM):
        cols = slice(head * HEAD_DIM, (head + 1) * HEAD_DIM)
        t_head = t_f32[:, cols]
        out_ref[rows, cols] = (t_head * cos_t + pltpu.roll(t_head, HALF, 1) * sin_t).astype(BF16)


def kv_kernel(x_ref, gain_ref, wk_ref, wv_ref, cos_ref, sin_ref, u_ref, kv_ref):
    u = normed(x_ref[...].astype(F32), gain_ref[...])
    u_ref[...] = u
    width = wk_ref.shape[1]
    store_rotated(kv_ref, slice(None), dot(u, wk_ref[...]), cos_ref[...], sin_ref[...])
    kv_ref[:, width:] = dot(u, wv_ref[...]).astype(BF16)


def project_kv(x, gain, w_k, w_v, cos_t, sin_t):
    rows, dim = x.shape
    width = w_k.shape[1]
    block = 256
    whole = lambda a, b: pl.BlockSpec((a, b), lambda i: (0, 0))
    banded = lambda b: pl.BlockSpec((block, b), lambda i: (i, 0))
    return pl.pallas_call(
        kv_kernel, grid=(rows // block,), name="project_kv",
        in_specs=[banded(dim), whole(1, dim), whole(dim, width), whole(dim, width), banded(HEAD_DIM), banded(HEAD_DIM)],
        out_specs=[banded(dim), banded(2 * width)],
        out_shape=[jax.ShapeDtypeStruct((rows, dim), BF16), jax.ShapeDtypeStruct((rows, 2 * width), BF16)],
        compiler_params=params(("arbitrary",), 48),
        cost_estimate=pl.CostEstimate(flops=4 * rows * dim * width, bytes_accessed=4 * dim * (rows + width), transcendentals=0),
    )(x, gain, w_k, w_v, cos_t, sin_t)


def q_kernel(u_ref, w_ref, cos_ref, sin_ref, q_ref):
    block = 256

    @pl.loop(0, u_ref.shape[0] // block)
    def _(i):
        rows = pl.ds(pl.multiple_of(i * block, block), block)
        store_rotated(q_ref, rows, dot(u_ref[rows, :], w_ref[...]), cos_ref[rows, :], sin_ref[rows, :])


def project_q(u, w_q, cos_t, sin_t):
    rows, dim = u.shape
    width = w_q.shape[1]
    block = 512
    return pl.pallas_call(
        q_kernel, grid=(width // block,), name="project_q",
        in_specs=[pl.BlockSpec((rows, dim), lambda i: (0, 0)), pl.BlockSpec((dim, block), lambda i: (0, i)),
                  pl.BlockSpec((rows, HEAD_DIM), lambda i: (0, 0)), pl.BlockSpec((rows, HEAD_DIM), lambda i: (0, 0))],
        out_specs=pl.BlockSpec((rows, block), lambda i: (0, i)),
        out_shape=jax.ShapeDtypeStruct((rows, width), BF16),
        compiler_params=params(("arbitrary",), 48),
        cost_estimate=pl.CostEstimate(flops=2 * rows * dim * width, bytes_accessed=2 * dim * (rows + width), transcendentals=0),
    )(u, w_q, cos_t, sin_t)


def attn_kernel(group, row_base, meta_ref, q_ref, *refs):
    parts = (len(refs) - 7) // 2
    k_refs, v_refs = refs[:parts], refs[parts:2 * parts]
    o_ref, k_all, v_all, q_t, m_ref, l_ref, acc_ref = refs[2 * parts:]
    shard, cut = meta_ref[0], meta_ref[1]
    block = q_ref.shape[0]
    keys = k_refs[0].shape[0]
    scale = (HEAD_DIM ** -0.5) * LOG2E

    @pl.when(pl.program_id(1) == 0)
    def _():
        for idx in range(parts):
            rows = pl.ds(pl.multiple_of((shard ^ idx) * keys, keys), keys)
            k_all[rows, :] = k_refs[idx][...]
            v_all[:, rows] = v_refs[idx][...].T

    first = shard * keys + row_base + pl.program_id(1) * block
    last = first + block - 1
    for head in range(group):
        q_t[head] = q_ref[:, head * HEAD_DIM:(head + 1) * HEAD_DIM].T
    m_ref[...] = jnp.full_like(m_ref, MASKED)
    l_ref[...] = jnp.zeros_like(l_ref)
    acc_ref[...] = jnp.zeros_like(acc_ref)

    def step(masked, kb, carry):
        start = pl.multiple_of(kb * K_BLOCK, K_BLOCK)
        k_blk = k_all[pl.ds(start, K_BLOCK), :]
        v_blk = v_all[:, pl.ds(start, K_BLOCK)]
        scores = [dot(k_blk, q_t[head]) for head in range(group)]
        m_old = [m_ref[head] for head in range(group)]
        l_old = [l_ref[head] for head in range(group)]
        if masked:
            k_idx = start + lax.broadcasted_iota(jnp.int32, (K_BLOCK, block), 0)
            r_idx = first + lax.broadcasted_iota(jnp.int32, (K_BLOCK, block), 1)
            allowed = (k_idx <= r_idx) & ((k_idx >= cut) | (r_idx < cut))
            scores = [jnp.where(allowed, s, MASKED) for s in scores]
        news = []
        for head in range(group):
            m_new = jnp.maximum(m_old[head], jnp.max(scores[head], axis=0, keepdims=True) * scale)
            p = jnp.exp2(scores[head] * scale - m_new)
            alpha = jnp.exp2(m_old[head] - m_new)
            total = alpha * l_old[head] + jnp.sum(p, axis=0, keepdims=True)
            news.append((m_new, total, alpha, dot(v_blk, p.astype(BF16))))
        for head in range(group):
            m_ref[head], l_ref[head] = news[head][:2]
            acc_ref[head] = news[head][2] * acc_ref[head] + news[head][3]
        return carry

    low = jnp.where(first >= cut, cut, 0) // K_BLOCK
    high = last // K_BLOCK + 1
    clear = (jnp.where(last >= cut, cut, 0) + K_BLOCK - 1) // K_BLOCK
    edge_a = jnp.minimum(jnp.maximum(clear, low), high)
    edge_b = jnp.maximum(edge_a, (first + 1) // K_BLOCK)
    lax.fori_loop(edge_a, edge_b, functools.partial(step, False), 0)
    head_count = edge_a - low
    lax.fori_loop(0, head_count + high - edge_b,
                  lambda i, carry: step(True, jnp.where(i < head_count, low + i, edge_b + i - head_count), carry), 0)
    for head in range(group):
        o_ref[:, head * HEAD_DIM:(head + 1) * HEAD_DIM] = (acc_ref[head] / l_ref[head]).T.astype(BF16)


def attention(meta, q_rot, kv_parts, row_base, rows, flops):
    kv_rows, kv_width = kv_parts[0].shape
    kv_heads = kv_width // (2 * HEAD_DIM)
    group = q_rot.shape[1] // HEAD_DIM // kv_heads
    width = group * HEAD_DIM
    parts = len(kv_parts)
    base = row_base // Q_BLOCK
    k_spec = pl.BlockSpec((kv_rows, HEAD_DIM), lambda h, i, m: (0, h))
    v_spec = pl.BlockSpec((kv_rows, HEAD_DIM), lambda h, i, m: (0, kv_heads + h))
    return pl.pallas_call(
        functools.partial(attn_kernel, group, row_base), name="attention",
        grid_spec=pltpu.PrefetchScalarGridSpec(
            num_scalar_prefetch=1, grid=(kv_heads, rows // Q_BLOCK),
            in_specs=[pl.BlockSpec((Q_BLOCK, width), lambda h, i, m: (base + i, h))] + [k_spec] * parts + [v_spec] * parts,
            out_specs=pl.BlockSpec((Q_BLOCK, width), lambda h, i, m: (i, h ^ m[0])),
            scratch_shapes=[pltpu.VMEM((parts * kv_rows, HEAD_DIM), BF16), pltpu.VMEM((HEAD_DIM, parts * kv_rows), BF16),
                            pltpu.VMEM((group, HEAD_DIM, Q_BLOCK), BF16), pltpu.VMEM((group, 1, Q_BLOCK), F32),
                            pltpu.VMEM((group, 1, Q_BLOCK), F32), pltpu.VMEM((group, HEAD_DIM, Q_BLOCK), F32)]),
        out_shape=jax.ShapeDtypeStruct((rows, kv_heads * width), BF16),
        compiler_params=params(("arbitrary", "arbitrary"), 48),
        cost_estimate=pl.CostEstimate(flops=flops, bytes_accessed=16 << 20, transcendentals=0),
    )(meta, q_rot, *kv_parts, *kv_parts)


def mid_kernel(pieces, meta_ref, x_ref, a_ref, b_ref, gain_ref, *refs):
    wa_refs, wb_refs = refs[:pieces], refs[pieces:2 * pieces]
    u_ref, own_ref, mid_ref, wa_all, wb_all = refs[2 * pieces:]
    step = pl.program_id(0)
    depth, width = wa_refs[0].shape
    for idx in range(pieces):
        wa_all[idx * depth:(idx + 1) * depth, :] = wa_refs[idx][...]
        wb_all[idx * depth:(idx + 1) * depth, :] = wb_refs[idx][...]
    cols = pl.ds(pl.multiple_of(step * width, width), width)
    mid_ref[:, cols] = x_ref[...].astype(F32) + (dot(a_ref[...], wa_all[...]) + dot(b_ref[...], wb_all[...]))

    @pl.when(step == pl.num_programs(0) - 1)
    def _():
        half = own_ref.shape[0]
        own_ref[...] = mid_ref[pl.ds(pl.multiple_of(meta_ref[2] * half, half), half), :]
        block = 128

        @pl.loop(0, u_ref.shape[0] // block)
        def _(i):
            rows = pl.ds(pl.multiple_of(i * block, block), block)
            u_ref[rows, :] = normed(mid_ref[rows, :], gain_ref[...])


def attn_out(meta, x, chunk, attn_mine, attn_peer, wo_mine, wo_pieces, gain):
    rows, depth = attn_mine.shape
    dim = x.shape[1]
    block = 512
    pieces = len(wo_pieces)
    resident = lambda a, b: pl.BlockSpec((a, b), lambda i, m: (0, 0))
    mine_specs = [pl.BlockSpec((depth // pieces, block), lambda i, m, p=p: (p ^ m[0], i)) for p in range(pieces)]
    peer_specs = [pl.BlockSpec((depth // pieces, block), lambda i, m: (0, i))] * pieces
    return pl.pallas_call(
        functools.partial(mid_kernel, pieces), name="attn_out",
        grid_spec=pltpu.PrefetchScalarGridSpec(
            num_scalar_prefetch=1, grid=(dim // block,),
            in_specs=[pl.BlockSpec((rows, block), lambda i, m: (chunk, i)), resident(rows, depth), resident(rows, depth),
                      resident(1, dim)] + mine_specs + peer_specs,
            out_specs=[resident(rows, dim), resident(rows // 2, dim)],
            scratch_shapes=[pltpu.VMEM((rows, dim), F32), pltpu.VMEM((depth, block), BF16), pltpu.VMEM((depth, block), BF16)]),
        out_shape=[jax.ShapeDtypeStruct((rows, dim), BF16), jax.ShapeDtypeStruct((rows // 2, dim), F32)],
        compiler_params=params(("arbitrary",), 56),
        cost_estimate=pl.CostEstimate(flops=4 * rows * depth * dim, bytes_accessed=4 * depth * dim, transcendentals=0),
    )(meta, x, attn_mine, attn_peer, gain, *([wo_mine] * pieces), *wo_pieces)


def mlp_kernel(u_ref, wg_ref, wu_ref, wd_ref, p_ref):
    u = u_ref[...]
    gate = dot(u, wg_ref[...])
    hidden = (gate * jax.nn.sigmoid(gate) * dot(u, wu_ref[...])).astype(BF16)

    @pl.when(pl.program_id(0) == 0)
    def _():
        p_ref[...] = dot(hidden, wd_ref[...])

    @pl.when(pl.program_id(0) > 0)
    def _():
        p_ref[...] += dot(hidden, wd_ref[...])


def mlp_part(u_mid, w_gate, w_up, w_down):
    dim, ff = w_gate.shape
    rows = u_mid.shape[0]
    return pl.pallas_call(
        mlp_kernel, grid=(ff // FF_BLOCK,), name="mlp_part",
        in_specs=[pl.BlockSpec((rows, dim), lambda i: (0, 0)),
                  pl.BlockSpec((dim, FF_BLOCK), lambda i: (0, i)), pl.BlockSpec((dim, FF_BLOCK), lambda i: (0, i)),
                  pl.BlockSpec((FF_BLOCK, dim), lambda i: (i, 0))],
        out_specs=pl.BlockSpec((rows, dim), lambda i: (0, 0)),
        out_shape=jax.ShapeDtypeStruct((rows, dim), F32),
        compiler_params=params(("arbitrary",), 56),
        cost_estimate=pl.CostEstimate(flops=6 * rows * dim * ff, bytes_accessed=6 * dim * ff, transcendentals=0),
    )(u_mid, w_gate, w_up, w_down)


def solution(mesh):
    sp_size = mesh.shape["sp"]
    row_spec = P(("rep", "sp"), None)
    tok_spec = P(("rep", "sp"))
    full_spec = P(None)
    col_spec = P(None, "tp")
    wrow_spec = P("tp", None)
    cache_spec = P("rep", ("tp", "sp"), None)
    tp_swap = [(0, 1), (1, 0)]
    core_swap = [(i, i ^ 1) for i in range(sp_size)]
    chip_swap = [(i, i ^ 2) for i in range(sp_size)]

    def layer(x_in, positions, segments, gain_attn, w_q, w_k, w_v, w_o, gain_mlp, w_gate, w_up, w_down):
        rows_local, dim = x_in.shape
        tp_idx, sp_idx = lax.axis_index("tp"), lax.axis_index("sp")
        odd, high = (sp_idx & 1) == 1, (sp_idx & 2) == 2

        depth = w_o.shape[0]
        quarter = depth // sp_size
        wo_own = lax.ppermute(lax.dynamic_slice(w_o, (sp_idx * quarter, 0), (quarter, dim)), "tp", tp_swap)

        zeros = jnp.sum((segments == 0).astype(jnp.int32)).reshape(1)
        zeros = zeros + lax.ppermute(zeros, "sp", core_swap)
        cut = (zeros + lax.ppermute(zeros, "sp", chip_swap))[0]
        meta = jnp.stack([sp_idx, cut, tp_idx, 1 - tp_idx]).astype(jnp.int32)

        cos_t, sin_t = rope_tables(positions)
        gain_a, gain_m = gain_attn.reshape(1, dim), gain_mlp.reshape(1, dim)
        u, kv_own = project_kv(x_in, gain_a, w_k, w_v, cos_t, sin_t)
        kv_chip = lax.ppermute(kv_own, "sp", chip_swap)
        kv_core = lax.ppermute(kv_own, "sp", core_swap)
        kv_diag = lax.ppermute(kv_chip, "sp", core_swap)
        kv_parts = (kv_own, kv_core, kv_chip, kv_diag)
        q_rot = project_q(u, w_q, cos_t, sin_t)

        wo_chip = lax.ppermute(wo_own, "sp", chip_swap)
        wo_core = lax.ppermute(wo_own, "sp", core_swap)
        wo_diag = lax.ppermute(wo_chip, "sp", core_swap)
        wo_pieces = (wo_own, wo_core, wo_chip, wo_diag)

        def ordered(own, core, chip, diag):
            near = jnp.concatenate([jnp.where(odd, core, own), jnp.where(odd, own, core)], axis=0)
            far = jnp.concatenate([jnp.where(odd, diag, chip), jnp.where(odd, chip, diag)], axis=0)
            return jnp.concatenate([jnp.where(high, far, near), jnp.where(high, near, far)], axis=0)

        def cache(offset):
            cols = [lax.dynamic_slice(part, (0, offset + sp_idx * HEAD_DIM), (rows_local, HEAD_DIM)) for part in kv_parts]
            return ordered(*cols).reshape(sp_size * rows_local, 1, HEAD_DIM)

        chunk_rows = rows_local // CHUNKS
        half = chunk_rows // 2
        attn_flops = 4 * chunk_rows * sp_size * rows_local * w_q.shape[1] // 4
        attn_mine, attn_peer = [], []
        for c in range(CHUNKS):
            attn_mine.append(attention(meta, q_rot, kv_parts, c * chunk_rows, chunk_rows, attn_flops))
            attn_peer.append(lax.ppermute(attn_mine[c], "tp", tp_swap))
        k_cache, v_cache = cache(0), cache(w_k.shape[1])
        y_out = jnp.zeros((rows_local, dim), BF16)
        k_cache, v_cache, y_out, attn_peer[0] = lax.optimization_barrier((k_cache, v_cache, y_out, attn_peer[0]))

        own, sums, sent = [], [], []
        for c in range(CHUNKS):
            u_mid, x_own = attn_out(meta, x_in, c, attn_mine[c], attn_peer[c], w_o, wo_pieces, gain_m)
            p_sum = mlp_part(u_mid, w_gate, w_up, w_down)
            sent.append(lax.ppermute(lax.dynamic_slice(p_sum, ((1 - tp_idx) * half, 0), (half, dim)), "tp", tp_swap))
            sums.append(lax.dynamic_slice(p_sum, (tp_idx * half, 0), (half, dim)))
            own.append(x_own)
        for c in range(CHUNKS):
            y_own = lax.optimization_barrier((own[c] + (sums[c] + sent[c])).astype(BF16))
            y_peer = lax.ppermute(y_own, "tp", tp_swap)
            y_out = lax.dynamic_update_slice(y_out, y_own, (c * chunk_rows + tp_idx * half, 0))
            y_out = lax.dynamic_update_slice(y_out, y_peer, (c * chunk_rows + (1 - tp_idx) * half, 0))
        return y_out, k_cache, v_cache


    return jax.shard_map(layer, mesh=mesh,
                         in_specs=(row_spec, tok_spec, tok_spec, full_spec, col_spec, col_spec, col_spec, wrow_spec,
                                   full_spec, col_spec, col_spec, wrow_spec),
                         out_specs=(row_spec, cache_spec, cache_spec), check_vma=False)
```

profile of v0, /device:TPU:2, one launch (start us, length us, event | category | flops | bytes accessed | tf_op | source)
XLA Modules:
  0.0 558.2 jit_solution(10862301229894230153)
XLA Ops:
  6.4 12.7 %project_kv.1 = (bf16[1024,3072]{1,0:T(8,128)(2,1)}, bf16[1024,1024]{1,0:T(8,128)(2,1)S(1)}) custom-call(bf16[1024,3072]{1,0:T(8,128)(2,1)} %x_ref.9, f32[1,3072]{1,0:T(1,128)S(1)} %bitcast.10, bf16[3072,512]{1,0:T(8,128)(2,1)} %wk_ref.1, bf16[3072,512]{1,0:T(8,128)(2,1)} %wv_ref.1, f32[1024,128]{1,0:T(8,128)S(1)} %pad_maximum_fusion.cos_ref, ...), custom_call_target="tpu_custom_call" | custom-call | flops 6442450944 | bytes 18874368 | tf_op jit(solution)/shard_map/project_kv/pallas_call | solution.py:66
  19.7 35.9 %collective-permute-done.6.refs_4_ = bf16[384,3072]{1,0:T(8,128)(2,1)} collective-permute-done((bf16[384,3072]{1,0:T(8,128)(2,1)S(1)}, bf16[384,3072]{1,0:T(8,128)(2,1)}, u32[]{:S(2)}, u32[]{:S(2)}) %collective-permute-start.6) | collective-permute-done | bytes 2359328 | tf_op jit(solution)/shard_map/ppermute | solution.py:278
  55.9 11.8 %collective-permute-done.refs_2_.refs_6_ = bf16[1024,1024]{1,0:T(8,128)(2,1)} collective-permute-done((bf16[1024,1024]{1,0:T(8,128)(2,1)S(1)}, bf16[1024,1024]{1,0:T(8,128)(2,1)}, u32[]{:S(2)}, u32[]{:S(2)}) %collective-permute-start) | collective-permute-done | bytes 2097184 | tf_op jit(solution)/shard_map/ppermute | solution.py:288
  68.9 48.0 %collective-permute-done.8.refs_6_ = bf16[384,3072]{1,0:T(8,128)(2,1)} collective-permute-done((bf16[384,3072]{1,0:T(8,128)(2,1)}, bf16[384,3072]{1,0:T(8,128)(2,1)}, u32[]{:S(2)}, u32[]{:S(2)}) %collective-permute-start.8) | collective-permute-done | bytes 2359328 | tf_op jit(solution)/shard_map/ppermute | solution.py:294
  116.9 17.4 %project_q.1.q_ref = bf16[1024,1536]{1,0:T(8,128)(2,1)S(1)} custom-call(bf16[1024,3072]{1,0:T(8,128)(2,1)} %get-tuple-element.18.u_ref, bf16[3072,1536]{1,0:T(8,128)(2,1)} %w_ref.1, f32[1024,128]{1,0:T(8,128)S(1)} %pad_maximum_fusion.cos_ref, f32[1024,128]{1,0:T(8,128)S(1)} %pad_maximum_fusion.1.sin_ref), custom_call_target="tpu_custom_call" | custom-call | flops 9663676416 | bytes 15728640 | tf_op jit(solution)/shard_map/project_q/pallas_call | solution.py:89
  142.7 24.3 %attention.7.a_ref = bf16[256,1536]{1,0:T(8,128)(2,1)S(1)} custom-call(s32[4]{0:T(128)S(1)} %pad_add_fusion.meta_ref, bf16[1024,1536]{1,0:T(8,128)(2,1)} %copy-done, bf16[1024,1024]{1,0:T(8,128)(2,1)S(1)} %get-tuple-element.17.refs_0_.refs_4_, bf16[1024,1024]{1,0:T(8,128)(2,1)} %collective-permute-done.2.refs_1_.refs_5_, ...), custom_call_target="tpu_custom_call" | custom-call | flops 1610612736 | bytes 16777216 | tf_op jit(solution)/shard_map/attention/pallas_call | solution.py:170
  167.5 22.8 %attention.6.a_ref = bf16[256,1536]{1,0:T(8,128)(2,1)S(1)} custom-call(s32[4]{0:T(128)S(1)} %pad_add_fusion.meta_ref, bf16[1024,1536]{1,0:T(8,128)(2,1)} %copy-done, bf16[1024,1024]{1,0:T(8,128)(2,1)S(1)} %get-tuple-element.17.refs_0_.refs_4_, bf16[1024,1024]{1,0:T(8,128)(2,1)} %collective-permute-done.2.refs_1_.refs_5_, ...), custom_call_target="tpu_custom_call" | custom-call | flops 1610612736 | bytes 16777216 | tf_op jit(solution)/shard_map/attention/pallas_call | solution.py:170
  191.9 23.0 %attention.4.a_ref = bf16[256,1536]{1,0:T(8,128)(2,1)S(1)} custom-call(s32[4]{0:T(128)S(1)} %pad_add_fusion.meta_ref, bf16[1024,1536]{1,0:T(8,128)(2,1)} %copy-done, bf16[1024,1024]{1,0:T(8,128)(2,1)S(1)} %get-tuple-element.17.refs_0_.refs_4_, bf16[1024,1024]{1,0:T(8,128)(2,1)} %collective-permute-done.2.refs_1_.refs_5_, ...), custom_call_target="tpu_custom_call" | custom-call | flops 1610612736 | bytes 16777216 | tf_op jit(solution)/shard_map/attention/pallas_call | solution.py:170
  218.3 22.8 %attention.5.a_ref = bf16[256,1536]{1,0:T(8,128)(2,1)S(1)} custom-call(s32[4]{0:T(128)S(1)} %pad_add_fusion.meta_ref, bf16[1024,1536]{1,0:T(8,128)(2,1)} %copy-done, bf16[1024,1024]{1,0:T(8,128)(2,1)S(1)} %get-tuple-element.17.refs_0_.refs_4_, bf16[1024,1024]{1,0:T(8,128)(2,1)} %collective-permute-done.2.refs_1_.refs_5_, ...), custom_call_target="tpu_custom_call" | custom-call | flops 1610612736 | bytes 16777216 | tf_op jit(solution)/shard_map/attention/pallas_call | solution.py:170
  244.7 14.4 %attn_out.7 = (bf16[256,3072]{1,0:T(8,128)(2,1)}, f32[128,3072]{1,0:T(8,128)}) custom-call(s32[4]{0:T(128)} %copy-done.5, bf16[1024,3072]{1,0:T(8,128)(2,1)} %x_ref.9, bf16[256,1536]{1,0:T(8,128)(2,1)} %copy-done.3, bf16[256,1536]{1,0:T(8,128)(2,1)} %copy-done.17, f32[1,3072]{1,0:T(1,128)} %bitcast.11, bf16[1536,3072]{1,0:T(8,128)(2,1)} %refs_3_.7, ...), custom_call_target="tpu_custom_call" | custom-call | flops 4831838208 | bytes 18874368 | tf_op jit(solution)/shard_map/attn_out/pallas_call | solution.py:216
  259.1 32.5 %mlp_part.7 = f32[256,3072]{1,0:T(8,128)} custom-call(bf16[256,3072]{1,0:T(8,128)(2,1)} %get-tuple-element.28.u_ref, bf16[3072,4096]{1,0:T(8,128)(2,1)} %wg_ref.7, bf16[3072,4096]{1,0:T(8,128)(2,1)} %wu_ref.7, bf16[4096,3072]{1,0:T(8,128)(2,1)} %wd_ref.7), custom_call_target="tpu_custom_call" | custom-call | flops 19327352832 | bytes 75497472 | tf_op jit(solution)/shard_map/mlp_part/pallas_call | solution.py:247
  293.6 14.6 %attn_out.6 = (bf16[256,3072]{1,0:T(8,128)(2,1)}, f32[128,3072]{1,0:T(8,128)}) custom-call(s32[4]{0:T(128)} %copy-done.5, bf16[1024,3072]{1,0:T(8,128)(2,1)} %x_ref.9, bf16[256,1536]{1,0:T(8,128)(2,1)} %copy-done.2, bf16[256,1536]{1,0:T(8,128)(2,1)} %collective-permute-done.15.b_ref, f32[1,3072]{1,0:T(1,128)} %bitcast.12, bf16[1536,3072]{1,0:T(8,128)(2,1)} %refs_3_.7, ...), custom_call_target="tpu_custom_call" | custom-call | flops 4831838208 | bytes 18874368 | tf_op jit(solution)/shard_map/attn_out/pallas_call | solution.py:216
  308.3 32.5 %mlp_part.6 = f32[256,3072]{1,0:T(8,128)} custom-call(bf16[256,3072]{1,0:T(8,128)(2,1)} %get-tuple-element.26.u_ref, bf16[3072,4096]{1,0:T(8,128)(2,1)} %wg_ref.7, bf16[3072,4096]{1,0:T(8,128)(2,1)} %wu_ref.7, bf16[4096,3072]{1,0:T(8,128)(2,1)} %wd_ref.7), custom_call_target="tpu_custom_call" | custom-call | flops 19327352832 | bytes 75497472 | tf_op jit(solution)/shard_map/mlp_part/pallas_call | solution.py:247
  340.8 2.8 constant_dynamic-slice_fusion.1
  345.1 14.4 %attn_out.5 = (bf16[256,3072]{1,0:T(8,128)(2,1)}, f32[128,3072]{1,0:T(8,128)}) custom-call(s32[4]{0:T(128)} %copy-done.5, bf16[1024,3072]{1,0:T(8,128)(2,1)} %x_ref.9, bf16[256,1536]{1,0:T(8,128)(2,1)} %copy-done.4, bf16[256,1536]{1,0:T(8,128)(2,1)} %collective-permute-done.12.b_ref, f32[1,3072]{1,0:T(1,128)} %bitcast.13, bf16[1536,3072]{1,0:T(8,128)(2,1)} %refs_3_.7, ...), custom_call_target="tpu_custom_call" | custom-call | flops 4831838208 | bytes 18874368 | tf_op jit(solution)/shard_map/attn_out/pallas_call | solution.py:216
  359.5 32.5 %mlp_part.5 = f32[256,3072]{1,0:T(8,128)} custom-call(bf16[256,3072]{1,0:T(8,128)(2,1)} %get-tuple-element.24.u_ref, bf16[3072,4096]{1,0:T(8,128)(2,1)} %wg_ref.7, bf16[3072,4096]{1,0:T(8,128)(2,1)} %wu_ref.7, bf16[4096,3072]{1,0:T(8,128)(2,1)} %wd_ref.7), custom_call_target="tpu_custom_call" | custom-call | flops 19327352832 | bytes 75497472 | tf_op jit(solution)/shard_map/mlp_part/pallas_call | solution.py:247
  392.0 14.5 %attn_out.4 = (bf16[256,3072]{1,0:T(8,128)(2,1)}, f32[128,3072]{1,0:T(8,128)}) custom-call(s32[4]{0:T(128)} %copy-done.5, bf16[1024,3072]{1,0:T(8,128)(2,1)} %x_ref.9, bf16[256,1536]{1,0:T(8,128)(2,1)} %copy-done.1, bf16[256,1536]{1,0:T(8,128)(2,1)} %copy-done.16, f32[1,3072]{1,0:T(1,128)} %bitcast.14, bf16[1536,3072]{1,0:T(8,128)(2,1)} %refs_3_.7, ...), custom_call_target="tpu_custom_call" | custom-call | flops 4831838208 | bytes 18874368 | tf_op jit(solution)/shard_map/attn_out/pallas_call | solution.py:216
  406.5 32.8 %mlp_part.4 = f32[256,3072]{1,0:T(8,128)} custom-call(bf16[256,3072]{1,0:T(8,128)(2,1)} %get-tuple-element.22.u_ref, bf16[3072,4096]{1,0:T(8,128)(2,1)} %wg_ref.7, bf16[3072,4096]{1,0:T(8,128)(2,1)} %wu_ref.7, bf16[4096,3072]{1,0:T(8,128)(2,1)} %wd_ref.7), custom_call_target="tpu_custom_call" | custom-call | flops 19327352832 | bytes 75497472 | tf_op jit(solution)/shard_map/mlp_part/pallas_call | solution.py:247
  446.0 32.4 %collective-permute-done.10 = f32[128,3072]{1,0:T(8,128)S(1)} collective-permute-done((f32[128,3072]{1,0:T(8,128)S(1)}, f32[128,3072]{1,0:T(8,128)S(1)}, u32[]{:S(2)}, u32[]{:S(2)}) %collective-permute-start.10) | collective-permute-done | bytes 1572896 | tf_op jit(solution)/shard_map/ppermute | solution.py:323
  479.1 32.9 %collective-permute-done.13 = f32[128,3072]{1,0:T(8,128)S(1)} collective-permute-done((f32[128,3072]{1,0:T(8,128)S(1)}, f32[128,3072]{1,0:T(8,128)S(1)}, u32[]{:S(2)}, u32[]{:S(2)}) %collective-permute-start.13) | collective-permute-done | bytes 1572896 | tf_op jit(solution)/shard_map/ppermute | solution.py:323
  515.7 13.2 %collective-permute-done.11 = bf16[128,3072]{1,0:T(8,128)(2,1)S(1)} collective-permute-done((bf16[128,3072]{1,0:T(8,128)(2,1)S(1)}, bf16[128,3072]{1,0:T(8,128)(2,1)S(1)}, u32[]{:S(2)}, u32[]{:S(2)}) %collective-permute-start.11) | collective-permute-done | bytes 786464 | tf_op jit(solution)/shard_map/ppermute | solution.py:328
  529.1 9.2 %collective-permute-done.14 = bf16[128,3072]{1,0:T(8,128)(2,1)S(1)} collective-permute-done((bf16[128,3072]{1,0:T(8,128)(2,1)S(1)}, bf16[128,3072]{1,0:T(8,128)(2,1)S(1)}, u32[]{:S(2)}, u32[]{:S(2)}) %collective-permute-start.14) | collective-permute-done | bytes 786464 | tf_op jit(solution)/shard_map/ppermute | solution.py:328
  538.4 8.3 %collective-permute-done.17 = bf16[128,3072]{1,0:T(8,128)(2,1)S(1)} collective-permute-done((bf16[128,3072]{1,0:T(8,128)(2,1)S(1)}, bf16[128,3072]{1,0:T(8,128)(2,1)S(1)}, u32[]{:S(2)}, u32[]{:S(2)}) %collective-permute-start.17) | collective-permute-done | bytes 786464 | tf_op jit(solution)/shard_map/ppermute | solution.py:328
  546.8 8.3 %collective-permute-done.20 = bf16[128,3072]{1,0:T(8,128)(2,1)S(1)} collective-permute-done((bf16[128,3072]{1,0:T(8,128)(2,1)S(1)}, bf16[128,3072]{1,0:T(8,128)(2,1)S(1)}, u32[]{:S(2)}, u32[]{:S(2)}) %collective-permute-start.20) | collective-permute-done | bytes 786464 | tf_op jit(solution)/shard_map/ppermute | solution.py:328
  (102 shorter events, 41.1 us)
Async XLA Ops:
  2.5 53.1 %collective-permute-start.6 = (bf16[384,3072]{1,0:T(8,128)(2,1)S(1)}, bf16[384,3072]{1,0:T(8,128)(2,1)}, u32[]{:S(2)}, u32[]{:S(2)}) collective-permute-start(bf16[384,3072]{1,0:T(8,128)(2,1)S(1)} %constant_dynamic-slice_fusion.4), channel_id=1, source_target_pairs={{0,4},{4,0},{1,5},{5,1},{2,6},{6,2},{3,7},{7,3}} | collective-permute-start | bytes 7077896 | tf_op jit(solution)/shard_map/ppermute | solution.py:278
  6.4 61.4 %copy-start.18 = (s32[1024]{0:T(1024)S(1)}, s32[1024]{0:T(1024)}, u32[]{:S(2)}) copy-start(s32[1024]{0:T(1024)} %param.14) | copy-start | bytes 12292
  19.1 48.6 %collective-permute-start = (bf16[1024,1024]{1,0:T(8,128)(2,1)S(1)}, bf16[1024,1024]{1,0:T(8,128)(2,1)}, u32[]{:S(2)}, u32[]{:S(2)}) collective-permute-start(bf16[1024,1024]{1,0:T(8,128)(2,1)S(1)} %get-tuple-element.17.refs_0_.refs_4_), channel_id=1, source_target_pairs={{0,2},{1,3},{2,0},{3,1},{4,6},{5,7},{6,4},{7,5}} | collective-permute-start | bytes 6291464 | tf_op jit(solution)/shard_map/ppermute | solution.py:288
  55.6 61.3 %collective-permute-start.8 = (bf16[384,3072]{1,0:T(8,128)(2,1)}, bf16[384,3072]{1,0:T(8,128)(2,1)}, u32[]{:S(2)}, u32[]{:S(2)}) collective-permute-start(bf16[384,3072]{1,0:T(8,128)(2,1)} %collective-permute-done.6.refs_4_), channel_id=1, source_target_pairs={{0,2},{1,3},{2,0},{3,1},{4,6},{5,7},{6,4},{7,5}} | collective-permute-start | bytes 7077896 | tf_op jit(solution)/shard_map/ppermute | solution.py:294
  55.9 85.5 %collective-permute-start.2 = (bf16[1024,1024]{1,0:T(8,128)(2,1)S(1)}, bf16[1024,1024]{1,0:T(8,128)(2,1)}, u32[]{:S(2)}, u32[]{:S(2)}) collective-permute-start(bf16[1024,1024]{1,0:T(8,128)(2,1)S(1)} %get-tuple-element.17.refs_0_.refs_4_), channel_id=1, source_target_pairs={{0,1},{1,0},{2,3},{3,2},{4,5},{5,4},{6,7},{7,6}} | collective-permute-start | bytes 6291464 | tf_op jit(solution)/shard_map/ppermute | solution.py:289
  67.7 74.9 %collective-permute-start.1 = (bf16[1024,1024]{1,0:T(8,128)(2,1)}, bf16[1024,1024]{1,0:T(8,128)(2,1)}, u32[]{:S(2)}, u32[]{:S(2)}) collective-permute-start(bf16[1024,1024]{1,0:T(8,128)(2,1)} %collective-permute-done.refs_2_.refs_6_), channel_id=1, source_target_pairs={{0,1},{1,0},{2,3},{3,2},{4,5},{5,4},{6,7},{7,6}} | collective-permute-start | bytes 6291464 | tf_op jit(solution)/shard_map/ppermute | solution.py:290
  68.4 67.6 %collective-permute-start.3 = (s32[1]{0:T(128)}, s32[1]{0:T(128)}, u32[]{:S(2)}, u32[]{:S(2)}) collective-permute-start(s32[1]{0:T(128)} %bitcast.4), channel_id=1, source_target_pairs={{0,1},{1,0},{2,3},{3,2},{4,5},{5,4},{6,7},{7,6}} | collective-permute-start | bytes 20 | tf_op jit(solution)/shard_map/ppermute | solution.py:281
  68.9 174.8 %collective-permute-start.7 = (bf16[384,3072]{1,0:T(8,128)(2,1)}, bf16[384,3072]{1,0:T(8,128)(2,1)}, u32[]{:S(2)}, u32[]{:S(2)}) collective-permute-start(bf16[384,3072]{1,0:T(8,128)(2,1)} %collective-permute-done.6.refs_4_), channel_id=1, source_target_pairs={{0,1},{1,0},{2,3},{3,2},{4,5},{5,4},{6,7},{7,6}} | collective-permute-start | bytes 7077896 | tf_op jit(solution)/shard_map/ppermute | solution.py:295
  116.9 127.8 %collective-permute-start.9 = (bf16[384,3072]{1,0:T(8,128)(2,1)}, bf16[384,3072]{1,0:T(8,128)(2,1)}, u32[]{:S(2)}, u32[]{:S(2)}) collective-permute-start(bf16[384,3072]{1,0:T(8,128)(2,1)} %collective-permute-done.8.refs_6_), channel_id=1, source_target_pairs={{0,1},{1,0},{2,3},{3,2},{4,5},{5,4},{6,7},{7,6}} | collective-permute-start | bytes 7077896 | tf_op jit(solution)/shard_map/ppermute | solution.py:296
  137.2 3.5 collective-permute-start.4
  141.4 76.9 %copy-start.5 = (s32[4]{0:T(128)}, s32[4]{0:T(128)S(1)}, u32[]{:S(2)}) copy-start(s32[4]{0:T(128)S(1)} %pad_add_fusion.meta_ref) | copy-start | bytes 52
  167.0 76.8 %collective-permute-start.18 = (bf16[256,1536]{1,0:T(8,128)(2,1)S(1)}, bf16[256,1536]{1,0:T(8,128)(2,1)S(1)}, u32[]{:S(2)}, u32[]{:S(2)}) collective-permute-start(bf16[256,1536]{1,0:T(8,128)(2,1)S(1)} %attention.7.a_ref), channel_id=1, source_target_pairs={{0,4},{4,0},{1,5},{5,1},{2,6},{6,2},{3,7},{7,3}} | collective-permute-start | bytes 2359304 | tf_op jit(solution)/shard_map/ppermute | solution.py:314
  190.3 103.3 %collective-permute-start.15 = (bf16[256,1536]{1,0:T(8,128)(2,1)S(1)}, bf16[256,1536]{1,0:T(8,128)(2,1)}, u32[]{:S(2)}, u32[]{:S(2)}) collective-permute-start(bf16[256,1536]{1,0:T(8,128)(2,1)S(1)} %attention.6.a_ref), channel_id=1, source_target_pairs={{0,4},{4,0},{1,5},{5,1},{2,6},{6,2},{3,7},{7,3}} | collective-permute-start | bytes 2359304 | tf_op jit(solution)/shard_map/ppermute | solution.py:314
  214.9 27.3 %collective-permute-start.5 = (bf16[256,1536]{1,0:T(8,128)(2,1)S(1)}, bf16[256,1536]{1,0:T(8,128)(2,1)S(1)}, u32[]{:S(2)}, u32[]{:S(2)}) collective-permute-start(bf16[256,1536]{1,0:T(8,128)(2,1)S(1)} %attention.4.a_ref), channel_id=1, source_target_pairs={{0,4},{4,0},{1,5},{5,1},{2,6},{6,2},{3,7},{7,3}} | collective-permute-start | bytes 2359304 | tf_op jit(solution)/shard_map/ppermute | solution.py:314
  242.2 102.9 %collective-permute-start.12 = (bf16[256,1536]{1,0:T(8,128)(2,1)S(1)}, bf16[256,1536]{1,0:T(8,128)(2,1)}, u32[]{:S(2)}, u32[]{:S(2)}) collective-permute-start(bf16[256,1536]{1,0:T(8,128)(2,1)S(1)} %attention.5.a_ref), channel_id=1, source_target_pairs={{0,4},{4,0},{1,5},{5,1},{2,6},{6,2},{3,7},{7,3}} | collective-permute-start | bytes 2359304 | tf_op jit(solution)/shard_map/ppermute | solution.py:314
  293.1 150.2 %collective-permute-start.19 = (f32[128,3072]{1,0:T(8,128)S(1)}, f32[128,3072]{1,0:T(8,128)S(1)}, u32[]{:S(2)}, u32[]{:S(2)}) collective-permute-start(f32[128,3072]{1,0:T(8,128)S(1)} %constant_dynamic-slice_fusion), channel_id=1, source_target_pairs={{0,4},{4,0},{1,5},{5,1},{2,6},{6,2},{3,7},{7,3}} | collective-permute-start | bytes 4718600 | tf_op jit(solution)/shard_map/ppermute | solution.py:323
  343.6 100.1 %collective-permute-start.16 = (f32[128,3072]{1,0:T(8,128)}, f32[128,3072]{1,0:T(8,128)S(1)}, u32[]{:S(2)}, u32[]{:S(2)}) collective-permute-start(f32[128,3072]{1,0:T(8,128)} %constant_dynamic-slice_fusion.1), channel_id=1, source_target_pairs={{0,4},{4,0},{1,5},{5,1},{2,6},{6,2},{3,7},{7,3}} | collective-permute-start | bytes 4718600 | tf_op jit(solution)/shard_map/ppermute | solution.py:323
  406.5 36.8 %copy-start.13 = (f32[128,3072]{1,0:T(8,128)S(1)}, f32[128,3072]{1,0:T(8,128)}, u32[]{:S(2)}) copy-start(f32[128,3072]{1,0:T(8,128)} %get-tuple-element.27) | copy-start | bytes 4718596
  441.1 37.3 %collective-permute-start.10 = (f32[128,3072]{1,0:T(8,128)S(1)}, f32[128,3072]{1,0:T(8,128)S(1)}, u32[]{:S(2)}, u32[]{:S(2)}) collective-permute-start(f32[128,3072]{1,0:T(8,128)S(1)} %constant_dynamic-slice_fusion.3), channel_id=1, source_target_pairs={{0,4},{4,0},{1,5},{5,1},{2,6},{6,2},{3,7},{7,3}} | collective-permute-start | bytes 4718600 | tf_op jit(solution)/shard_map/ppermute | solution.py:323
  441.9 70.2 %collective-permute-start.13 = (f32[128,3072]{1,0:T(8,128)S(1)}, f32[128,3072]{1,0:T(8,128)S(1)}, u32[]{:S(2)}, u32[]{:S(2)}) collective-permute-start(f32[128,3072]{1,0:T(8,128)S(1)} %constant_dynamic-slice_fusion.2), channel_id=1, source_target_pairs={{0,4},{4,0},{1,5},{5,1},{2,6},{6,2},{3,7},{7,3}} | collective-permute-start | bytes 4718600 | tf_op jit(solution)/shard_map/ppermute | solution.py:323
  478.6 50.3 %collective-permute-start.11 = (bf16[128,3072]{1,0:T(8,128)(2,1)S(1)}, bf16[128,3072]{1,0:T(8,128)(2,1)S(1)}, u32[]{:S(2)}, u32[]{:S(2)}) collective-permute-start(bf16[128,3072]{1,0:T(8,128)(2,1)S(1)} %add_convert_fusion.3), channel_id=1, source_target_pairs={{0,4},{4,0},{1,5},{5,1},{2,6},{6,2},{3,7},{7,3}} | collective-permute-start | bytes 2359304 | tf_op jit(solution)/shard_map/ppermute | solution.py:328
  512.3 25.9 %collective-permute-start.14 = (bf16[128,3072]{1,0:T(8,128)(2,1)S(1)}, bf16[128,3072]{1,0:T(8,128)(2,1)S(1)}, u32[]{:S(2)}, u32[]{:S(2)}) collective-permute-start(bf16[128,3072]{1,0:T(8,128)(2,1)S(1)} %add_convert_fusion.2), channel_id=1, source_target_pairs={{0,4},{4,0},{1,5},{5,1},{2,6},{6,2},{3,7},{7,3}} | collective-permute-start | bytes 2359304 | tf_op jit(solution)/shard_map/ppermute | solution.py:328
  512.8 33.8 %collective-permute-start.17 = (bf16[128,3072]{1,0:T(8,128)(2,1)S(1)}, bf16[128,3072]{1,0:T(8,128)(2,1)S(1)}, u32[]{:S(2)}, u32[]{:S(2)}) collective-permute-start(bf16[128,3072]{1,0:T(8,128)(2,1)S(1)} %add_convert_fusion.1), channel_id=1, source_target_pairs={{0,4},{4,0},{1,5},{5,1},{2,6},{6,2},{3,7},{7,3}} | collective-permute-start | bytes 2359304 | tf_op jit(solution)/shard_map/ppermute | solution.py:328
  514.4 40.7 %collective-permute-start.20 = (bf16[128,3072]{1,0:T(8,128)(2,1)S(1)}, bf16[128,3072]{1,0:T(8,128)(2,1)S(1)}, u32[]{:S(2)}, u32[]{:S(2)}) collective-permute-start(bf16[128,3072]{1,0:T(8,128)(2,1)S(1)} %add_convert_fusion), channel_id=1, source_target_pairs={{0,4},{4,0},{1,5},{5,1},{2,6},{6,2},{3,7},{7,3}} | collective-permute-start | bytes 2359304 | tf_op jit(solution)/shard_map/ppermute | solution.py:328
  (17 other events, 205.6 us)
where the time goes:
time: 561 us; the launch traced here: 558 us
  Pallas kernels  311 us (55%)
  waiting for transfers between devices  202 us (36%)
  local copies, waits for them, and re-layouts  16.7 us (3%)
  starting transfers between devices  15.9 us (3%)
  other arithmetic  9.52 us (2%)
    pallas_call x4, Pallas kernels, mlp_part(): pl.pallas_call(mlp_kernel, grid=(ff // FF_BLOCK,), name='mlp_part', in_sp...  130 us
    pallas_call x4, Pallas kernels, attention(): pl.pallas_call(functools.partial(attn_kernel, group, row_base), name='att...  92.9 us
    ppermute x4, waiting for transfers between devices, layer(): lax.ppermute(lax.dynamic_slice(p_sum, ((1 - tp_idx) * half, 0), (half, di...  65.3 us
    pallas_call x4, Pallas kernels, attn_out(): pl.pallas_call(functools.partial(mid_kernel, pieces), name='attn_out', gr...  57.9 us
    ppermute x1, waiting for transfers between devices, layer(): wo_chip = lax.ppermute(wo_own, 'sp', chip_swap)  48 us
    ppermute x4, waiting for transfers between devices, layer(): y_peer = lax.ppermute(y_own, 'tp', tp_swap)  38.9 us
    ppermute x1, waiting for transfers between devices, layer(): lax.ppermute(lax.dynamic_slice(w_o, (sp_idx * quarter, 0), (quarter, dim)...  35.9 us
    pallas_call x1, Pallas kernels, project_q(): pl.pallas_call(q_kernel, grid=(width // block,), name='project_q', in_spe...  17.4 us
  transfers between devices with their start and end apart: 21, of which 10 were waited for; matrix products, arithmetic and copies ran while one was open for 3% of the time, Pallas kernels for 56%

commit v1 on v0

v1 whole, which is shorter than its diff:
```python
import functools
import jax
import jax.numpy as jnp
from jax import lax
from jax.experimental import pallas as pl
from jax.experimental.pallas import tpu as pltpu
from jax.sharding import PartitionSpec as P


HEAD_DIM = 128
HALF = HEAD_DIM // 2
ROPE_BASE = 500000.0
NORM_EPS = 1e-5
LOG2E = 1.4426950408889634
BF16 = jnp.bfloat16
F32 = jnp.float32

CHUNKS = 4
Q_BLOCK = 256
K_BLOCK = 1024
FF_BLOCK = 512
MASKED = -1e30


def params(semantics, mib):
    return pltpu.CompilerParams(dimension_semantics=semantics, vmem_limit_bytes=mib << 20)


def dot(a, b):
    return jnp.dot(a, b, preferred_element_type=F32)


def normed(x, gain):
    mean_sq = jnp.mean(x * x, axis=-1, keepdims=True)
    return (x * lax.rsqrt(mean_sq + NORM_EPS) * gain).astype(BF16)


def rope_tables(positions):
    inv_freq = jnp.power(jnp.float32(ROPE_BASE), -jnp.arange(HALF, dtype=F32) * (2.0 / HEAD_DIM))
    angles = positions.astype(F32)[:, None] * jnp.concatenate([inv_freq, inv_freq])
    sign = jnp.where(jnp.arange(HEAD_DIM) < HALF, -1.0, 1.0).astype(F32)
    return jnp.cos(angles), jnp.sin(angles) * sign


def store_rotated(out_ref, rows, t_f32, cos_t, sin_t):
    for head in range(t_f32.shape[1] // HEAD_DIM):
        cols = slice(head * HEAD_DIM, (head + 1) * HEAD_DIM)
        t_head = t_f32[:, cols]
        out_ref[rows, cols] = (t_head * cos_t + pltpu.roll(t_head, HALF, 1) * sin_t).astype(BF16)


def kv_kernel(x_ref, gain_ref, wk_ref, wv_ref, cos_ref, sin_ref, u_ref, kv_ref):
    u = normed(x_ref[...].astype(F32), gain_ref[...])
    u_ref[...] = u
    width = wk_ref.shape[1]
    store_rotated(kv_ref, slice(None), dot(u, wk_ref[...]), cos_ref[...], sin_ref[...])
    kv_ref[:, width:] = dot(u, wv_ref[...]).astype(BF16)


def project_kv(x, gain, w_k, w_v, cos_t, sin_t):
    rows, dim = x.shape
    width = w_k.shape[1]
    block = 256
    whole = lambda a, b: pl.BlockSpec((a, b), lambda i: (0, 0))
    banded = lambda b: pl.BlockSpec((block, b), lambda i: (i, 0))
    return pl.pallas_call(
        kv_kernel, grid=(rows // block,), name="project_kv",
        in_specs=[banded(dim), whole(1, dim), whole(dim, width), whole(dim, width), banded(HEAD_DIM), banded(HEAD_DIM)],
        out_specs=[banded(dim), banded(2 * width)],
        out_shape=[jax.ShapeDtypeStruct((rows, dim), BF16), jax.ShapeDtypeStruct((rows, 2 * width), BF16)],
        compiler_params=params(("arbitrary",), 48),
        cost_estimate=pl.CostEstimate(flops=4 * rows * dim * width, bytes_accessed=4 * dim * (rows + width), transcendentals=0),
    )(x, gain, w_k, w_v, cos_t, sin_t)


def q_kernel(u_ref, w_ref, cos_ref, sin_ref, q_ref):
    block = 512

    @pl.loop(0, u_ref.shape[0] // block)
    def _(i):
        rows = pl.ds(pl.multiple_of(i * block, block), block)
        store_rotated(q_ref, rows, dot(u_ref[rows, :], w_ref[...]), cos_ref[rows, :], sin_ref[rows, :])


def project_q(u, w_q, cos_t, sin_t):
    rows, dim = u.shape
    width = w_q.shape[1]
    block = 512
    return pl.pallas_call(
        q_kernel, grid=(width // block,), name="project_q",
        in_specs=[pl.BlockSpec((rows, dim), lambda i: (0, 0)), pl.BlockSpec((dim, block), lambda i: (0, i)),
                  pl.BlockSpec((rows, HEAD_DIM), lambda i: (0, 0)), pl.BlockSpec((rows, HEAD_DIM), lambda i: (0, 0))],
        out_specs=pl.BlockSpec((rows, block), lambda i: (0, i)),
        out_shape=jax.ShapeDtypeStruct((rows, width), BF16),
        compiler_params=params(("arbitrary",), 48),
        cost_estimate=pl.CostEstimate(flops=2 * rows * dim * width, bytes_accessed=2 * dim * (rows + width), transcendentals=0),
    )(u, w_q, cos_t, sin_t)


def attn_kernel(group, row_base, finish, meta_ref, q_ref, *refs):
    k_refs, v_refs = refs[:2], refs[2:4]
    if finish:
        acc_in, m_in, l_in, o_ref = refs[4:8]
    else:
        acc_out, m_out, l_out = refs[4:7]
    k_all, v_all, q_t, m_ref, l_ref, acc_ref = refs[-6:]
    shard, cut = meta_ref[0], meta_ref[1]
    block = q_ref.shape[0]
    keys = k_refs[0].shape[0]
    scale = (HEAD_DIM ** -0.5) * LOG2E
    chip_base = (shard // 2) * (2 * keys)
    base = 0 if finish else chip_base

    @pl.when(pl.program_id(1) == 0)
    def _():
        for idx in range(2):
            rows = pl.ds(pl.multiple_of(((shard ^ idx) & 1) * keys, keys), keys)
            k_all[rows, :] = k_refs[idx][...]
            v_all[:, rows] = v_refs[idx][...].T

    first = shard * keys + row_base + pl.program_id(1) * block
    last = first + block - 1
    for head in range(group):
        q_t[head] = q_ref[:, head * HEAD_DIM:(head + 1) * HEAD_DIM].T
    if finish:
        m_ref[...], l_ref[...], acc_ref[...] = m_in[...], l_in[...], acc_in[...]
    else:
        m_ref[...] = jnp.full_like(m_ref, MASKED)
        l_ref[...] = jnp.zeros_like(l_ref)
        acc_ref[...] = jnp.zeros_like(acc_ref)

    def step(masked, kb, carry):
        start = kb * K_BLOCK
        rows = pl.ds(pl.multiple_of(start - base, K_BLOCK), K_BLOCK)
        k_blk = k_all[rows, :]
        v_blk = v_all[:, rows]
        scores = [dot(k_blk, q_t[head]) for head in range(group)]
        m_old = [m_ref[head] for head in range(group)]
        l_old = [l_ref[head] for head in range(group)]
        if masked:
            k_idx = start + lax.broadcasted_iota(jnp.int32, (K_BLOCK, block), 0)
            r_idx = first + lax.broadcasted_iota(jnp.int32, (K_BLOCK, block), 1)
            allowed = (k_idx <= r_idx) & ((k_idx >= cut) | (r_idx < cut))
            scores = [jnp.where(allowed, s, MASKED) for s in scores]
        news = []
        for head in range(group):
            m_new = jnp.maximum(m_old[head], jnp.max(scores[head], axis=0, keepdims=True) * scale)
            p = jnp.exp2(scores[head] * scale - m_new)
            alpha = jnp.exp2(m_old[head] - m_new)
            total = alpha * l_old[head] + jnp.sum(p, axis=0, keepdims=True)
            news.append((m_new, total, alpha, dot(v_blk, p.astype(BF16))))
        for head in range(group):
            m_ref[head], l_ref[head] = news[head][:2]
            acc_ref[head] = news[head][2] * acc_ref[head] + news[head][3]
        return carry

    seg_low = jnp.where(first >= cut, cut, 0)
    seg_high = jnp.where(last >= cut, cut, 0)
    low = jnp.maximum(seg_low, base) // K_BLOCK
    high = chip_base // K_BLOCK if finish else last // K_BLOCK + 1
    clear = (seg_high + K_BLOCK - 1) // K_BLOCK
    edge_a = jnp.maximum(low, jnp.minimum(clear, high))
    edge_b = jnp.maximum(edge_a, jnp.minimum((first + 1) // K_BLOCK, high))
    head_count = edge_a - low
    lax.fori_loop(edge_a, edge_b, functools.partial(step, False), 0)
    lax.fori_loop(0, head_count + jnp.maximum(high - edge_b, 0),
                  lambda i, carry: step(True, jnp.where(i < head_count, low + i, edge_b + i - head_count), carry), 0)
    if finish:
        for head in range(group):
            o_ref[:, head * HEAD_DIM:(head + 1) * HEAD_DIM] = (acc_ref[head] / l_ref[head]).T.astype(BF16)
    else:
        acc_out[...], m_out[...], l_out[...] = acc_ref[...], m_ref[...], l_ref[...]


def attention(meta, q_rot, kv_parts, row_base, rows, flops, partial_sums=None):
    kv_rows, kv_width = kv_parts[0].shape
    kv_heads = kv_width // (2 * HEAD_DIM)
    group = q_rot.shape[1] // HEAD_DIM // kv_heads
    width = group * HEAD_DIM
    base = row_base // Q_BLOCK
    finish = partial_sums is not None
    k_spec = pl.BlockSpec((kv_rows, HEAD_DIM), lambda h, i, m: (0, h))
    v_spec = pl.BlockSpec((kv_rows, HEAD_DIM), lambda h, i, m: (0, kv_heads + h))
    sums_specs = [pl.BlockSpec((group, depth, Q_BLOCK), lambda h, i, m: (h, 0, base + i)) for depth in (HEAD_DIM, 1, 1)]
    sums_shapes = [jax.ShapeDtypeStruct((kv_heads * group, depth, rows), F32) for depth in (HEAD_DIM, 1, 1)]
    return pl.pallas_call(
        functools.partial(attn_kernel, group, row_base, finish), name="attention",
        grid_spec=pltpu.PrefetchScalarGridSpec(
            num_scalar_prefetch=1, grid=(kv_heads, rows // Q_BLOCK),
            in_specs=[pl.BlockSpec((Q_BLOCK, width), lambda h, i, m: (base + i, h)), k_spec, k_spec, v_spec, v_spec]
                     + (sums_specs if finish else []),
            out_specs=pl.BlockSpec((Q_BLOCK, width), lambda h, i, m: (i, h ^ m[0])) if finish else sums_specs,
            scratch_shapes=[pltpu.VMEM((2 * kv_rows, HEAD_DIM), BF16), pltpu.VMEM((HEAD_DIM, 2 * kv_rows), BF16),
                            pltpu.VMEM((group, HEAD_DIM, Q_BLOCK), BF16), pltpu.VMEM((group, 1, Q_BLOCK), F32),
                            pltpu.VMEM((group, 1, Q_BLOCK), F32), pltpu.VMEM((group, HEAD_DIM, Q_BLOCK), F32)]),
        out_shape=jax.ShapeDtypeStruct((rows, kv_heads * width), BF16) if finish else sums_shapes,
        compiler_params=params(("arbitrary", "arbitrary"), 48),
        cost_estimate=pl.CostEstimate(flops=flops, bytes_accessed=16 << 20, transcendentals=0),
    )(meta, q_rot, *kv_parts, *kv_parts, *(partial_sums or ()))


def chunk_kernel(mine, peer, out_steps, meta_ref, x_ref, a_ref, b_ref, gain_ref, *refs):
    wa_refs, wb_refs = refs[:mine], refs[mine:mine + peer]
    wg_ref, wu_ref, wd_ref, send_ref, keep_ref, mid_ref, u_ref, acc_ref, wa_all, wb_all = refs[mine + peer:]
    step = pl.program_id(0)
    half = send_ref.shape[0]
    own = pl.ds(pl.multiple_of(meta_ref[2] * half, half), half)
    other = pl.ds(pl.multiple_of(meta_ref[3] * half, half), half)

    @pl.when(step < out_steps)
    def _():
        width = wa_all.shape[1]
        for pieces, whole in ((wa_refs, wa_all), (wb_refs, wb_all)):
            top = 0
            for piece in pieces:
                whole[top:top + piece.shape[0], :] = piece[...]
                top += piece.shape[0]
        cols = pl.ds(pl.multiple_of(step * width, width), width)
        mid_ref[:, cols] = x_ref[...].astype(F32) + (dot(a_ref[...], wa_all[...]) + dot(b_ref[...], wb_all[...]))

    @pl.when(step == out_steps - 1)
    def _():
        u_ref[:half, :] = normed(mid_ref[other, :], gain_ref[...])
        u_ref[half:, :] = normed(mid_ref[own, :], gain_ref[...])
        acc_ref[...] = jnp.zeros_like(acc_ref)

    @pl.when(step >= out_steps)
    def _():
        u = u_ref[...]
        gate = dot(u, wg_ref[...])
        hidden = (gate * jax.nn.sigmoid(gate) * dot(u, wu_ref[...])).astype(BF16)
        acc_ref[...] += dot(hidden, wd_ref[...])

    @pl.when(step == pl.num_programs(0) - 1)
    def _():
        send_ref[...] = acc_ref[:half, :]
        keep_ref[...] = mid_ref[own, :] + acc_ref[half:, :]


def chunk_layer(meta, x, chunk, attn_mine, attn_peer, wo_mine, wo_pieces, gain, w_gate, w_up, w_down):
    rows, depth = attn_mine.shape
    dim, ff = w_gate.shape
    block = 512
    out_steps, mlp_steps = dim // block, ff // FF_BLOCK
    heads = 4
    resident = lambda a, b: pl.BlockSpec((a, b), lambda i, m: (0, 0))
    early = lambda i: jnp.minimum(i, out_steps - 1)
    late = lambda i: jnp.maximum(i - out_steps, 0)
    mine_specs = [pl.BlockSpec((depth // heads, block), lambda i, m, p=p: (p ^ m[0], early(i))) for p in range(heads)]
    peer_specs = [pl.BlockSpec((w.shape[0], block), lambda i, m: (0, early(i))) for w in wo_pieces]
    return pl.pallas_call(
        functools.partial(chunk_kernel, heads, len(wo_pieces), out_steps), name="chunk_layer",
        grid_spec=pltpu.PrefetchScalarGridSpec(
            num_scalar_prefetch=1, grid=(out_steps + mlp_steps,),
            in_specs=[pl.BlockSpec((rows, block), lambda i, m: (chunk, early(i))), resident(rows, depth), resident(rows, depth),
                      resident(1, dim)] + mine_specs + peer_specs
                     + [pl.BlockSpec((dim, FF_BLOCK), lambda i, m: (0, late(i))), pl.BlockSpec((dim, FF_BLOCK), lambda i, m: (0, late(i))),
                        pl.BlockSpec((FF_BLOCK, dim), lambda i, m: (late(i), 0))],
            out_specs=[resident(rows // 2, dim)] * 2,
            scratch_shapes=[pltpu.VMEM((rows, dim), F32), pltpu.VMEM((rows, dim), BF16), pltpu.VMEM((rows, dim), F32),
                            pltpu.VMEM((depth, block), BF16), pltpu.VMEM((depth, block), BF16)]),
        out_shape=[jax.ShapeDtypeStruct((rows // 2, dim), F32)] * 2,
        compiler_params=params(("arbitrary",), 60),
        cost_estimate=pl.CostEstimate(flops=4 * rows * depth * dim + 6 * rows * dim * ff, bytes_accessed=6 * dim * ff, transcendentals=0),
    )(meta, x, attn_mine, attn_peer, gain, *([wo_mine] * heads), *wo_pieces, w_gate, w_up, w_down)


def solution(mesh):
    sp_size = mesh.shape["sp"]
    row_spec = P(("rep", "sp"), None)
    tok_spec = P(("rep", "sp"))
    full_spec = P(None)
    col_spec = P(None, "tp")
    wrow_spec = P("tp", None)
    cache_spec = P("rep", ("tp", "sp"), None)
    tp_swap = [(0, 1), (1, 0)]
    core_swap = [(i, i ^ 1) for i in range(sp_size)]
    chip_swap = [(i, i ^ 2) for i in range(sp_size)]

    def layer(x_in, positions, segments, gain_attn, w_q, w_k, w_v, w_o, gain_mlp, w_gate, w_up, w_down):
        rows_local, dim = x_in.shape
        tp_idx, sp_idx = lax.axis_index("tp"), lax.axis_index("sp")
        odd, high = (sp_idx & 1) == 1, (sp_idx & 2) == 2

        depth = w_o.shape[0]
        quarter = depth // sp_size
        half_q = quarter // 2
        wo_own = lax.ppermute(lax.dynamic_slice(w_o, (sp_idx * quarter, 0), (quarter, dim)), "tp", tp_swap)
        wo_far = lax.ppermute(lax.dynamic_slice(w_o, ((sp_idx ^ 2) * quarter, 0), (half_q, dim)), "tp", tp_swap)

        zeros = jnp.sum((segments == 0).astype(jnp.int32)).reshape(1)
        zeros = zeros + lax.ppermute(zeros, "sp", core_swap)
        cut = (zeros + lax.ppermute(zeros, "sp", chip_swap))[0]
        meta = jnp.stack([sp_idx, cut, tp_idx, 1 - tp_idx]).astype(jnp.int32)

        cos_t, sin_t = rope_tables(positions)
        gain_a, gain_m = gain_attn.reshape(1, dim), gain_mlp.reshape(1, dim)
        u, kv_own = project_kv(x_in, gain_a, w_k, w_v, cos_t, sin_t)
        kv_chip = lax.ppermute(kv_own, "sp", chip_swap)
        kv_core = lax.ppermute(kv_own, "sp", core_swap)
        kv_diag = lax.ppermute(kv_chip, "sp", core_swap)
        kv_parts = (kv_own, kv_core, kv_chip, kv_diag)
        q_rot = project_q(u, w_q, cos_t, sin_t)

        wo_near = lax.ppermute(wo_own[half_q:], "sp", chip_swap)
        wo_core = lax.ppermute(wo_own, "sp", core_swap)
        wo_dfar = lax.ppermute(wo_far, "sp", core_swap)
        wo_dnear = lax.ppermute(wo_near, "sp", core_swap)
        wo_pieces = (wo_own, wo_core, wo_far, wo_near, wo_dfar, wo_dnear)

        def ordered(own, core, chip, diag):
            near = jnp.concatenate([jnp.where(odd, core, own), jnp.where(odd, own, core)], axis=0)
            far = jnp.concatenate([jnp.where(odd, diag, chip), jnp.where(odd, chip, diag)], axis=0)
            return jnp.concatenate([jnp.where(high, far, near), jnp.where(high, near, far)], axis=0)

        def cache(offset):
            cols = [lax.dynamic_slice(part, (0, offset + sp_idx * HEAD_DIM), (rows_local, HEAD_DIM)) for part in kv_parts]
            return ordered(*cols).reshape(sp_size * rows_local, 1, HEAD_DIM)

        chunk_rows = rows_local // CHUNKS
        half = chunk_rows // 2
        attn_flops = 4 * chunk_rows * sp_size * rows_local * w_q.shape[1] // 4
        partial_sums = attention(meta, q_rot, kv_parts[:2], 0, rows_local, attn_flops)
        attn_mine, attn_peer = [], []
        for c in range(CHUNKS):
            attn_mine.append(attention(meta, q_rot, kv_parts[2:], c * chunk_rows, chunk_rows, attn_flops, partial_sums))
            attn_peer.append(lax.ppermute(attn_mine[c], "tp", tp_swap))
        k_cache, v_cache = cache(0), cache(w_k.shape[1])
        y_out = jnp.zeros((rows_local, dim), BF16)
        k_cache, v_cache, y_out, attn_peer[0] = lax.optimization_barrier((k_cache, v_cache, y_out, attn_peer[0]))

        kept, sent = [], []
        for c in range(CHUNKS):
            p_peer, p_own = chunk_layer(meta, x_in, c, attn_mine[c], attn_peer[c], w_o, wo_pieces, gain_m,
                                   w_gate, w_up, w_down)
            sent.append(lax.ppermute(p_peer, "tp", tp_swap))
            kept.append(p_own)
        for c in range(CHUNKS):
            y_own = lax.optimization_barrier((kept[c] + sent[c]).astype(BF16))
            y_peer = lax.ppermute(y_own, "tp", tp_swap)
            y_out = lax.dynamic_update_slice(y_out, y_own, (c * chunk_rows + tp_idx * half, 0))
            y_out = lax.dynamic_update_slice(y_out, y_peer, (c * chunk_rows + (1 - tp_idx) * half, 0))
        return y_out, k_cache, v_cache


    return jax.shard_map(layer, mesh=mesh,
                         in_specs=(row_spec, tok_spec, tok_spec, full_spec, col_spec, col_spec, col_spec, wrow_spec,
                                   full_spec, col_spec, col_spec, wrow_spec),
                         out_specs=(row_spec, cache_spec, cache_spec), check_vma=False)
```

time: 561 us -> 503 us (0.90); the launches traced: 558 us -> 493 us
  waiting for transfers between devices: 202 us -> 111 us
  starting transfers between devices: 15.9 us -> 48.2 us
  Pallas kernels: 311 us -> 300 us
    ppermute x6 -> x8, waiting for transfers between devices: 113 us -> 29.1 us  [the longest x4 29.1 us: layer(): sent.append(lax.ppermute(p_peer, 'tp', tp_swap))]
    ppermute x1, waiting for transfers between devices: 35.9 us -> 5.31 us  [layer(): lax.ppermute(lax.dynamic_slice(w_o, (sp_idx * quarter, 0), (quarter, dim)...]
    ppermute x1, waiting for transfers between devices: 11.8 us -> 42.3 us  [layer(): kv_chip = lax.ppermute(kv_own, 'sp', chip_swap)]
    ppermute x6 -> x8, starting transfers between devices: 4.29 us -> 33.9 us  [the longest x1 25.8 us: layer(): wo_dnear = lax.ppermute(wo_near, 'sp', core_swap)]
    pallas_call x12 -> x9, Pallas kernels: 281 us -> 271 us  [the longest x4 174 us: chunk_layer(): pl.pallas_call(functools.partial(chunk_kernel, heads, len(wo_pieces), out...]
    ppermute x4, waiting for transfers between devices: 38.9 us -> 33.3 us  [layer(): y_peer = lax.ppermute(y_own, 'tp', tp_swap)]
  transfers between devices with their start and end apart: 21 -> 23, of which waited for: 10 -> 8; matrix products, arithmetic and copies ran while one was open for 3% -> 4% of each run, Pallas kernels for 56% -> 58%
where the time goes in v1:
time: 503 us; the launch traced here: 493 us
  Pallas kernels  300 us (60%)
  waiting for transfers between devices  111 us (22%)
  starting transfers between devices  48.2 us (10%)
  local copies, waits for them, and re-layouts  17 us (3%)
  other arithmetic  13.8 us (3%)
    pallas_call x4, Pallas kernels, chunk_layer(): pl.pallas_call(functools.partial(chunk_kernel, heads, len(wo_pieces), out...  174 us
    pallas_call x5, Pallas kernels, attention(): pl.pallas_call(functools.partial(attn_kernel, group, row_base, finish), n...  97.2 us
    ppermute x1, waiting for transfers between devices, layer(): kv_chip = lax.ppermute(kv_own, 'sp', chip_swap)  42.3 us
    ppermute x4, waiting for transfers between devices, layer(): y_peer = lax.ppermute(y_own, 'tp', tp_swap)  33.3 us
    ppermute x4, waiting for transfers between devices, layer(): sent.append(lax.ppermute(p_peer, 'tp', tp_swap))  29.1 us
    ppermute x1, starting transfers between devices, layer(): wo_dnear = lax.ppermute(wo_near, 'sp', core_swap)  25.8 us
    pallas_call x1, Pallas kernels, project_q(): pl.pallas_call(q_kernel, grid=(width // block,), name='project_q', in_spe...  16 us
    pallas_call x1, Pallas kernels, project_kv(): pl.pallas_call(kv_kernel, grid=(rows // block,), name='project_kv', in_sp...  12.9 us
  transfers between devices with their start and end apart: 23, of which 8 were waited for; matrix products, arithmetic and copies ran while one was open for 4% of the time, Pallas kernels for 58%

profile of v1, /device:TPU:2, one launch (start us, length us, event | category | flops | bytes accessed | tf_op | source)
XLA Modules:
  0.0 493.4 jit_solution(2467103164704730265)
XLA Ops:
  4.0 12.9 %project_kv.1 = (bf16[1024,3072]{1,0:T(8,128)(2,1)}, bf16[1024,1024]{1,0:T(8,128)(2,1)}) custom-call(bf16[1024,3072]{1,0:T(8,128)(2,1)} %x_ref.9, f32[1,3072]{1,0:T(1,128)S(1)} %bitcast.10, bf16[3072,512]{1,0:T(8,128)(2,1)} %wk_ref.1, bf16[3072,512]{1,0:T(8,128)(2,1)} %wv_ref.1, f32[1024,128]{1,0:T(8,128)S(1)} %get-tuple-element.50.cos_ref, ...), custom_call_target="tpu_custom_call" | custom-call | flops 6442450944 | bytes 18874368 | tf_op jit(solution)/shard_map/project_kv/pallas_call | solution.py:66
  17.0 3.2 constant_dynamic-slice_fusion.1
  20.2 2.0 collective-permute-start.6
  22.3 42.3 %collective-permute-done.refs_0_.refs_2_ = bf16[1024,1024]{1,0:T(8,128)(2,1)S(1)} collective-permute-done((bf16[1024,1024]{1,0:T(8,128)(2,1)}, bf16[1024,1024]{1,0:T(8,128)(2,1)S(1)}, u32[]{:S(2)}, u32[]{:S(2)}) %collective-permute-start) | collective-permute-done | bytes 2097184 | tf_op jit(solution)/shard_map/ppermute | solution.py:299
  64.5 2.4 constant_dynamic-slice_fusion
  69.4 5.3 %collective-permute-done.6.refs_4_ = bf16[384,3072]{1,0:T(8,128)(2,1)} collective-permute-done((bf16[384,3072]{1,0:T(8,128)(2,1)}, bf16[384,3072]{1,0:T(8,128)(2,1)}, u32[]{:S(2)}, u32[]{:S(2)}) %collective-permute-start.6) | collective-permute-done | bytes 2359328 | tf_op jit(solution)/shard_map/ppermute | solution.py:288
  78.1 16.0 %project_q.1.q_ref = bf16[1024,1536]{1,0:T(8,128)(2,1)S(1)} custom-call(bf16[1024,3072]{1,0:T(8,128)(2,1)} %get-tuple-element.21.u_ref, bf16[3072,1536]{1,0:T(8,128)(2,1)} %w_ref.1, f32[1024,128]{1,0:T(8,128)S(1)} %get-tuple-element.50.cos_ref, f32[1024,128]{1,0:T(8,128)S(1)} %get-tuple-element.49.sin_ref), custom_call_target="tpu_custom_call" | custom-call | flops 9663676416 | bytes 15728640 | tf_op jit(solution)/shard_map/project_q/pallas_call | solution.py:89
  97.0 3.8 collective-permute-start.4
  104.5 32.4 %attention.5 = (f32[12,128,1024]{2,1,0:T(8,128)}, f32[12,1,1024]{2,1,0:T(1,128)S(1)}, f32[12,1,1024]{2,1,0:T(1,128)S(1)}) custom-call(s32[4]{0:T(128)S(1)} %pad_add_fusion.meta_ref, bf16[1024,1536]{1,0:T(8,128)(2,1)} %copy-done, bf16[1024,1024]{1,0:T(8,128)(2,1)} %get-tuple-element.20.refs_0_.refs_2_, ...), custom_call_target="tpu_custom_call" | custom-call | flops 1610612736 | bytes 16777216 | tf_op jit(solution)/shard_map/attention/pallas_call | solution.py:186
  136.9 25.8 %collective-permute-start.11 = (bf16[192,3072]{1,0:T(8,128)(2,1)S(1)}, bf16[192,3072]{1,0:T(8,128)(2,1)S(1)}, u32[]{:S(2)}, u32[]{:S(2)}) collective-permute-start(bf16[192,3072]{1,0:T(8,128)(2,1)S(1)} %collective-permute-done.9.refs_7_), channel_id=1, source_target_pairs={{0,1},{1,0},{2,3},{3,2},{4,5},{5,4},{6,7},{7,6}} | collective-permute-start | bytes 3538952 | tf_op jit(solution)/shard_map/ppermute | solution.py:308
  162.7 16.9 %attention.9.a_ref = bf16[256,1536]{1,0:T(8,128)(2,1)S(1)} custom-call(s32[4]{0:T(128)S(1)} %pad_add_fusion.meta_ref, bf16[1024,1536]{1,0:T(8,128)(2,1)} %copy-done, bf16[1024,1024]{1,0:T(8,128)(2,1)S(1)} %collective-permute-done.refs_0_.refs_2_, bf16[1024,1024]{1,0:T(8,128)(2,1)} %collective-permute-done.1.refs_1_.refs_3_, ...), custom_call_target="tpu_custom_call" | custom-call | flops 1610612736 | bytes 16777216 | tf_op jit(solution)/shard_map/attention/pallas_call | solution.py:186
  181.0 15.9 %attention.8.a_ref = bf16[256,1536]{1,0:T(8,128)(2,1)S(1)} custom-call(s32[4]{0:T(128)S(1)} %pad_add_fusion.meta_ref, bf16[1024,1536]{1,0:T(8,128)(2,1)} %copy-done, bf16[1024,1024]{1,0:T(8,128)(2,1)S(1)} %collective-permute-done.refs_0_.refs_2_, bf16[1024,1024]{1,0:T(8,128)(2,1)} %collective-permute-done.1.refs_1_.refs_3_, ...), custom_call_target="tpu_custom_call" | custom-call | flops 1610612736 | bytes 16777216 | tf_op jit(solution)/shard_map/attention/pallas_call | solution.py:186
  200.2 16.1 %attention.7.a_ref = bf16[256,1536]{1,0:T(8,128)(2,1)} custom-call(s32[4]{0:T(128)S(1)} %pad_add_fusion.meta_ref, bf16[1024,1536]{1,0:T(8,128)(2,1)} %copy-done, bf16[1024,1024]{1,0:T(8,128)(2,1)S(1)} %collective-permute-done.refs_0_.refs_2_, bf16[1024,1024]{1,0:T(8,128)(2,1)} %collective-permute-done.1.refs_1_.refs_3_, ...), custom_call_target="tpu_custom_call" | custom-call | flops 1610612736 | bytes 16777216 | tf_op jit(solution)/shard_map/attention/pallas_call | solution.py:186
  216.3 16.0 %attention.6.a_ref = bf16[256,1536]{1,0:T(8,128)(2,1)} custom-call(s32[4]{0:T(128)S(1)} %pad_add_fusion.meta_ref, bf16[1024,1536]{1,0:T(8,128)(2,1)} %copy-done, bf16[1024,1024]{1,0:T(8,128)(2,1)S(1)} %collective-permute-done.refs_0_.refs_2_, bf16[1024,1024]{1,0:T(8,128)(2,1)} %collective-permute-done.1.refs_1_.refs_3_, ...), custom_call_target="tpu_custom_call" | custom-call | flops 1610612736 | bytes 16777216 | tf_op jit(solution)/shard_map/attention/pallas_call | solution.py:186
  237.8 43.6 %chunk_layer.7 = (f32[128,3072]{1,0:T(8,128)}, f32[128,3072]{1,0:T(8,128)}) custom-call(s32[4]{0:T(128)} %copy-done.3, bf16[1024,3072]{1,0:T(8,128)(2,1)} %x_ref.9, bf16[256,1536]{1,0:T(8,128)(2,1)} %copy-done.2, bf16[256,1536]{1,0:T(8,128)(2,1)} %copy-done.15, f32[1,3072]{1,0:T(1,128)} %bitcast.11, bf16[1536,3072]{1,0:T(8,128)(2,1)} %refs_3_.7, ...), custom_call_target="tpu_custom_call" | custom-call | flops 24159191040 | bytes 75497472 | tf_op jit(solution)/shard_map/chunk_layer/pallas_call | solution.py:251
  282.9 43.5 %chunk_layer.6 = (f32[128,3072]{1,0:T(8,128)}, f32[128,3072]{1,0:T(8,128)}) custom-call(s32[4]{0:T(128)} %copy-done.3, bf16[1024,3072]{1,0:T(8,128)(2,1)} %x_ref.9, bf16[256,1536]{1,0:T(8,128)(2,1)} %copy-done.1, bf16[256,1536]{1,0:T(8,128)(2,1)} %collective-permute-done.17.b_ref, f32[1,3072]{1,0:T(1,128)} %bitcast.12, bf16[1536,3072]{1,0:T(8,128)(2,1)} %refs_3_.7, ...), custom_call_target="tpu_custom_call" | custom-call | flops 24159191040 | bytes 75497472 | tf_op jit(solution)/shard_map/chunk_layer/pallas_call | solution.py:251
  327.0 43.4 %chunk_layer.4 = (f32[128,3072]{1,0:T(8,128)}, f32[128,3072]{1,0:T(8,128)}) custom-call(s32[4]{0:T(128)} %copy-done.3, bf16[1024,3072]{1,0:T(8,128)(2,1)} %x_ref.9, bf16[256,1536]{1,0:T(8,128)(2,1)} %attention.6.a_ref, bf16[256,1536]{1,0:T(8,128)(2,1)} %collective-permute-done.5.b_ref, f32[1,3072]{1,0:T(1,128)} %bitcast.13, bf16[1536,3072]{1,0:T(8,128)(2,1)} %refs_3_.7, ...), custom_call_target="tpu_custom_call" | custom-call | flops 24159191040 | bytes 75497472 | tf_op jit(solution)/shard_map/chunk_layer/pallas_call | solution.py:251
  371.9 43.7 %chunk_layer.5 = (f32[128,3072]{1,0:T(8,128)}, f32[128,3072]{1,0:T(8,128)}) custom-call(s32[4]{0:T(128)} %copy-done.3, bf16[1024,3072]{1,0:T(8,128)(2,1)} %x_ref.9, bf16[256,1536]{1,0:T(8,128)(2,1)} %attention.7.a_ref, bf16[256,1536]{1,0:T(8,128)(2,1)} %collective-permute-done.14.b_ref, f32[1,3072]{1,0:T(1,128)} %bitcast.14, bf16[1536,3072]{1,0:T(8,128)(2,1)} %refs_3_.7, ...), custom_call_target="tpu_custom_call" | custom-call | flops 24159191040 | bytes 75497472 | tf_op jit(solution)/shard_map/chunk_layer/pallas_call | solution.py:251
  424.0 29.1 %collective-permute-done.15 = f32[128,3072]{1,0:T(8,128)S(1)} collective-permute-done((f32[128,3072]{1,0:T(8,128)}, f32[128,3072]{1,0:T(8,128)S(1)}, u32[]{:S(2)}, u32[]{:S(2)}) %collective-permute-start.15) | collective-permute-done | bytes 1572896 | tf_op jit(solution)/shard_map/ppermute | solution.py:336
  456.7 8.5 %collective-permute-done.13 = bf16[128,3072]{1,0:T(8,128)(2,1)S(1)} collective-permute-done((bf16[128,3072]{1,0:T(8,128)(2,1)S(1)}, bf16[128,3072]{1,0:T(8,128)(2,1)S(1)}, u32[]{:S(2)}, u32[]{:S(2)}) %collective-permute-start.13) | collective-permute-done | bytes 786464 | tf_op jit(solution)/shard_map/ppermute | solution.py:340
  465.3 8.3 %collective-permute-done.16 = bf16[128,3072]{1,0:T(8,128)(2,1)S(1)} collective-permute-done((bf16[128,3072]{1,0:T(8,128)(2,1)S(1)}, bf16[128,3072]{1,0:T(8,128)(2,1)S(1)}, u32[]{:S(2)}, u32[]{:S(2)}) %collective-permute-start.16) | collective-permute-done | bytes 786464 | tf_op jit(solution)/shard_map/ppermute | solution.py:340
  473.7 8.3 %collective-permute-done.19 = bf16[128,3072]{1,0:T(8,128)(2,1)S(1)} collective-permute-done((bf16[128,3072]{1,0:T(8,128)(2,1)S(1)}, bf16[128,3072]{1,0:T(8,128)(2,1)S(1)}, u32[]{:S(2)}, u32[]{:S(2)}) %collective-permute-start.19) | collective-permute-done | bytes 786464 | tf_op jit(solution)/shard_map/ppermute | solution.py:340
  482.1 8.3 %collective-permute-done.22 = bf16[128,3072]{1,0:T(8,128)(2,1)S(1)} collective-permute-done((bf16[128,3072]{1,0:T(8,128)(2,1)S(1)}, bf16[128,3072]{1,0:T(8,128)(2,1)S(1)}, u32[]{:S(2)}, u32[]{:S(2)}) %collective-permute-start.22) | collective-permute-done | bytes 786464 | tf_op jit(solution)/shard_map/ppermute | solution.py:340
  490.5 2.7 copy-done.9
  (95 shorter events, 40.2 us)
Async XLA Ops:
  17.0 47.6 %collective-permute-start = (bf16[1024,1024]{1,0:T(8,128)(2,1)}, bf16[1024,1024]{1,0:T(8,128)(2,1)S(1)}, u32[]{:S(2)}, u32[]{:S(2)}) collective-permute-start(bf16[1024,1024]{1,0:T(8,128)(2,1)} %get-tuple-element.20.refs_0_.refs_2_), channel_id=1, source_target_pairs={{0,2},{1,3},{2,0},{3,1},{4,6},{5,7},{6,4},{7,5}} | collective-permute-start | bytes 6291464 | tf_op jit(solution)/shard_map/ppermute | solution.py:299
  20.2 54.5 %collective-permute-start.6 = (bf16[384,3072]{1,0:T(8,128)(2,1)}, bf16[384,3072]{1,0:T(8,128)(2,1)}, u32[]{:S(2)}, u32[]{:S(2)}) collective-permute-start(bf16[384,3072]{1,0:T(8,128)(2,1)} %constant_dynamic-slice_fusion.1), channel_id=1, source_target_pairs={{0,4},{4,0},{1,5},{5,1},{2,6},{6,2},{3,7},{7,3}} | collective-permute-start | bytes 7077896 | tf_op jit(solution)/shard_map/ppermute | solution.py:288
  22.3 80.8 %collective-permute-start.2 = (bf16[1024,1024]{1,0:T(8,128)(2,1)}, bf16[1024,1024]{1,0:T(8,128)(2,1)}, u32[]{:S(2)}, u32[]{:S(2)}) collective-permute-start(bf16[1024,1024]{1,0:T(8,128)(2,1)} %get-tuple-element.20.refs_0_.refs_2_), channel_id=1, source_target_pairs={{0,1},{1,0},{2,3},{3,2},{4,5},{5,4},{6,7},{7,6}} | collective-permute-start | bytes 6291464 | tf_op jit(solution)/shard_map/ppermute | solution.py:300
  64.5 98.1 %collective-permute-start.1 = (bf16[1024,1024]{1,0:T(8,128)(2,1)S(1)}, bf16[1024,1024]{1,0:T(8,128)(2,1)}, u32[]{:S(2)}, u32[]{:S(2)}) collective-permute-start(bf16[1024,1024]{1,0:T(8,128)(2,1)S(1)} %collective-permute-done.refs_0_.refs_2_), channel_id=1, source_target_pairs={{0,1},{1,0},{2,3},{3,2},{4,5},{5,4},{6,7},{7,6}} | collective-permute-start | bytes 6291464 | tf_op jit(solution)/shard_map/ppermute | solution.py:301
  67.0 35.6 %collective-permute-start.8 = (bf16[192,3072]{1,0:T(8,128)(2,1)}, bf16[192,3072]{1,0:T(8,128)(2,1)}, u32[]{:S(2)}, u32[]{:S(2)}) collective-permute-start(bf16[192,3072]{1,0:T(8,128)(2,1)} %constant_dynamic-slice_fusion), channel_id=1, source_target_pairs={{0,4},{4,0},{1,5},{5,1},{2,6},{6,2},{3,7},{7,3}} | collective-permute-start | bytes 3538952 | tf_op jit(solution)/shard_map/ppermute | solution.py:289
  69.1 26.6 %collective-permute-start.3 = (s32[1]{0:T(128)}, s32[1]{0:T(128)}, u32[]{:S(2)}, u32[]{:S(2)}) collective-permute-start(s32[1]{0:T(128)} %bitcast.4), channel_id=1, source_target_pairs={{0,1},{1,0},{2,3},{3,2},{4,5},{5,4},{6,7},{7,6}} | collective-permute-start | bytes 20 | tf_op jit(solution)/shard_map/ppermute | solution.py:292
  76.0 60.9 %collective-permute-start.9 = (bf16[192,3072]{1,0:T(8,128)(2,1)S(1)}, bf16[192,3072]{1,0:T(8,128)(2,1)S(1)}, u32[]{:S(2)}, u32[]{:S(2)}) collective-permute-start(bf16[192,3072]{1,0:T(8,128)(2,1)S(1)} %slice.4), channel_id=1, source_target_pairs={{0,2},{1,3},{2,0},{3,1},{4,6},{5,7},{6,4},{7,5}} | collective-permute-start | bytes 3538952 | tf_op jit(solution)/shard_map/ppermute | solution.py:305
  97.0 4.9 collective-permute-start.4
  102.5 133.0 %collective-permute-start.7 = (bf16[384,3072]{1,0:T(8,128)(2,1)}, bf16[384,3072]{1,0:T(8,128)(2,1)S(1)}, u32[]{:S(2)}, u32[]{:S(2)}) collective-permute-start(bf16[384,3072]{1,0:T(8,128)(2,1)} %collective-permute-done.6.refs_4_), channel_id=1, source_target_pairs={{0,1},{1,0},{2,3},{3,2},{4,5},{5,4},{6,7},{7,6}} | collective-permute-start | bytes 7077896 | tf_op jit(solution)/shard_map/ppermute | solution.py:306
  102.6 113.7 %copy-start.3 = (s32[4]{0:T(128)}, s32[4]{0:T(128)S(1)}, u32[]{:S(2)}) copy-start(s32[4]{0:T(128)S(1)} %pad_add_fusion.meta_ref) | copy-start | bytes 52
  102.6 130.8 %collective-permute-start.10 = (bf16[192,3072]{1,0:T(8,128)(2,1)}, bf16[192,3072]{1,0:T(8,128)(2,1)S(1)}, u32[]{:S(2)}, u32[]{:S(2)}) collective-permute-start(bf16[192,3072]{1,0:T(8,128)(2,1)} %collective-permute-done.8.refs_6_), channel_id=1, source_target_pairs={{0,1},{1,0},{2,3},{3,2},{4,5},{5,4},{6,7},{7,6}} | collective-permute-start | bytes 3538952 | tf_op jit(solution)/shard_map/ppermute | solution.py:307
  136.9 98.0 %collective-permute-start.11 = (bf16[192,3072]{1,0:T(8,128)(2,1)S(1)}, bf16[192,3072]{1,0:T(8,128)(2,1)S(1)}, u32[]{:S(2)}, u32[]{:S(2)}) collective-permute-start(bf16[192,3072]{1,0:T(8,128)(2,1)S(1)} %collective-permute-done.9.refs_7_), channel_id=1, source_target_pairs={{0,1},{1,0},{2,3},{3,2},{4,5},{5,4},{6,7},{7,6}} | collective-permute-start | bytes 3538952 | tf_op jit(solution)/shard_map/ppermute | solution.py:308
  179.5 55.9 %collective-permute-start.20 = (bf16[256,1536]{1,0:T(8,128)(2,1)S(1)}, bf16[256,1536]{1,0:T(8,128)(2,1)S(1)}, u32[]{:S(2)}, u32[]{:S(2)}) collective-permute-start(bf16[256,1536]{1,0:T(8,128)(2,1)S(1)} %attention.9.a_ref), channel_id=1, source_target_pairs={{0,4},{4,0},{1,5},{5,1},{2,6},{6,2},{3,7},{7,3}} | collective-permute-start | bytes 2359304 | tf_op jit(solution)/shard_map/ppermute | solution.py:327
  196.9 86.0 %collective-permute-start.17 = (bf16[256,1536]{1,0:T(8,128)(2,1)S(1)}, bf16[256,1536]{1,0:T(8,128)(2,1)}, u32[]{:S(2)}, u32[]{:S(2)}) collective-permute-start(bf16[256,1536]{1,0:T(8,128)(2,1)S(1)} %attention.8.a_ref), channel_id=1, source_target_pairs={{0,4},{4,0},{1,5},{5,1},{2,6},{6,2},{3,7},{7,3}} | collective-permute-start | bytes 2359304 | tf_op jit(solution)/shard_map/ppermute | solution.py:327
  233.4 138.5 %collective-permute-start.14 = (bf16[256,1536]{1,0:T(8,128)(2,1)}, bf16[256,1536]{1,0:T(8,128)(2,1)}, u32[]{:S(2)}, u32[]{:S(2)}) collective-permute-start(bf16[256,1536]{1,0:T(8,128)(2,1)} %attention.7.a_ref), channel_id=1, source_target_pairs={{0,4},{4,0},{1,5},{5,1},{2,6},{6,2},{3,7},{7,3}} | collective-permute-start | bytes 2359304 | tf_op jit(solution)/shard_map/ppermute | solution.py:327
  234.9 92.1 %collective-permute-start.5 = (bf16[256,1536]{1,0:T(8,128)(2,1)}, bf16[256,1536]{1,0:T(8,128)(2,1)}, u32[]{:S(2)}, u32[]{:S(2)}) collective-permute-start(bf16[256,1536]{1,0:T(8,128)(2,1)} %attention.6.a_ref), channel_id=1, source_target_pairs={{0,4},{4,0},{1,5},{5,1},{2,6},{6,2},{3,7},{7,3}} | collective-permute-start | bytes 2359304 | tf_op jit(solution)/shard_map/ppermute | solution.py:327
  281.4 134.7 %collective-permute-start.21 = (f32[128,3072]{1,0:T(8,128)}, f32[128,3072]{1,0:T(8,128)S(1)}, u32[]{:S(2)}, u32[]{:S(2)}) collective-permute-start(f32[128,3072]{1,0:T(8,128)} %get-tuple-element.34), channel_id=1, source_target_pairs={{0,4},{4,0},{1,5},{5,1},{2,6},{6,2},{3,7},{7,3}} | collective-permute-start | bytes 4718600 | tf_op jit(solution)/shard_map/ppermute | solution.py:336
  326.4 92.5 %collective-permute-start.18 = (f32[128,3072]{1,0:T(8,128)}, f32[128,3072]{1,0:T(8,128)}, u32[]{:S(2)}, u32[]{:S(2)}) collective-permute-start(f32[128,3072]{1,0:T(8,128)} %get-tuple-element.32), channel_id=1, source_target_pairs={{0,4},{4,0},{1,5},{5,1},{2,6},{6,2},{3,7},{7,3}} | collective-permute-start | bytes 4718600 | tf_op jit(solution)/shard_map/ppermute | solution.py:336
  370.4 50.3 %collective-permute-start.12 = (f32[128,3072]{1,0:T(8,128)}, f32[128,3072]{1,0:T(8,128)}, u32[]{:S(2)}, u32[]{:S(2)}) collective-permute-start(f32[128,3072]{1,0:T(8,128)} %get-tuple-element.28), channel_id=1, source_target_pairs={{0,4},{4,0},{1,5},{5,1},{2,6},{6,2},{3,7},{7,3}} | collective-permute-start | bytes 4718600 | tf_op jit(solution)/shard_map/ppermute | solution.py:336
  415.5 37.5 %collective-permute-start.15 = (f32[128,3072]{1,0:T(8,128)}, f32[128,3072]{1,0:T(8,128)S(1)}, u32[]{:S(2)}, u32[]{:S(2)}) collective-permute-start(f32[128,3072]{1,0:T(8,128)} %get-tuple-element.30), channel_id=1, source_target_pairs={{0,4},{4,0},{1,5},{5,1},{2,6},{6,2},{3,7},{7,3}} | collective-permute-start | bytes 4718600 | tf_op jit(solution)/shard_map/ppermute | solution.py:336
  422.5 42.7 %collective-permute-start.13 = (bf16[128,3072]{1,0:T(8,128)(2,1)S(1)}, bf16[128,3072]{1,0:T(8,128)(2,1)S(1)}, u32[]{:S(2)}, u32[]{:S(2)}) collective-permute-start(bf16[128,3072]{1,0:T(8,128)(2,1)S(1)} %add_convert_fusion.3), channel_id=1, source_target_pairs={{0,4},{4,0},{1,5},{5,1},{2,6},{6,2},{3,7},{7,3}} | collective-permute-start | bytes 2359304 | tf_op jit(solution)/shard_map/ppermute | solution.py:340
  453.2 20.4 %collective-permute-start.16 = (bf16[128,3072]{1,0:T(8,128)(2,1)S(1)}, bf16[128,3072]{1,0:T(8,128)(2,1)S(1)}, u32[]{:S(2)}, u32[]{:S(2)}) collective-permute-start(bf16[128,3072]{1,0:T(8,128)(2,1)S(1)} %add_convert_fusion.2), channel_id=1, source_target_pairs={{0,4},{4,0},{1,5},{5,1},{2,6},{6,2},{3,7},{7,3}} | collective-permute-start | bytes 2359304 | tf_op jit(solution)/shard_map/ppermute | solution.py:340
  453.8 28.2 %collective-permute-start.19 = (bf16[128,3072]{1,0:T(8,128)(2,1)S(1)}, bf16[128,3072]{1,0:T(8,128)(2,1)S(1)}, u32[]{:S(2)}, u32[]{:S(2)}) collective-permute-start(bf16[128,3072]{1,0:T(8,128)(2,1)S(1)} %add_convert_fusion.1), channel_id=1, source_target_pairs={{0,4},{4,0},{1,5},{5,1},{2,6},{6,2},{3,7},{7,3}} | collective-permute-start | bytes 2359304 | tf_op jit(solution)/shard_map/ppermute | solution.py:340
  455.3 35.2 %collective-permute-start.22 = (bf16[128,3072]{1,0:T(8,128)(2,1)S(1)}, bf16[128,3072]{1,0:T(8,128)(2,1)S(1)}, u32[]{:S(2)}, u32[]{:S(2)}) collective-permute-start(bf16[128,3072]{1,0:T(8,128)(2,1)S(1)} %add_convert_fusion), channel_id=1, source_target_pairs={{0,4},{4,0},{1,5},{5,1},{2,6},{6,2},{3,7},{7,3}} | collective-permute-start | bytes 2359304 | tf_op jit(solution)/shard_map/ppermute | solution.py:340
  (16 other events, 209.1 us)

commit v2 on v1

--- a/solution.py
+++ b/solution.py
@@ -17,7 +17,6 @@
 
 CHUNKS = 4
 Q_BLOCK = 256
-K_BLOCK = 1024
 FF_BLOCK = 512
 MASKED = -1e30
 
@@ -97,12 +96,14 @@
     )(u, w_q, cos_t, sin_t)
 
 
-def attn_kernel(group, row_base, finish, meta_ref, q_ref, *refs):
-    k_refs, v_refs = refs[:2], refs[2:4]
+def attn_kernel(group, row_base, parts, k_block, load, finish, meta_ref, q_ref, *refs):
+    k_refs, v_refs, refs = refs[:parts], refs[parts:2 * parts], refs[2 * parts:]
+    if load:
+        acc_in, m_in, l_in = refs[:3]
     if finish:
-        acc_in, m_in, l_in, o_ref = refs[4:8]
+        o_ref = refs[-7]
     else:
-        acc_out, m_out, l_out = refs[4:7]
+        acc_out, m_out, l_out = refs[:3]
     k_all, v_all, q_t, m_ref, l_ref, acc_ref = refs[-6:]
     shard, cut = meta_ref[0], meta_ref[1]
     block = q_ref.shape[0]
@@ -113,8 +114,8 @@
 
     @pl.when(pl.program_id(1) == 0)
     def _():
-        for idx in range(2):
-            rows = pl.ds(pl.multiple_of(((shard ^ idx) & 1) * keys, keys), keys)
+        for idx in range(parts):
+            rows = pl.ds(pl.multiple_of(((shard ^ idx) & (parts - 1)) * keys, keys), keys)
             k_all[rows, :] = k_refs[idx][...]
             v_all[:, rows] = v_refs[idx][...].T
 
@@ -122,7 +123,7 @@
     last = first + block - 1
     for head in range(group):
         q_t[head] = q_ref[:, head * HEAD_DIM:(head + 1) * HEAD_DIM].T
-    if finish:
+    if load:
         m_ref[...], l_ref[...], acc_ref[...] = m_in[...], l_in[...], acc_in[...]
     else:
         m_ref[...] = jnp.full_like(m_ref, MASKED)
@@ -130,16 +131,16 @@
         acc_ref[...] = jnp.zeros_like(acc_ref)
 
     def step(masked, kb, carry):
-        start = kb * K_BLOCK
-        rows = pl.ds(pl.multiple_of(start - base, K_BLOCK), K_BLOCK)
+        start = kb * k_block
+        rows = pl.ds(pl.multiple_of(start - base, k_block), k_block)
         k_blk = k_all[rows, :]
         v_blk = v_all[:, rows]
         scores = [dot(k_blk, q_t[head]) for head in range(group)]
         m_old = [m_ref[head] for head in range(group)]
         l_old = [l_ref[head] for head in range(group)]
         if masked:
-            k_idx = start + lax.broadcasted_iota(jnp.int32, (K_BLOCK, block), 0)
-            r_idx = first + lax.broadcasted_iota(jnp.int32, (K_BLOCK, block), 1)
+            k_idx = start + lax.broadcasted_iota(jnp.int32, (k_block, block), 0)
+            r_idx = first + lax.broadcasted_iota(jnp.int32, (k_block, block), 1)
             allowed = (k_idx <= r_idx) & ((k_idx >= cut) | (r_idx < cut))
             scores = [jnp.where(allowed, s, MASKED) for s in scores]
         news = []
@@ -156,11 +157,11 @@
 
     seg_low = jnp.where(first >= cut, cut, 0)
     seg_high = jnp.where(last >= cut, cut, 0)
-    low = jnp.maximum(seg_low, base) // K_BLOCK
-    high = chip_base // K_BLOCK if finish else last // K_BLOCK + 1
-    clear = (seg_high + K_BLOCK - 1) // K_BLOCK
+    low = jnp.maximum(seg_low, base) // k_block
+    high = chip_base // k_block if load else last // k_block + 1
+    clear = (seg_high + k_block - 1) // k_block
     edge_a = jnp.maximum(low, jnp.minimum(clear, high))
-    edge_b = jnp.maximum(edge_a, jnp.minimum((first + 1) // K_BLOCK, high))
+    edge_b = jnp.maximum(edge_a, jnp.minimum((first + 1) // k_block, high))
     head_count = edge_a - low
     lax.fori_loop(edge_a, edge_b, functools.partial(step, False), 0)
     lax.fori_loop(0, head_count + jnp.maximum(high - edge_b, 0),
@@ -172,25 +173,25 @@
         acc_out[...], m_out[...], l_out[...] = acc_ref[...], m_ref[...], l_ref[...]
 
 
-def attention(meta, q_rot, kv_parts, row_base, rows, flops, partial_sums=None):
+def attention(meta, q_rot, kv_parts, row_base, rows, k_block, flops, finish=True, partial_sums=None):
     kv_rows, kv_width = kv_parts[0].shape
     kv_heads = kv_width // (2 * HEAD_DIM)
     group = q_rot.shape[1] // HEAD_DIM // kv_heads
     width = group * HEAD_DIM
     base = row_base // Q_BLOCK
-    finish = partial_sums is not None
+    parts, load = len(kv_parts), partial_sums is not None
     k_spec = pl.BlockSpec((kv_rows, HEAD_DIM), lambda h, i, m: (0, h))
     v_spec = pl.BlockSpec((kv_rows, HEAD_DIM), lambda h, i, m: (0, kv_heads + h))
     sums_specs = [pl.BlockSpec((group, depth, Q_BLOCK), lambda h, i, m: (h, 0, base + i)) for depth in (HEAD_DIM, 1, 1)]
     sums_shapes = [jax.ShapeDtypeStruct((kv_heads * group, depth, rows), F32) for depth in (HEAD_DIM, 1, 1)]
     return pl.pallas_call(
-        functools.partial(attn_kernel, group, row_base, finish), name="attention",
+        functools.partial(attn_kernel, group, row_base, parts, k_block, load, finish), name="attention",
         grid_spec=pltpu.PrefetchScalarGridSpec(
             num_scalar_prefetch=1, grid=(kv_heads, rows // Q_BLOCK),
-            in_specs=[pl.BlockSpec((Q_BLOCK, width), lambda h, i, m: (base + i, h)), k_spec, k_spec, v_spec, v_spec]
-                     + (sums_specs if finish else []),
+            in_specs=[pl.BlockSpec((Q_BLOCK, width), lambda h, i, m: (base + i, h))] + [k_spec] * parts + [v_spec] * parts
+                     + (sums_specs if load else []),
             out_specs=pl.BlockSpec((Q_BLOCK, width), lambda h, i, m: (i, h ^ m[0])) if finish else sums_specs,
-            scratch_shapes=[pltpu.VMEM((2 * kv_rows, HEAD_DIM), BF16), pltpu.VMEM((HEAD_DIM, 2 * kv_rows), BF16),
+            scratch_shapes=[pltpu.VMEM((parts * kv_rows, HEAD_DIM), BF16), pltpu.VMEM((HEAD_DIM, parts * kv_rows), BF16),
                             pltpu.VMEM((group, HEAD_DIM, Q_BLOCK), BF16), pltpu.VMEM((group, 1, Q_BLOCK), F32),
                             pltpu.VMEM((group, 1, Q_BLOCK), F32), pltpu.VMEM((group, HEAD_DIM, Q_BLOCK), F32)]),
         out_shape=jax.ShapeDtypeStruct((rows, kv_heads * width), BF16) if finish else sums_shapes,
@@ -265,6 +266,11 @@
     )(meta, x, attn_mine, attn_peer, gain, *([wo_mine] * heads), *wo_pieces, w_gate, w_up, w_down)
 
 
+def unwritten(shape, dtype):
+    return pl.pallas_call(lambda out_ref: None, name="unwritten", out_shape=jax.ShapeDtypeStruct(shape, dtype),
+                          out_specs=pl.BlockSpec(memory_space=pl.ANY))()
+
+
 def solution(mesh):
     sp_size = mesh.shape["sp"]
     row_spec = P(("rep", "sp"), None)
@@ -320,14 +326,18 @@
         chunk_rows = rows_local // CHUNKS
         half = chunk_rows // 2
         attn_flops = 4 * chunk_rows * sp_size * rows_local * w_q.shape[1] // 4
-        partial_sums = attention(meta, q_rot, kv_parts[:2], 0, rows_local, attn_flops)
+        split = CHUNKS // 2
+        partial_sums = attention(meta, q_rot, kv_parts[:2], 0, split * chunk_rows, 512, attn_flops, False)
         attn_mine, attn_peer = [], []
         for c in range(CHUNKS):
-            attn_mine.append(attention(meta, q_rot, kv_parts[2:], c * chunk_rows, chunk_rows, attn_flops, partial_sums))
+            if c < split:
+                rest = (kv_parts[2:], c * chunk_rows, chunk_rows, 1024, attn_flops, True, partial_sums)
+            else:
+                rest = (kv_parts, c * chunk_rows, chunk_rows, 1024, attn_flops)
+            attn_mine.append(attention(meta, q_rot, *rest))
             attn_peer.append(lax.ppermute(attn_mine[c], "tp", tp_swap))
         k_cache, v_cache = cache(0), cache(w_k.shape[1])
-        y_out = jnp.zeros((rows_local, dim), BF16)
-        k_cache, v_cache, y_out, attn_peer[0] = lax.optimization_barrier((k_cache, v_cache, y_out, attn_peer[0]))
+        y_out = unwritten((rows_local, dim), BF16)
 
         kept, sent = [], []
         for c in range(CHUNKS):

time: 503 us -> 478 us (0.950)
  starting transfers between devices: 48.2 us -> 29.2 us
  Pallas kernels: 300 us -> 294 us
    ppermute x1, starting transfers between devices: 25.8 us -> 6.87 us  [layer(): wo_dnear = lax.ppermute(wo_near, 'sp', core_swap)]
    pallas_call x5 -> x6, Pallas kernels: 97.2 us -> 90.4 us  [the longest x5 90.4 us: attention(): pl.pallas_call(functools.partial(attn_kernel, group, row_base, parts, k_b...]
  transfers between devices with their start and end apart: 23 -> 23, of which waited for: 8 -> 8; matrix products, arithmetic and copies ran while one was open for 4% -> 4% of each run, Pallas kernels for 58% -> 60%
where the time goes in v2:
time: 478 us; the launch traced here: 470 us
  Pallas kernels  294 us (62%)
  waiting for transfers between devices  114 us (24%)
  starting transfers between devices  29.2 us (6%)
  other arithmetic  14.9 us (3%)
  local copies, waits for them, and re-layouts  14.8 us (3%)
    pallas_call x4, Pallas kernels, chunk_layer(): pl.pallas_call(functools.partial(chunk_kernel, heads, len(wo_pieces), out...  174 us
    pallas_call x5, Pallas kernels, attention(): pl.pallas_call(functools.partial(attn_kernel, group, row_base, parts, k_b...  90.4 us
    ppermute x1, waiting for transfers between devices, layer(): kv_chip = lax.ppermute(kv_own, 'sp', chip_swap)  42.3 us
    ppermute x4, waiting for transfers between devices, layer(): y_peer = lax.ppermute(y_own, 'tp', tp_swap)  35.7 us
    ppermute x4, waiting for transfers between devices, layer(): sent.append(lax.ppermute(p_peer, 'tp', tp_swap))  30 us
    pallas_call x1, Pallas kernels, project_q(): pl.pallas_call(q_kernel, grid=(width // block,), name='project_q', in_spe...  16 us
    pallas_call x1, Pallas kernels, project_kv(): pl.pallas_call(kv_kernel, grid=(rows // block,), name='project_kv', in_sp...  12.9 us
  transfers between devices with their start and end apart: 23, of which 8 were waited for; matrix products, arithmetic and copies ran while one was open for 4% of the time, Pallas kernels for 60%

profile of v2, /device:TPU:2, one launch (start us, length us, event | category | flops | bytes accessed | tf_op | source)
XLA Modules:
  0.0 469.6 jit_solution(4655239400511504142)
XLA Ops:
  4.0 12.9 %project_kv.1 = (bf16[1024,3072]{1,0:T(8,128)(2,1)}, bf16[1024,1024]{1,0:T(8,128)(2,1)}) custom-call(bf16[1024,3072]{1,0:T(8,128)(2,1)} %x_ref.9, f32[1,3072]{1,0:T(1,128)S(1)} %bitcast.10, bf16[3072,512]{1,0:T(8,128)(2,1)} %wk_ref.1, bf16[3072,512]{1,0:T(8,128)(2,1)} %wv_ref.1, f32[1024,128]{1,0:T(8,128)S(1)} %get-tuple-element.42.cos_ref, ...), custom_call_target="tpu_custom_call" | custom-call | flops 6442450944 | bytes 18874368 | tf_op jit(solution)/shard_map/project_kv/pallas_call | solution.py:65
  17.0 3.2 constant_dynamic-slice_fusion.1
  22.2 42.3 %collective-permute-done.2.refs_0_.refs_2_.refs_6_ = bf16[1024,1024]{1,0:T(8,128)(2,1)S(1)} collective-permute-done((bf16[1024,1024]{1,0:T(8,128)(2,1)}, bf16[1024,1024]{1,0:T(8,128)(2,1)S(1)}, u32[]{:S(2)}, u32[]{:S(2)}) %collective-permute-start.2) | collective-permute-done | bytes 2097184 | tf_op jit(solution)/shard_map/ppermute | solution.py:305
  64.6 3.1 constant_dynamic-slice_fusion
  69.8 4.8 %collective-permute-done.6.refs_4_ = bf16[384,3072]{1,0:T(8,128)(2,1)} collective-permute-done((bf16[384,3072]{1,0:T(8,128)(2,1)}, bf16[384,3072]{1,0:T(8,128)(2,1)}, u32[]{:S(2)}, u32[]{:S(2)}) %collective-permute-start.6) | collective-permute-done | bytes 2359328 | tf_op jit(solution)/shard_map/ppermute | solution.py:294
  78.0 16.0 %project_q.1.q_ref = bf16[1024,1536]{1,0:T(8,128)(2,1)S(1)} custom-call(bf16[1024,3072]{1,0:T(8,128)(2,1)} %get-tuple-element.16.u_ref, bf16[3072,1536]{1,0:T(8,128)(2,1)} %w_ref.1, f32[1024,128]{1,0:T(8,128)S(1)} %get-tuple-element.42.cos_ref, f32[1024,128]{1,0:T(8,128)S(1)} %get-tuple-element.41.sin_ref), custom_call_target="tpu_custom_call" | custom-call | flops 9663676416 | bytes 15728640 | tf_op jit(solution)/shard_map/project_q/pallas_call | solution.py:88
  96.9 3.8 collective-permute-start.1
  103.1 2.3 broadcast_select_fusion.5
  105.4 13.0 %attention.5 = (f32[12,128,512]{2,1,0:T(8,128)}, f32[12,1,512]{2,1,0:T(1,128)S(1)}, f32[12,1,512]{2,1,0:T(1,128)S(1)}) custom-call(s32[4]{0:T(128)S(1)} %pad_add_fusion.meta_ref, bf16[1024,1536]{1,0:T(8,128)(2,1)} %copy-done.2, bf16[1024,1024]{1,0:T(8,128)(2,1)} %get-tuple-element.17.refs_0_.refs_2_.refs_4_, ...), custom_call_target="tpu_custom_call" | custom-call | flops 1610612736 | bytes 16777216 | tf_op jit(solution)/shard_map/attention/pallas_call | solution.py:187
  118.4 6.9 %collective-permute-start.11 = (bf16[192,3072]{1,0:T(8,128)(2,1)S(1)}, bf16[192,3072]{1,0:T(8,128)(2,1)S(1)}, u32[]{:S(2)}, u32[]{:S(2)}) collective-permute-start(bf16[192,3072]{1,0:T(8,128)(2,1)S(1)} %collective-permute-done.9.refs_7_), channel_id=1, source_target_pairs={{0,1},{1,0},{2,3},{3,2},{4,5},{5,4},{6,7},{7,6}} | collective-permute-start | bytes 3538952 | tf_op jit(solution)/shard_map/ppermute | solution.py:314
  125.3 23.8 %attention.9.a_ref = bf16[256,1536]{1,0:T(8,128)(2,1)S(1)} custom-call(s32[4]{0:T(128)S(1)} %pad_add_fusion.meta_ref, bf16[1024,1536]{1,0:T(8,128)(2,1)} %copy-done.2, bf16[1024,1024]{1,0:T(8,128)(2,1)} %get-tuple-element.17.refs_0_.refs_2_.refs_4_, bf16[1024,1024]{1,0:T(8,128)(2,1)} %collective-permute-done.4.refs_1_.refs_3_.refs_5_, ...), custom_call_target="tpu_custom_call" | custom-call | flops 1610612736 | bytes 16777216 | tf_op jit(solution)/shard_map/attention/pallas_call | solution.py:187
  150.6 22.8 %attention.8.a_ref = bf16[256,1536]{1,0:T(8,128)(2,1)S(1)} custom-call(s32[4]{0:T(128)S(1)} %pad_add_fusion.meta_ref, bf16[1024,1536]{1,0:T(8,128)(2,1)} %copy-done.2, bf16[1024,1024]{1,0:T(8,128)(2,1)} %get-tuple-element.17.refs_0_.refs_2_.refs_4_, bf16[1024,1024]{1,0:T(8,128)(2,1)} %collective-permute-done.4.refs_1_.refs_3_.refs_5_, ...), custom_call_target="tpu_custom_call" | custom-call | flops 1610612736 | bytes 16777216 | tf_op jit(solution)/shard_map/attention/pallas_call | solution.py:187
  176.6 15.4 %attention.7.a_ref = bf16[256,1536]{1,0:T(8,128)(2,1)S(1)} custom-call(s32[4]{0:T(128)S(1)} %pad_add_fusion.meta_ref, bf16[1024,1536]{1,0:T(8,128)(2,1)} %copy-done.2, bf16[1024,1024]{1,0:T(8,128)(2,1)S(1)} %copy-done.1, bf16[1024,1024]{1,0:T(8,128)(2,1)} %collective-permute-done.3.refs_1_.refs_3_.refs_7_, bf16[1024,1024]{1,0:T(8,128)(2,1)S(1)} %copy-done.1, ...), custom_call_target="tpu_custom_call" | custom-call | flops 1610612736 | bytes 16777216 | tf_op jit(solution)/shard_map/attention/pallas_call | solution.py:187
  192.0 15.4 %attention.6.a_ref = bf16[256,1536]{1,0:T(8,128)(2,1)S(1)} custom-call(s32[4]{0:T(128)S(1)} %pad_add_fusion.meta_ref, bf16[1024,1536]{1,0:T(8,128)(2,1)} %copy-done.2, bf16[1024,1024]{1,0:T(8,128)(2,1)S(1)} %copy-done.1, bf16[1024,1024]{1,0:T(8,128)(2,1)} %collective-permute-done.3.refs_1_.refs_3_.refs_7_, bf16[1024,1024]{1,0:T(8,128)(2,1)S(1)} %copy-done.1, ...), custom_call_target="tpu_custom_call" | custom-call | flops 1610612736 | bytes 16777216 | tf_op jit(solution)/shard_map/attention/pallas_call | solution.py:187
  212.2 43.6 %chunk_layer.7 = (f32[128,3072]{1,0:T(8,128)}, f32[128,3072]{1,0:T(8,128)}) custom-call(s32[4]{0:T(128)} %copy-done.7, bf16[1024,3072]{1,0:T(8,128)(2,1)} %x_ref.9, bf16[256,1536]{1,0:T(8,128)(2,1)} %copy-done.4, bf16[256,1536]{1,0:T(8,128)(2,1)} %collective-permute-done.20.b_ref, f32[1,3072]{1,0:T(1,128)} %bitcast.13, bf16[1536,3072]{1,0:T(8,128)(2,1)} %refs_3_.7, ...), custom_call_target="tpu_custom_call" | custom-call | flops 24159191040 | bytes 75497472 | tf_op jit(solution)/shard_map/chunk_layer/pallas_call | solution.py:252
  257.3 43.5 %chunk_layer.6 = (f32[128,3072]{1,0:T(8,128)}, f32[128,3072]{1,0:T(8,128)}) custom-call(s32[4]{0:T(128)} %copy-done.7, bf16[1024,3072]{1,0:T(8,128)(2,1)} %x_ref.9, bf16[256,1536]{1,0:T(8,128)(2,1)} %copy-done.3, bf16[256,1536]{1,0:T(8,128)(2,1)} %collective-permute-done.17.b_ref, f32[1,3072]{1,0:T(1,128)} %bitcast.14, bf16[1536,3072]{1,0:T(8,128)(2,1)} %refs_3_.7, ...), custom_call_target="tpu_custom_call" | custom-call | flops 24159191040 | bytes 75497472 | tf_op jit(solution)/shard_map/chunk_layer/pallas_call | solution.py:252
  301.4 43.4 %chunk_layer.4 = (f32[128,3072]{1,0:T(8,128)}, f32[128,3072]{1,0:T(8,128)}) custom-call(s32[4]{0:T(128)} %copy-done.7, bf16[1024,3072]{1,0:T(8,128)(2,1)} %x_ref.9, bf16[256,1536]{1,0:T(8,128)(2,1)} %copy-done.6, bf16[256,1536]{1,0:T(8,128)(2,1)} %collective-permute-done.5.b_ref, f32[1,3072]{1,0:T(1,128)} %bitcast.15, bf16[1536,3072]{1,0:T(8,128)(2,1)} %refs_3_.7, ...), custom_call_target="tpu_custom_call" | custom-call | flops 24159191040 | bytes 75497472 | tf_op jit(solution)/shard_map/chunk_layer/pallas_call | solution.py:252
  346.3 43.7 %chunk_layer.5 = (f32[128,3072]{1,0:T(8,128)}, f32[128,3072]{1,0:T(8,128)}) custom-call(s32[4]{0:T(128)} %copy-done.7, bf16[1024,3072]{1,0:T(8,128)(2,1)} %x_ref.9, bf16[256,1536]{1,0:T(8,128)(2,1)} %copy-done.5, bf16[256,1536]{1,0:T(8,128)(2,1)} %collective-permute-done.14.b_ref, f32[1,3072]{1,0:T(1,128)} %bitcast.16, bf16[1536,3072]{1,0:T(8,128)(2,1)} %refs_3_.7, ...), custom_call_target="tpu_custom_call" | custom-call | flops 24159191040 | bytes 75497472 | tf_op jit(solution)/shard_map/chunk_layer/pallas_call | solution.py:252
  397.5 30.0 %collective-permute-done.15 = f32[128,3072]{1,0:T(8,128)S(1)} collective-permute-done((f32[128,3072]{1,0:T(8,128)}, f32[128,3072]{1,0:T(8,128)S(1)}, u32[]{:S(2)}, u32[]{:S(2)}) %collective-permute-start.15) | collective-permute-done | bytes 1572896 | tf_op jit(solution)/shard_map/ppermute | solution.py:346
  430.4 10.9 %collective-permute-done.13 = bf16[128,3072]{1,0:T(8,128)(2,1)S(1)} collective-permute-done((bf16[128,3072]{1,0:T(8,128)(2,1)S(1)}, bf16[128,3072]{1,0:T(8,128)(2,1)S(1)}, u32[]{:S(2)}, u32[]{:S(2)}) %collective-permute-start.13) | collective-permute-done | bytes 786464 | tf_op jit(solution)/shard_map/ppermute | solution.py:350
  441.4 8.3 %collective-permute-done.16 = bf16[128,3072]{1,0:T(8,128)(2,1)S(1)} collective-permute-done((bf16[128,3072]{1,0:T(8,128)(2,1)S(1)}, bf16[128,3072]{1,0:T(8,128)(2,1)S(1)}, u32[]{:S(2)}, u32[]{:S(2)}) %collective-permute-start.16) | collective-permute-done | bytes 786464 | tf_op jit(solution)/shard_map/ppermute | solution.py:350
  449.9 8.3 %collective-permute-done.19 = bf16[128,3072]{1,0:T(8,128)(2,1)S(1)} collective-permute-done((bf16[128,3072]{1,0:T(8,128)(2,1)S(1)}, bf16[128,3072]{1,0:T(8,128)(2,1)S(1)}, u32[]{:S(2)}, u32[]{:S(2)}) %collective-permute-start.19) | collective-permute-done | bytes 786464 | tf_op jit(solution)/shard_map/ppermute | solution.py:350
  458.3 8.3 %collective-permute-done.22 = bf16[128,3072]{1,0:T(8,128)(2,1)S(1)} collective-permute-done((bf16[128,3072]{1,0:T(8,128)(2,1)S(1)}, bf16[128,3072]{1,0:T(8,128)(2,1)S(1)}, u32[]{:S(2)}, u32[]{:S(2)}) %collective-permute-start.22) | collective-permute-done | bytes 786464 | tf_op jit(solution)/shard_map/ppermute | solution.py:350
  466.6 2.7 copy-done.13
  (110 shorter events, 38.0 us)
Async XLA Ops:
  17.0 47.6 %collective-permute-start.2 = (bf16[1024,1024]{1,0:T(8,128)(2,1)}, bf16[1024,1024]{1,0:T(8,128)(2,1)S(1)}, u32[]{:S(2)}, u32[]{:S(2)}) collective-permute-start(bf16[1024,1024]{1,0:T(8,128)(2,1)} %get-tuple-element.17.refs_0_.refs_2_.refs_4_), channel_id=1, source_target_pairs={{0,2},{1,3},{2,0},{3,1},{4,6},{5,7},{6,4},{7,5}} | collective-permute-start | bytes 6291464 | tf_op jit(solution)/shard_map/ppermute | solution.py:305
  20.2 54.5 %collective-permute-start.6 = (bf16[384,3072]{1,0:T(8,128)(2,1)}, bf16[384,3072]{1,0:T(8,128)(2,1)}, u32[]{:S(2)}, u32[]{:S(2)}) collective-permute-start(bf16[384,3072]{1,0:T(8,128)(2,1)} %constant_dynamic-slice_fusion.1), channel_id=1, source_target_pairs={{0,4},{4,0},{1,5},{5,1},{2,6},{6,2},{3,7},{7,3}} | collective-permute-start | bytes 7077896 | tf_op jit(solution)/shard_map/ppermute | solution.py:294
  22.2 80.9 %collective-permute-start.4 = (bf16[1024,1024]{1,0:T(8,128)(2,1)}, bf16[1024,1024]{1,0:T(8,128)(2,1)}, u32[]{:S(2)}, u32[]{:S(2)}) collective-permute-start(bf16[1024,1024]{1,0:T(8,128)(2,1)} %get-tuple-element.17.refs_0_.refs_2_.refs_4_), channel_id=1, source_target_pairs={{0,1},{1,0},{2,3},{3,2},{4,5},{5,4},{6,7},{7,6}} | collective-permute-start | bytes 6291464 | tf_op jit(solution)/shard_map/ppermute | solution.py:306
  64.5 60.7 %collective-permute-start.3 = (bf16[1024,1024]{1,0:T(8,128)(2,1)S(1)}, bf16[1024,1024]{1,0:T(8,128)(2,1)}, u32[]{:S(2)}, u32[]{:S(2)}) collective-permute-start(bf16[1024,1024]{1,0:T(8,128)(2,1)S(1)} %collective-permute-done.2.refs_0_.refs_2_.refs_6_), channel_id=1, source_target_pairs={{0,1},{1,0},{2,3},{3,2},{4,5},{5,4},{6,7},{7,6}} | collective-permute-start | bytes 6291464 | tf_op jit(solution)/shard_map/ppermute | solution.py:307
  67.7 34.9 %collective-permute-start.8 = (bf16[192,3072]{1,0:T(8,128)(2,1)}, bf16[192,3072]{1,0:T(8,128)(2,1)}, u32[]{:S(2)}, u32[]{:S(2)}) collective-permute-start(bf16[192,3072]{1,0:T(8,128)(2,1)} %constant_dynamic-slice_fusion), channel_id=1, source_target_pairs={{0,4},{4,0},{1,5},{5,1},{2,6},{6,2},{3,7},{7,3}} | collective-permute-start | bytes 3538952 | tf_op jit(solution)/shard_map/ppermute | solution.py:295
  69.8 25.8 %collective-permute-start = (s32[1]{0:T(128)}, s32[1]{0:T(128)}, u32[]{:S(2)}, u32[]{:S(2)}) collective-permute-start(s32[1]{0:T(128)} %bitcast.1), channel_id=1, source_target_pairs={{0,1},{1,0},{2,3},{3,2},{4,5},{5,4},{6,7},{7,6}} | collective-permute-start | bytes 20 | tf_op jit(solution)/shard_map/ppermute | solution.py:298
  76.0 42.4 %collective-permute-start.9 = (bf16[192,3072]{1,0:T(8,128)(2,1)S(1)}, bf16[192,3072]{1,0:T(8,128)(2,1)S(1)}, u32[]{:S(2)}, u32[]{:S(2)}) collective-permute-start(bf16[192,3072]{1,0:T(8,128)(2,1)S(1)} %slice.4), channel_id=1, source_target_pairs={{0,2},{1,3},{2,0},{3,1},{4,6},{5,7},{6,4},{7,5}} | collective-permute-start | bytes 3538952 | tf_op jit(solution)/shard_map/ppermute | solution.py:311
  96.9 5.0 %collective-permute-start.1 = (s32[1]{0:T(128)}, s32[1]{0:T(128)}, u32[]{:S(2)}, u32[]{:S(2)}) collective-permute-start(s32[1]{0:T(128)} %add.98), channel_id=1, source_target_pairs={{0,2},{1,3},{2,0},{3,1},{4,6},{5,7},{6,4},{7,5}} | collective-permute-start | bytes 20 | tf_op jit(solution)/shard_map/ppermute | solution.py:299
  102.6 89.4 %copy-start.7 = (s32[4]{0:T(128)}, s32[4]{0:T(128)S(1)}, u32[]{:S(2)}) copy-start(s32[4]{0:T(128)S(1)} %pad_add_fusion.meta_ref) | copy-start | bytes 52
  102.6 106.1 %collective-permute-start.10 = (bf16[192,3072]{1,0:T(8,128)(2,1)}, bf16[192,3072]{1,0:T(8,128)(2,1)S(1)}, u32[]{:S(2)}, u32[]{:S(2)}) collective-permute-start(bf16[192,3072]{1,0:T(8,128)(2,1)} %collective-permute-done.8.refs_6_), channel_id=1, source_target_pairs={{0,1},{1,0},{2,3},{3,2},{4,5},{5,4},{6,7},{7,6}} | collective-permute-start | bytes 3538952 | tf_op jit(solution)/shard_map/ppermute | solution.py:313
  102.6 108.2 %collective-permute-start.7 = (bf16[384,3072]{1,0:T(8,128)(2,1)}, bf16[384,3072]{1,0:T(8,128)(2,1)S(1)}, u32[]{:S(2)}, u32[]{:S(2)}) collective-permute-start(bf16[384,3072]{1,0:T(8,128)(2,1)} %collective-permute-done.6.refs_4_), channel_id=1, source_target_pairs={{0,1},{1,0},{2,3},{3,2},{4,5},{5,4},{6,7},{7,6}} | collective-permute-start | bytes 7077896 | tf_op jit(solution)/shard_map/ppermute | solution.py:312
  118.4 91.8 %collective-permute-start.11 = (bf16[192,3072]{1,0:T(8,128)(2,1)S(1)}, bf16[192,3072]{1,0:T(8,128)(2,1)S(1)}, u32[]{:S(2)}, u32[]{:S(2)}) collective-permute-start(bf16[192,3072]{1,0:T(8,128)(2,1)S(1)} %collective-permute-done.9.refs_7_), channel_id=1, source_target_pairs={{0,1},{1,0},{2,3},{3,2},{4,5},{5,4},{6,7},{7,6}} | collective-permute-start | bytes 3538952 | tf_op jit(solution)/shard_map/ppermute | solution.py:314
  149.1 61.7 %collective-permute-start.20 = (bf16[256,1536]{1,0:T(8,128)(2,1)S(1)}, bf16[256,1536]{1,0:T(8,128)(2,1)}, u32[]{:S(2)}, u32[]{:S(2)}) collective-permute-start(bf16[256,1536]{1,0:T(8,128)(2,1)S(1)} %attention.9.a_ref), channel_id=1, source_target_pairs={{0,4},{4,0},{1,5},{5,1},{2,6},{6,2},{3,7},{7,3}} | collective-permute-start | bytes 2359304 | tf_op jit(solution)/shard_map/ppermute | solution.py:338
  173.5 83.9 %collective-permute-start.17 = (bf16[256,1536]{1,0:T(8,128)(2,1)S(1)}, bf16[256,1536]{1,0:T(8,128)(2,1)}, u32[]{:S(2)}, u32[]{:S(2)}) collective-permute-start(bf16[256,1536]{1,0:T(8,128)(2,1)S(1)} %attention.8.a_ref), channel_id=1, source_target_pairs={{0,4},{4,0},{1,5},{5,1},{2,6},{6,2},{3,7},{7,3}} | collective-permute-start | bytes 2359304 | tf_op jit(solution)/shard_map/ppermute | solution.py:338
  208.7 137.6 %collective-permute-start.14 = (bf16[256,1536]{1,0:T(8,128)(2,1)S(1)}, bf16[256,1536]{1,0:T(8,128)(2,1)}, u32[]{:S(2)}, u32[]{:S(2)}) collective-permute-start(bf16[256,1536]{1,0:T(8,128)(2,1)S(1)} %attention.7.a_ref), channel_id=1, source_target_pairs={{0,4},{4,0},{1,5},{5,1},{2,6},{6,2},{3,7},{7,3}} | collective-permute-start | bytes 2359304 | tf_op jit(solution)/shard_map/ppermute | solution.py:338
  210.2 91.2 %collective-permute-start.5 = (bf16[256,1536]{1,0:T(8,128)(2,1)S(1)}, bf16[256,1536]{1,0:T(8,128)(2,1)}, u32[]{:S(2)}, u32[]{:S(2)}) collective-permute-start(bf16[256,1536]{1,0:T(8,128)(2,1)S(1)} %attention.6.a_ref), channel_id=1, source_target_pairs={{0,4},{4,0},{1,5},{5,1},{2,6},{6,2},{3,7},{7,3}} | collective-permute-start | bytes 2359304 | tf_op jit(solution)/shard_map/ppermute | solution.py:338
  255.8 134.8 %collective-permute-start.21 = (f32[128,3072]{1,0:T(8,128)}, f32[128,3072]{1,0:T(8,128)}, u32[]{:S(2)}, u32[]{:S(2)}) collective-permute-start(f32[128,3072]{1,0:T(8,128)} %get-tuple-element.28), channel_id=1, source_target_pairs={{0,4},{4,0},{1,5},{5,1},{2,6},{6,2},{3,7},{7,3}} | collective-permute-start | bytes 4718600 | tf_op jit(solution)/shard_map/ppermute | solution.py:346
  300.8 91.5 %collective-permute-start.18 = (f32[128,3072]{1,0:T(8,128)}, f32[128,3072]{1,0:T(8,128)}, u32[]{:S(2)}, u32[]{:S(2)}) collective-permute-start(f32[128,3072]{1,0:T(8,128)} %get-tuple-element.26), channel_id=1, source_target_pairs={{0,4},{4,0},{1,5},{5,1},{2,6},{6,2},{3,7},{7,3}} | collective-permute-start | bytes 4718600 | tf_op jit(solution)/shard_map/ppermute | solution.py:346
  344.8 49.4 %collective-permute-start.12 = (f32[128,3072]{1,0:T(8,128)}, f32[128,3072]{1,0:T(8,128)}, u32[]{:S(2)}, u32[]{:S(2)}) collective-permute-start(f32[128,3072]{1,0:T(8,128)} %get-tuple-element.22), channel_id=1, source_target_pairs={{0,4},{4,0},{1,5},{5,1},{2,6},{6,2},{3,7},{7,3}} | collective-permute-start | bytes 4718600 | tf_op jit(solution)/shard_map/ppermute | solution.py:346
  390.0 37.5 %collective-permute-start.15 = (f32[128,3072]{1,0:T(8,128)}, f32[128,3072]{1,0:T(8,128)S(1)}, u32[]{:S(2)}, u32[]{:S(2)}) collective-permute-start(f32[128,3072]{1,0:T(8,128)} %get-tuple-element.24), channel_id=1, source_target_pairs={{0,4},{4,0},{1,5},{5,1},{2,6},{6,2},{3,7},{7,3}} | collective-permute-start | bytes 4718600 | tf_op jit(solution)/shard_map/ppermute | solution.py:346
  396.0 45.3 %collective-permute-start.13 = (bf16[128,3072]{1,0:T(8,128)(2,1)S(1)}, bf16[128,3072]{1,0:T(8,128)(2,1)S(1)}, u32[]{:S(2)}, u32[]{:S(2)}) collective-permute-start(bf16[128,3072]{1,0:T(8,128)(2,1)S(1)} %add_convert_fusion.3), channel_id=1, source_target_pairs={{0,4},{4,0},{1,5},{5,1},{2,6},{6,2},{3,7},{7,3}} | collective-permute-start | bytes 2359304 | tf_op jit(solution)/shard_map/ppermute | solution.py:350
  427.7 22.0 %collective-permute-start.16 = (bf16[128,3072]{1,0:T(8,128)(2,1)S(1)}, bf16[128,3072]{1,0:T(8,128)(2,1)S(1)}, u32[]{:S(2)}, u32[]{:S(2)}) collective-permute-start(bf16[128,3072]{1,0:T(8,128)(2,1)S(1)} %add_convert_fusion.2), channel_id=1, source_target_pairs={{0,4},{4,0},{1,5},{5,1},{2,6},{6,2},{3,7},{7,3}} | collective-permute-start | bytes 2359304 | tf_op jit(solution)/shard_map/ppermute | solution.py:350
  428.3 29.9 %collective-permute-start.19 = (bf16[128,3072]{1,0:T(8,128)(2,1)S(1)}, bf16[128,3072]{1,0:T(8,128)(2,1)S(1)}, u32[]{:S(2)}, u32[]{:S(2)}) collective-permute-start(bf16[128,3072]{1,0:T(8,128)(2,1)S(1)} %add_convert_fusion.1), channel_id=1, source_target_pairs={{0,4},{4,0},{1,5},{5,1},{2,6},{6,2},{3,7},{7,3}} | collective-permute-start | bytes 2359304 | tf_op jit(solution)/shard_map/ppermute | solution.py:350
  429.7 36.8 %collective-permute-start.22 = (bf16[128,3072]{1,0:T(8,128)(2,1)S(1)}, bf16[128,3072]{1,0:T(8,128)(2,1)S(1)}, u32[]{:S(2)}, u32[]{:S(2)}) collective-permute-start(bf16[128,3072]{1,0:T(8,128)(2,1)S(1)} %add_convert_fusion), channel_id=1, source_target_pairs={{0,4},{4,0},{1,5},{5,1},{2,6},{6,2},{3,7},{7,3}} | collective-permute-start | bytes 2359304 | tf_op jit(solution)/shard_map/ppermute | solution.py:350
  (23 other events, 345.3 us)

commit v3 on v2

--- a/solution.py
+++ b/solution.py
@@ -268,7 +268,47 @@
 
 def unwritten(shape, dtype):
     return pl.pallas_call(lambda out_ref: None, name="unwritten", out_shape=jax.ShapeDtypeStruct(shape, dtype),
-                          out_specs=pl.BlockSpec(memory_space=pl.ANY))()
+                          out_specs=pl.BlockSpec(memory_space=pltpu.HBM))()
+
+
+def finish_kernel(meta_ref, kept_ref, sent_ref, y_in, own_ref, y_ref):
+    y_own = (kept_ref[...] + sent_ref[...]).astype(BF16)
+    own_ref[...] = y_own
+    y_ref[...] = y_own
+
+
+def finish_rows(meta, chunk, kept, sent, y_out):
+    rows, dim = kept.shape
+    whole = pl.BlockSpec((rows, dim), lambda i, m: (0, 0))
+    return pl.pallas_call(
+        finish_kernel, name="finish_rows",
+        grid_spec=pltpu.PrefetchScalarGridSpec(
+            num_scalar_prefetch=1, grid=(1,), in_specs=[whole, whole, pl.BlockSpec(memory_space=pltpu.HBM)],
+            out_specs=[whole, pl.BlockSpec((rows, dim), lambda i, m: (2 * chunk + m[2], 0))]),
+        out_shape=[jax.ShapeDtypeStruct((rows, dim), BF16), jax.ShapeDtypeStruct(y_out.shape, BF16)],
+        input_output_aliases={3: 1},
+        compiler_params=params(("arbitrary",), 32),
+        cost_estimate=pl.CostEstimate(flops=rows * dim, bytes_accessed=12 * rows * dim, transcendentals=0),
+    )(meta, kept, sent, y_out)
+
+
+def place_kernel(meta_ref, piece_ref, y_in, y_ref):
+    y_ref[...] = piece_ref[...]
+
+
+def place_rows(meta, chunk, piece, y_out):
+    rows, dim = piece.shape
+    return pl.pallas_call(
+        place_kernel, name="place_rows",
+        grid_spec=pltpu.PrefetchScalarGridSpec(
+            num_scalar_prefetch=1, grid=(1,),
+            in_specs=[pl.BlockSpec((rows, dim), lambda i, m: (0, 0)), pl.BlockSpec(memory_space=pltpu.HBM)],
+            out_specs=pl.BlockSpec((rows, dim), lambda i, m: (2 * chunk + m[3], 0))),
+        out_shape=jax.ShapeDtypeStruct(y_out.shape, BF16),
+        input_output_aliases={2: 0},
+        compiler_params=params(("arbitrary",), 32),
+        cost_estimate=pl.CostEstimate(flops=rows * dim, bytes_accessed=4 * rows * dim, transcendentals=0),
+    )(meta, piece, y_out)
 
 
 def solution(mesh):
@@ -291,8 +331,11 @@
         depth = w_o.shape[0]
         quarter = depth // sp_size
         half_q = quarter // 2
-        wo_own = lax.ppermute(lax.dynamic_slice(w_o, (sp_idx * quarter, 0), (quarter, dim)), "tp", tp_swap)
-        wo_far = lax.ppermute(lax.dynamic_slice(w_o, ((sp_idx ^ 2) * quarter, 0), (half_q, dim)), "tp", tp_swap)
+
+        def wo_rows(index, second):
+            return lax.dynamic_slice(w_o, (index * quarter + second * half_q, 0), (half_q, dim))
+
+        wo_a = lax.ppermute(wo_rows(sp_idx, 0), "tp", tp_swap)
 
         zeros = jnp.sum((segments == 0).astype(jnp.int32)).reshape(1)
         zeros = zeros + lax.ppermute(zeros, "sp", core_swap)
@@ -308,11 +351,12 @@
         kv_parts = (kv_own, kv_core, kv_chip, kv_diag)
         q_rot = project_q(u, w_q, cos_t, sin_t)
 
-        wo_near = lax.ppermute(wo_own[half_q:], "sp", chip_swap)
-        wo_core = lax.ppermute(wo_own, "sp", core_swap)
-        wo_dfar = lax.ppermute(wo_far, "sp", core_swap)
-        wo_dnear = lax.ppermute(wo_near, "sp", core_swap)
-        wo_pieces = (wo_own, wo_core, wo_far, wo_near, wo_dfar, wo_dnear)
+        wo_b = lax.ppermute(wo_rows(sp_idx, 1), "tp", tp_swap)
+        wo_far = lax.ppermute(wo_rows(sp_idx ^ 2, 1), "tp", tp_swap)
+        wo_near = lax.ppermute(wo_a, "sp", chip_swap)
+        wo_core = [lax.ppermute(piece, "sp", core_swap) for piece in
+                   (wo_a, wo_b, wo_near, wo_far)]
+        wo_pieces = (wo_a, wo_b, wo_core[0], wo_core[1], wo_near, wo_far, wo_core[2], wo_core[3])
 
         def ordered(own, core, chip, diag):
             near = jnp.concatenate([jnp.where(odd, core, own), jnp.where(odd, own, core)], axis=0)
@@ -324,7 +368,6 @@
             return ordered(*cols).reshape(sp_size * rows_local, 1, HEAD_DIM)
 
         chunk_rows = rows_local // CHUNKS
-        half = chunk_rows // 2
         attn_flops = 4 * chunk_rows * sp_size * rows_local * w_q.shape[1] // 4
         split = CHUNKS // 2
         partial_sums = attention(meta, q_rot, kv_parts[:2], 0, split * chunk_rows, 512, attn_flops, False)
@@ -345,11 +388,12 @@
                                    w_gate, w_up, w_down)
             sent.append(lax.ppermute(p_peer, "tp", tp_swap))
             kept.append(p_own)
+        y_peer = []
         for c in range(CHUNKS):
-            y_own = lax.optimization_barrier((kept[c] + sent[c]).astype(BF16))
-            y_peer = lax.ppermute(y_own, "tp", tp_swap)
-            y_out = lax.dynamic_update_slice(y_out, y_own, (c * chunk_rows + tp_idx * half, 0))
-            y_out = lax.dynamic_update_slice(y_out, y_peer, (c * chunk_rows + (1 - tp_idx) * half, 0))
+            y_own, y_out = finish_rows(meta, c, kept[c], sent[c], y_out)
+            y_peer.append(lax.ppermute(y_own, "tp", tp_swap))
+        for c in range(CHUNKS):
+            y_out = place_rows(meta, c, y_peer[c], y_out)
         return y_out, k_cache, v_cache
 
 

time: 478 us -> 492 us (1.029)
  starting transfers between devices: 29.2 us -> 52.9 us
  Pallas kernels: 294 us -> 313 us
  waiting for transfers between devices: 114 us -> 97.5 us
  local copies, waits for them, and re-layouts: 14.8 us -> 8.49 us
  other arithmetic: 14.9 us -> 8.68 us
    ppermute x1, waiting for transfers between devices: 42.3 us -> 0.01 us  [layer(): kv_chip = lax.ppermute(kv_own, 'sp', chip_swap)]
    ppermute x1, starting transfers between devices: 3.84 us -> 35.5 us  [layer(): cut = (zeros + lax.ppermute(zeros, 'sp', chip_swap))[0]]
    ppermute x10 -> x12, waiting for transfers between devices: 40.5 us -> 66.9 us  [the longest x4 36 us: layer(): y_peer.append(lax.ppermute(y_own, 'tp', tp_swap))]
    pallas_call x0 -> x8, Pallas kernels: none -> 17.8 us  [the longest x4 12 us: finish_rows(): pl.pallas_call(finish_kernel, name='finish_rows', grid_spec=pltpu.Prefetc...]
    ppermute x10 -> x12, starting transfers between devices: 17.1 us -> 8.74 us  [the longest x4 4.05 us: layer(): y_peer.append(lax.ppermute(y_own, 'tp', tp_swap))]
    convert_element_type x4 -> x0, other arithmetic: 5.42 us -> none  [layer(): y_own = lax.optimization_barrier((kept[c] + sent[c]).astype(BF16))]
  transfers between devices with their start and end apart: 23 -> 25, of which waited for: 8 -> 6; matrix products, arithmetic and copies ran while one was open for 4% -> 2% of each run, Pallas kernels for 60% -> 61%
where the time goes in v3:
time: 492 us; the launch traced here: 483 us
  Pallas kernels  313 us (64%)
  waiting for transfers between devices  97.5 us (20%)
  starting transfers between devices  52.9 us (11%)
  other arithmetic  8.68 us (2%)
  local copies, waits for them, and re-layouts  8.49 us (2%)
    pallas_call x4, Pallas kernels, chunk_layer(): pl.pallas_call(functools.partial(chunk_kernel, heads, len(wo_pieces), out...  174 us
    pallas_call x5, Pallas kernels, attention(): pl.pallas_call(functools.partial(attn_kernel, group, row_base, parts, k_b...  91.6 us
    ppermute x4, waiting for transfers between devices, layer(): y_peer.append(lax.ppermute(y_own, 'tp', tp_swap))  36 us
    ppermute x1, starting transfers between devices, layer(): cut = (zeros + lax.ppermute(zeros, 'sp', chip_swap))[0]  35.5 us
    ppermute x4, waiting for transfers between devices, layer(): sent.append(lax.ppermute(p_peer, 'tp', tp_swap))  25.2 us
    ppermute x1, waiting for transfers between devices, layer(): wo_far = lax.ppermute(wo_rows(sp_idx ^ 2, 1), 'tp', tp_swap)  24.2 us
    pallas_call x1, Pallas kernels, project_q(): pl.pallas_call(q_kernel, grid=(width // block,), name='project_q', in_spe...  16 us
    pallas_call x1, Pallas kernels, project_kv(): pl.pallas_call(kv_kernel, grid=(rows // block,), name='project_kv', in_sp...  12.9 us
  transfers between devices with their start and end apart: 25, of which 6 were waited for; matrix products, arithmetic and copies ran while one was open for 2% of the time, Pallas kernels for 61%

profile of v3, /device:TPU:2, one launch (start us, length us, event | category | flops | bytes accessed | tf_op | source)
XLA Modules:
  0.0 483.4 jit_solution(16826380779362934998)
XLA Ops:
  4.0 12.9 %project_kv.1 = (bf16[1024,3072]{1,0:T(8,128)(2,1)}, bf16[1024,1024]{1,0:T(8,128)(2,1)}) custom-call(bf16[1024,3072]{1,0:T(8,128)(2,1)} %x_ref.9, f32[1,3072]{1,0:T(1,128)S(1)} %bitcast.10, bf16[3072,512]{1,0:T(8,128)(2,1)} %wk_ref.1, bf16[3072,512]{1,0:T(8,128)(2,1)} %wv_ref.1, f32[1024,128]{1,0:T(8,128)S(1)} %get-tuple-element.61.cos_ref, ...), custom_call_target="tpu_custom_call" | custom-call | flops 6442450944 | bytes 18874368 | tf_op jit(solution)/shard_map/project_kv/pallas_call | solution.py:65
  17.0 2.2 constant_dynamic-slice_fusion
  19.2 2.1 collective-permute-start.6
  22.4 3.2 collective-permute-done
  27.0 35.5 %collective-permute-start.1 = (s32[1]{0:T(128)}, s32[1]{0:T(128)}, u32[]{:S(2)}, u32[]{:S(2)}) collective-permute-start(s32[1]{0:T(128)} %add.45), channel_id=1, source_target_pairs={{0,2},{1,3},{2,0},{3,1},{4,6},{5,7},{6,4},{7,5}} | collective-permute-start | bytes 20 | tf_op jit(solution)/shard_map/ppermute | solution.py:342
  62.5 2.1 collective-permute-done.1
  66.7 6.8 %collective-permute-done.7.refs_5_ = bf16[192,3072]{1,0:T(8,128)(2,1)} collective-permute-done((bf16[192,3072]{1,0:T(8,128)(2,1)S(1)}, bf16[192,3072]{1,0:T(8,128)(2,1)}, u32[]{:S(2)}, u32[]{:S(2)}) %collective-permute-start.7) | collective-permute-done | bytes 1179680 | tf_op jit(solution)/shard_map/ppermute | solution.py:354
  73.5 24.2 %collective-permute-done.11.refs_9_ = bf16[192,3072]{1,0:T(8,128)(2,1)} collective-permute-done((bf16[192,3072]{1,0:T(8,128)(2,1)S(1)}, bf16[192,3072]{1,0:T(8,128)(2,1)}, u32[]{:S(2)}, u32[]{:S(2)}) %collective-permute-start.11) | collective-permute-done | bytes 1179680 | tf_op jit(solution)/shard_map/ppermute | solution.py:355
  99.5 16.0 %project_q.1.q_ref = bf16[1024,1536]{1,0:T(8,128)(2,1)S(1)} custom-call(bf16[1024,3072]{1,0:T(8,128)(2,1)} %get-tuple-element.24.u_ref, bf16[3072,1536]{1,0:T(8,128)(2,1)} %w_ref.1, f32[1024,128]{1,0:T(8,128)S(1)} %get-tuple-element.61.cos_ref, f32[1024,128]{1,0:T(8,128)S(1)} %get-tuple-element.60.sin_ref), custom_call_target="tpu_custom_call" | custom-call | flops 9663676416 | bytes 15728640 | tf_op jit(solution)/shard_map/project_q/pallas_call | solution.py:88
  119.6 22.5 %attention.6.a_ref = bf16[256,1536]{1,0:T(8,128)(2,1)S(1)} custom-call(s32[4]{0:T(128)S(1)} %pad_add_fusion.meta_ref, bf16[1024,1536]{1,0:T(8,128)(2,1)} %copy-done.4, bf16[1024,1024]{1,0:T(8,128)(2,1)} %get-tuple-element.25.refs_0_.refs_4_.refs_2_, bf16[1024,1024]{1,0:T(8,128)(2,1)S(1)} %copy-done.3, bf16[1024,1024]{1,0:T(8,128)(2,1)} %copy-done, ...), custom_call_target="tpu_custom_call" | custom-call | flops 1610612736 | bytes 16777216 | tf_op jit(solution)/shard_map/attention/pallas_call | solution.py:187
  143.8 12.7 %attention.7 = (f32[12,128,512]{2,1,0:T(8,128)}, f32[12,1,512]{2,1,0:T(1,128)S(1)}, f32[12,1,512]{2,1,0:T(1,128)S(1)}) custom-call(s32[4]{0:T(128)S(1)} %pad_add_fusion.meta_ref, bf16[1024,1536]{1,0:T(8,128)(2,1)} %copy-done.4, bf16[1024,1024]{1,0:T(8,128)(2,1)} %get-tuple-element.25.refs_0_.refs_4_.refs_2_, bf16[1024,1024]{1,0:T(8,128)(2,1)S(1)} %copy-done.3, ...), custom_call_target="tpu_custom_call" | custom-call | flops 1610612736 | bytes 16777216 | tf_op jit(solution)/shard_map/attention/pallas_call | solution.py:187
  156.5 24.4 %attention.5.a_ref = bf16[256,1536]{1,0:T(8,128)(2,1)S(1)} custom-call(s32[4]{0:T(128)S(1)} %pad_add_fusion.meta_ref, bf16[1024,1536]{1,0:T(8,128)(2,1)} %copy-done.4, bf16[1024,1024]{1,0:T(8,128)(2,1)} %get-tuple-element.25.refs_0_.refs_4_.refs_2_, bf16[1024,1024]{1,0:T(8,128)(2,1)S(1)} %copy-done.3, bf16[1024,1024]{1,0:T(8,128)(2,1)} %copy-done, ...), custom_call_target="tpu_custom_call" | custom-call | flops 1610612736 | bytes 16777216 | tf_op jit(solution)/shard_map/attention/pallas_call | solution.py:187
  180.9 16.0 %attention.8.a_ref = bf16[256,1536]{1,0:T(8,128)(2,1)} custom-call(s32[4]{0:T(128)S(1)} %pad_add_fusion.meta_ref, bf16[1024,1536]{1,0:T(8,128)(2,1)} %copy-done.4, bf16[1024,1024]{1,0:T(8,128)(2,1)S(1)} %copy-done.1, bf16[1024,1024]{1,0:T(8,128)(2,1)} %collective-permute-done.4.refs_3_.refs_7_.refs_1_, bf16[1024,1024]{1,0:T(8,128)(2,1)S(1)} %copy-done.1, ...), custom_call_target="tpu_custom_call" | custom-call | flops 1610612736 | bytes 16777216 | tf_op jit(solution)/shard_map/attention/pallas_call | solution.py:187
  196.9 16.0 %attention.9.a_ref = bf16[256,1536]{1,0:T(8,128)(2,1)} custom-call(s32[4]{0:T(128)S(1)} %pad_add_fusion.meta_ref, bf16[1024,1536]{1,0:T(8,128)(2,1)} %copy-done.4, bf16[1024,1024]{1,0:T(8,128)(2,1)S(1)} %copy-done.1, bf16[1024,1024]{1,0:T(8,128)(2,1)} %collective-permute-done.4.refs_3_.refs_7_.refs_1_, bf16[1024,1024]{1,0:T(8,128)(2,1)S(1)} %copy-done.1, ...), custom_call_target="tpu_custom_call" | custom-call | flops 1610612736 | bytes 16777216 | tf_op jit(solution)/shard_map/attention/pallas_call | solution.py:187
  216.2 43.6 %chunk_layer.5 = (f32[128,3072]{1,0:T(8,128)}, f32[128,3072]{1,0:T(8,128)}) custom-call(s32[4]{0:T(128)} %copy-done.11, bf16[1024,3072]{1,0:T(8,128)(2,1)} %x_ref.9, bf16[256,1536]{1,0:T(8,128)(2,1)} %copy-done.6, bf16[256,1536]{1,0:T(8,128)(2,1)} %copy-done.14, f32[1,3072]{1,0:T(1,128)} %bitcast.11, bf16[1536,3072]{1,0:T(8,128)(2,1)} %refs_3_.7, ...), custom_call_target="tpu_custom_call" | custom-call | flops 24159191040 | bytes 75497472 | tf_op jit(solution)/shard_map/chunk_layer/pallas_call | solution.py:252
  261.6 43.5 %chunk_layer.6 = (f32[128,3072]{1,0:T(8,128)}, f32[128,3072]{1,0:T(8,128)}) custom-call(s32[4]{0:T(128)} %copy-done.11, bf16[1024,3072]{1,0:T(8,128)(2,1)} %x_ref.9, bf16[256,1536]{1,0:T(8,128)(2,1)} %attention.8.a_ref, bf16[256,1536]{1,0:T(8,128)(2,1)} %collective-permute-done.17.b_ref, f32[1,3072]{1,0:T(1,128)} %bitcast.12, bf16[1536,3072]{1,0:T(8,128)(2,1)} %refs_3_.7, ...), custom_call_target="tpu_custom_call" | custom-call | flops 24159191040 | bytes 75497472 | tf_op jit(solution)/shard_map/chunk_layer/pallas_call | solution.py:252
  305.4 43.5 %chunk_layer.7 = (f32[128,3072]{1,0:T(8,128)}, f32[128,3072]{1,0:T(8,128)}) custom-call(s32[4]{0:T(128)} %copy-done.11, bf16[1024,3072]{1,0:T(8,128)(2,1)} %x_ref.9, bf16[256,1536]{1,0:T(8,128)(2,1)} %attention.9.a_ref, bf16[256,1536]{1,0:T(8,128)(2,1)} %collective-permute-done.19.b_ref, f32[1,3072]{1,0:T(1,128)} %bitcast.13, bf16[1536,3072]{1,0:T(8,128)(2,1)} %refs_3_.7, ...), custom_call_target="tpu_custom_call" | custom-call | flops 24159191040 | bytes 75497472 | tf_op jit(solution)/shard_map/chunk_layer/pallas_call | solution.py:252
  350.7 43.7 %chunk_layer.4 = (f32[128,3072]{1,0:T(8,128)}, f32[128,3072]{1,0:T(8,128)}) custom-call(s32[4]{0:T(128)} %copy-done.11, bf16[1024,3072]{1,0:T(8,128)(2,1)} %x_ref.9, bf16[256,1536]{1,0:T(8,128)(2,1)} %copy-done.5, bf16[256,1536]{1,0:T(8,128)(2,1)} %collective-permute-done.5.b_ref, f32[1,3072]{1,0:T(1,128)} %bitcast.14, bf16[1536,3072]{1,0:T(8,128)(2,1)} %refs_3_.7, ...), custom_call_target="tpu_custom_call" | custom-call | flops 24159191040 | bytes 75497472 | tf_op jit(solution)/shard_map/chunk_layer/pallas_call | solution.py:252
  397.8 3.0 finish_rows.4
  400.8 3.0 finish_rows.5
  403.8 3.0 finish_rows.6
  406.8 25.2 %collective-permute-done.14.sent_ref = f32[128,3072]{1,0:T(8,128)} collective-permute-done((f32[128,3072]{1,0:T(8,128)}, f32[128,3072]{1,0:T(8,128)}, u32[]{:S(2)}, u32[]{:S(2)}) %collective-permute-start.14) | collective-permute-done | bytes 1572896 | tf_op jit(solution)/shard_map/ppermute | solution.py:389
  432.0 3.0 finish_rows.7
  441.3 35.9 %collective-permute-done.24.piece_ref = bf16[128,3072]{1,0:T(8,128)(2,1)S(1)} collective-permute-done((bf16[128,3072]{1,0:T(8,128)(2,1)S(1)}, bf16[128,3072]{1,0:T(8,128)(2,1)S(1)}, u32[]{:S(2)}, u32[]{:S(2)}) %collective-permute-start.24) | collective-permute-done | bytes 786464 | tf_op jit(solution)/shard_map/ppermute | solution.py:394
  (91 shorter events, 36.3 us)
Async XLA Ops:
  17.0 49.7 %collective-permute-start.3 = (bf16[1024,1024]{1,0:T(8,128)(2,1)}, bf16[1024,1024]{1,0:T(8,128)(2,1)S(1)}, u32[]{:S(2)}, u32[]{:S(2)}) collective-permute-start(bf16[1024,1024]{1,0:T(8,128)(2,1)} %get-tuple-element.25.refs_0_.refs_4_.refs_2_), channel_id=1, source_target_pairs={{0,2},{1,3},{2,0},{3,1},{4,6},{5,7},{6,4},{7,5}} | collective-permute-start | bytes 6291464 | tf_op jit(solution)/shard_map/ppermute | solution.py:348
  19.2 46.9 %collective-permute-start.6 = (bf16[192,3072]{1,0:T(8,128)(2,1)S(1)}, bf16[192,3072]{1,0:T(8,128)(2,1)}, u32[]{:S(2)}, u32[]{:S(2)}) collective-permute-start(bf16[192,3072]{1,0:T(8,128)(2,1)S(1)} %get-tuple-element.47), channel_id=1, source_target_pairs={{0,4},{4,0},{1,5},{5,1},{2,6},{6,2},{3,7},{7,3}} | collective-permute-start | bytes 3538952 | tf_op jit(solution)/shard_map/ppermute | solution.py:338
  21.3 76.4 %collective-permute-start.2 = (bf16[1024,1024]{1,0:T(8,128)(2,1)}, bf16[1024,1024]{1,0:T(8,128)(2,1)S(1)}, u32[]{:S(2)}, u32[]{:S(2)}) collective-permute-start(bf16[1024,1024]{1,0:T(8,128)(2,1)} %get-tuple-element.25.refs_0_.refs_4_.refs_2_), channel_id=1, source_target_pairs={{0,1},{1,0},{2,3},{3,2},{4,5},{5,4},{6,7},{7,6}} | collective-permute-start | bytes 6291464 | tf_op jit(solution)/shard_map/ppermute | solution.py:349
  22.4 51.1 %collective-permute-start.7 = (bf16[192,3072]{1,0:T(8,128)(2,1)S(1)}, bf16[192,3072]{1,0:T(8,128)(2,1)}, u32[]{:S(2)}, u32[]{:S(2)}) collective-permute-start(bf16[192,3072]{1,0:T(8,128)(2,1)S(1)} %get-tuple-element.46), channel_id=1, source_target_pairs={{0,4},{4,0},{1,5},{5,1},{2,6},{6,2},{3,7},{7,3}} | collective-permute-start | bytes 3538952 | tf_op jit(solution)/shard_map/ppermute | solution.py:354
  27.0 37.6 %collective-permute-start.1 = (s32[1]{0:T(128)}, s32[1]{0:T(128)}, u32[]{:S(2)}, u32[]{:S(2)}) collective-permute-start(s32[1]{0:T(128)} %add.45), channel_id=1, source_target_pairs={{0,2},{1,3},{2,0},{3,1},{4,6},{5,7},{6,4},{7,5}} | collective-permute-start | bytes 20 | tf_op jit(solution)/shard_map/ppermute | solution.py:342
  64.6 33.0 %collective-permute-start.11 = (bf16[192,3072]{1,0:T(8,128)(2,1)S(1)}, bf16[192,3072]{1,0:T(8,128)(2,1)}, u32[]{:S(2)}, u32[]{:S(2)}) collective-permute-start(bf16[192,3072]{1,0:T(8,128)(2,1)S(1)} %get-tuple-element.45), channel_id=1, source_target_pairs={{0,4},{4,0},{1,5},{5,1},{2,6},{6,2},{3,7},{7,3}} | collective-permute-start | bytes 3538952 | tf_op jit(solution)/shard_map/ppermute | solution.py:355
  66.1 33.4 %collective-permute-start.10 = (bf16[192,3072]{1,0:T(8,128)(2,1)}, bf16[192,3072]{1,0:T(8,128)(2,1)}, u32[]{:S(2)}, u32[]{:S(2)}) collective-permute-start(bf16[192,3072]{1,0:T(8,128)(2,1)} %collective-permute-done.6.refs_4_), channel_id=1, source_target_pairs={{0,2},{1,3},{2,0},{3,1},{4,6},{5,7},{6,4},{7,5}} | collective-permute-start | bytes 3538952 | tf_op jit(solution)/shard_map/ppermute | solution.py:356
  66.7 51.3 %collective-permute-start.4 = (bf16[1024,1024]{1,0:T(8,128)(2,1)S(1)}, bf16[1024,1024]{1,0:T(8,128)(2,1)}, u32[]{:S(2)}, u32[]{:S(2)}) collective-permute-start(bf16[1024,1024]{1,0:T(8,128)(2,1)S(1)} %collective-permute-done.3.refs_2_.refs_6_.refs_0_), channel_id=1, source_target_pairs={{0,1},{1,0},{2,3},{3,2},{4,5},{5,4},{6,7},{7,6}} | collective-permute-start | bytes 6291464 | tf_op jit(solution)/shard_map/ppermute | solution.py:350
  73.5 139.5 %collective-permute-start.8 = (bf16[192,3072]{1,0:T(8,128)(2,1)}, bf16[192,3072]{1,0:T(8,128)(2,1)}, u32[]{:S(2)}, u32[]{:S(2)}) collective-permute-start(bf16[192,3072]{1,0:T(8,128)(2,1)} %collective-permute-done.6.refs_4_), channel_id=1, source_target_pairs={{0,1},{1,0},{2,3},{3,2},{4,5},{5,4},{6,7},{7,6}} | collective-permute-start | bytes 3538952 | tf_op jit(solution)/shard_map/ppermute | solution.py:357
  97.6 115.7 %collective-permute-start.9 = (bf16[192,3072]{1,0:T(8,128)(2,1)}, bf16[192,3072]{1,0:T(8,128)(2,1)}, u32[]{:S(2)}, u32[]{:S(2)}) collective-permute-start(bf16[192,3072]{1,0:T(8,128)(2,1)} %collective-permute-done.7.refs_5_), channel_id=1, source_target_pairs={{0,1},{1,0},{2,3},{3,2},{4,5},{5,4},{6,7},{7,6}} | collective-permute-start | bytes 3538952 | tf_op jit(solution)/shard_map/ppermute | solution.py:357
  99.0 116.0 %collective-permute-start.13 = (bf16[192,3072]{1,0:T(8,128)(2,1)}, bf16[192,3072]{1,0:T(8,128)(2,1)}, u32[]{:S(2)}, u32[]{:S(2)}) collective-permute-start(bf16[192,3072]{1,0:T(8,128)(2,1)} %collective-permute-done.11.refs_9_), channel_id=1, source_target_pairs={{0,1},{1,0},{2,3},{3,2},{4,5},{5,4},{6,7},{7,6}} | collective-permute-start | bytes 3538952 | tf_op jit(solution)/shard_map/ppermute | solution.py:357
  99.5 115.8 %collective-permute-start.12 = (bf16[192,3072]{1,0:T(8,128)(2,1)}, bf16[192,3072]{1,0:T(8,128)(2,1)}, u32[]{:S(2)}, u32[]{:S(2)}) collective-permute-start(bf16[192,3072]{1,0:T(8,128)(2,1)} %collective-permute-done.10.refs_8_), channel_id=1, source_target_pairs={{0,1},{1,0},{2,3},{3,2},{4,5},{5,4},{6,7},{7,6}} | collective-permute-start | bytes 3538952 | tf_op jit(solution)/shard_map/ppermute | solution.py:357
  142.1 73.2 %collective-permute-start.15 = (bf16[256,1536]{1,0:T(8,128)(2,1)S(1)}, bf16[256,1536]{1,0:T(8,128)(2,1)S(1)}, u32[]{:S(2)}, u32[]{:S(2)}) collective-permute-start(bf16[256,1536]{1,0:T(8,128)(2,1)S(1)} %attention.6.a_ref), channel_id=1, source_target_pairs={{0,4},{4,0},{1,5},{5,1},{2,6},{6,2},{3,7},{7,3}} | collective-permute-start | bytes 2359304 | tf_op jit(solution)/shard_map/ppermute | solution.py:381
  213.0 137.7 %collective-permute-start.5 = (bf16[256,1536]{1,0:T(8,128)(2,1)S(1)}, bf16[256,1536]{1,0:T(8,128)(2,1)}, u32[]{:S(2)}, u32[]{:S(2)}) collective-permute-start(bf16[256,1536]{1,0:T(8,128)(2,1)S(1)} %attention.5.a_ref), channel_id=1, source_target_pairs={{0,4},{4,0},{1,5},{5,1},{2,6},{6,2},{3,7},{7,3}} | collective-permute-start | bytes 2359304 | tf_op jit(solution)/shard_map/ppermute | solution.py:381
  213.3 48.3 %collective-permute-start.17 = (bf16[256,1536]{1,0:T(8,128)(2,1)}, bf16[256,1536]{1,0:T(8,128)(2,1)}, u32[]{:S(2)}, u32[]{:S(2)}) collective-permute-start(bf16[256,1536]{1,0:T(8,128)(2,1)} %attention.8.a_ref), channel_id=1, source_target_pairs={{0,4},{4,0},{1,5},{5,1},{2,6},{6,2},{3,7},{7,3}} | collective-permute-start | bytes 2359304 | tf_op jit(solution)/shard_map/ppermute | solution.py:381
  215.1 90.4 %collective-permute-start.19 = (bf16[256,1536]{1,0:T(8,128)(2,1)}, bf16[256,1536]{1,0:T(8,128)(2,1)}, u32[]{:S(2)}, u32[]{:S(2)}) collective-permute-start(bf16[256,1536]{1,0:T(8,128)(2,1)} %attention.9.a_ref), channel_id=1, source_target_pairs={{0,4},{4,0},{1,5},{5,1},{2,6},{6,2},{3,7},{7,3}} | collective-permute-start | bytes 2359304 | tf_op jit(solution)/shard_map/ppermute | solution.py:381
  259.8 144.0 %collective-permute-start.16 = (f32[128,3072]{1,0:T(8,128)}, f32[128,3072]{1,0:T(8,128)}, u32[]{:S(2)}, u32[]{:S(2)}) collective-permute-start(f32[128,3072]{1,0:T(8,128)} %get-tuple-element.29), channel_id=1, source_target_pairs={{0,4},{4,0},{1,5},{5,1},{2,6},{6,2},{3,7},{7,3}} | collective-permute-start | bytes 4718600 | tf_op jit(solution)/shard_map/ppermute | solution.py:389
  305.2 95.6 %collective-permute-start.18 = (f32[128,3072]{1,0:T(8,128)}, f32[128,3072]{1,0:T(8,128)}, u32[]{:S(2)}, u32[]{:S(2)}) collective-permute-start(f32[128,3072]{1,0:T(8,128)} %get-tuple-element.34), channel_id=1, source_target_pairs={{0,4},{4,0},{1,5},{5,1},{2,6},{6,2},{3,7},{7,3}} | collective-permute-start | bytes 4718600 | tf_op jit(solution)/shard_map/ppermute | solution.py:389
  348.9 48.8 %collective-permute-start.20 = (f32[128,3072]{1,0:T(8,128)}, f32[128,3072]{1,0:T(8,128)}, u32[]{:S(2)}, u32[]{:S(2)}) collective-permute-start(f32[128,3072]{1,0:T(8,128)} %get-tuple-element.36), channel_id=1, source_target_pairs={{0,4},{4,0},{1,5},{5,1},{2,6},{6,2},{3,7},{7,3}} | collective-permute-start | bytes 4718600 | tf_op jit(solution)/shard_map/ppermute | solution.py:389
  394.4 37.6 %collective-permute-start.14 = (f32[128,3072]{1,0:T(8,128)}, f32[128,3072]{1,0:T(8,128)}, u32[]{:S(2)}, u32[]{:S(2)}) collective-permute-start(f32[128,3072]{1,0:T(8,128)} %get-tuple-element.27), channel_id=1, source_target_pairs={{0,4},{4,0},{1,5},{5,1},{2,6},{6,2},{3,7},{7,3}} | collective-permute-start | bytes 4718600 | tf_op jit(solution)/shard_map/ppermute | solution.py:389
  435.0 46.7 %collective-permute-start.21 = (bf16[128,3072]{1,0:T(8,128)(2,1)S(1)}, bf16[128,3072]{1,0:T(8,128)(2,1)S(1)}, u32[]{:S(2)}, u32[]{:S(2)}) collective-permute-start(bf16[128,3072]{1,0:T(8,128)(2,1)S(1)} %get-tuple-element.40), channel_id=1, source_target_pairs={{0,4},{4,0},{1,5},{5,1},{2,6},{6,2},{3,7},{7,3}} | collective-permute-start | bytes 2359304 | tf_op jit(solution)/shard_map/ppermute | solution.py:394
  435.3 45.0 %collective-permute-start.22 = (bf16[128,3072]{1,0:T(8,128)(2,1)S(1)}, bf16[128,3072]{1,0:T(8,128)(2,1)S(1)}, u32[]{:S(2)}, u32[]{:S(2)}) collective-permute-start(bf16[128,3072]{1,0:T(8,128)(2,1)S(1)} %get-tuple-element.41), channel_id=1, source_target_pairs={{0,4},{4,0},{1,5},{5,1},{2,6},{6,2},{3,7},{7,3}} | collective-permute-start | bytes 2359304 | tf_op jit(solution)/shard_map/ppermute | solution.py:394
  437.0 41.7 %collective-permute-start.23 = (bf16[128,3072]{1,0:T(8,128)(2,1)S(1)}, bf16[128,3072]{1,0:T(8,128)(2,1)S(1)}, u32[]{:S(2)}, u32[]{:S(2)}) collective-permute-start(bf16[128,3072]{1,0:T(8,128)(2,1)S(1)} %get-tuple-element.42), channel_id=1, source_target_pairs={{0,4},{4,0},{1,5},{5,1},{2,6},{6,2},{3,7},{7,3}} | collective-permute-start | bytes 2359304 | tf_op jit(solution)/shard_map/ppermute | solution.py:394
  437.3 40.0 %collective-permute-start.24 = (bf16[128,3072]{1,0:T(8,128)(2,1)S(1)}, bf16[128,3072]{1,0:T(8,128)(2,1)S(1)}, u32[]{:S(2)}, u32[]{:S(2)}) collective-permute-start(bf16[128,3072]{1,0:T(8,128)(2,1)S(1)} %get-tuple-element.43), channel_id=1, source_target_pairs={{0,4},{4,0},{1,5},{5,1},{2,6},{6,2},{3,7},{7,3}} | collective-permute-start | bytes 2359304 | tf_op jit(solution)/shard_map/ppermute | solution.py:394
  (17 other events, 250.6 us)

commit v4 on v3

--- a/solution.py
+++ b/solution.py
@@ -18,6 +18,7 @@
 CHUNKS = 4
 Q_BLOCK = 256
 FF_BLOCK = 512
+HEAD_GROUPS = 4
 MASKED = -1e30
 
 
@@ -200,70 +201,106 @@
     )(meta, q_rot, *kv_parts, *kv_parts, *(partial_sums or ()))
 
 
-def chunk_kernel(mine, peer, out_steps, meta_ref, x_ref, a_ref, b_ref, gain_ref, *refs):
-    wa_refs, wb_refs = refs[:mine], refs[mine:mine + peer]
-    wg_ref, wu_ref, wd_ref, send_ref, keep_ref, mid_ref, u_ref, acc_ref, wa_all, wb_all = refs[mine + peer:]
-    step = pl.program_id(0)
+def chunk_kernel(pieces, x_ref, a_ref, b_ref, gain_ref, wo_ref, *refs):
+    piece_refs, (wg_ref, wu_ref, wd_ref, send_ref, keep_ref) = refs[:pieces], refs[pieces:pieces + 5]
+    mid_ref, u_ref, acc_ref, wa_buf, wb_buf, wg_buf, wu_buf, wd_buf, wo_sem, mlp_sem = refs[pieces + 5:]
+    tp_idx, sp_idx = lax.axis_index("tp"), lax.axis_index("sp")
     half = send_ref.shape[0]
-    own = pl.ds(pl.multiple_of(meta_ref[2] * half, half), half)
-    other = pl.ds(pl.multiple_of(meta_ref[3] * half, half), half)
-
-    @pl.when(step < out_steps)
-    def _():
-        width = wa_all.shape[1]
-        for pieces, whole in ((wa_refs, wa_all), (wb_refs, wb_all)):
-            top = 0
-            for piece in pieces:
-                whole[top:top + piece.shape[0], :] = piece[...]
-                top += piece.shape[0]
+    own = pl.ds(pl.multiple_of(tp_idx * half, half), half)
+    other = pl.ds(pl.multiple_of((1 - tp_idx) * half, half), half)
+    depth, width = wa_buf.shape[1:]
+    quarter = depth // HEAD_GROUPS
+    out_steps = wo_ref.shape[1] // width
+    mlp_steps = wg_ref.shape[1] // FF_BLOCK
+
+    def wo_copies(step, slot):
         cols = pl.ds(pl.multiple_of(step * width, width), width)
-        mid_ref[:, cols] = x_ref[...].astype(F32) + (dot(a_ref[...], wa_all[...]) + dot(b_ref[...], wb_all[...]))
-
-    @pl.when(step == out_steps - 1)
-    def _():
-        u_ref[:half, :] = normed(mid_ref[other, :], gain_ref[...])
-        u_ref[half:, :] = normed(mid_ref[own, :], gain_ref[...])
-        acc_ref[...] = jnp.zeros_like(acc_ref)
-
-    @pl.when(step >= out_steps)
-    def _():
+        copies, top = [], 0
+        for p in range(HEAD_GROUPS):
+            rows = pl.ds(pl.multiple_of((p ^ sp_idx) * quarter, quarter), quarter)
+            copies.append((wo_ref.at[rows, cols], wa_buf.at[slot, p * quarter:(p + 1) * quarter, :]))
+        for piece in piece_refs:
+            rows = piece.shape[0]
+            copies.append((piece.at[:, cols], wb_buf.at[slot, top:top + rows, :]))
+            top += rows
+        return [pltpu.make_async_copy(src, dst, wo_sem.at[slot, n]) for n, (src, dst) in enumerate(copies)]
+
+    def mlp_copies(step, slot):
+        cols = pl.ds(pl.multiple_of(step * FF_BLOCK, FF_BLOCK), FF_BLOCK)
+        copies = ((wg_ref.at[:, cols], wg_buf.at[slot]), (wu_ref.at[:, cols], wu_buf.at[slot]), (wd_ref.at[cols, :], wd_buf.at[slot]))
+        return [pltpu.make_async_copy(src, dst, mlp_sem.at[slot, n]) for n, (src, dst) in enumerate(copies)]
+
+    def start(copies):
+        for copy in copies:
+            copy.start()
+
+    def finish(copies):
+        for copy in copies:
+            copy.wait()
+
+    start(wo_copies(0, 0))
+    start(wo_copies(1, 1))
+    acc_ref[...] = jnp.zeros_like(acc_ref)
+
+    def out_step(step, carry):
+        slot = step % 2
+        finish(wo_copies(step, slot))
+        cols = pl.ds(pl.multiple_of(step * width, width), width)
+        mid_ref[:, cols] = x_ref[:, cols].astype(F32) + (dot(a_ref[...], wa_buf[slot]) + dot(b_ref[...], wb_buf[slot]))
+
+        @pl.when(step + 2 < out_steps)
+        def _():
+            start(wo_copies(step + 2, slot))
+
+        @pl.when(step == out_steps - 3)
+        def _():
+            start(mlp_copies(0, 0))
+
+        return carry
+
+    lax.fori_loop(0, out_steps, out_step, 0)
+    start(mlp_copies(1, 1))
+    u_ref[:half, :] = normed(mid_ref[other, :], gain_ref[...])
+    u_ref[half:, :] = normed(mid_ref[own, :], gain_ref[...])
+
+    def mlp_step(step, carry):
+        slot = step % 2
+        finish(mlp_copies(step, slot))
         u = u_ref[...]
-        gate = dot(u, wg_ref[...])
-        hidden = (gate * jax.nn.sigmoid(gate) * dot(u, wu_ref[...])).astype(BF16)
-        acc_ref[...] += dot(hidden, wd_ref[...])
-
-    @pl.when(step == pl.num_programs(0) - 1)
-    def _():
-        send_ref[...] = acc_ref[:half, :]
-        keep_ref[...] = mid_ref[own, :] + acc_ref[half:, :]
-
-
-def chunk_layer(meta, x, chunk, attn_mine, attn_peer, wo_mine, wo_pieces, gain, w_gate, w_up, w_down):
+        gate = dot(u, wg_buf[slot])
+        hidden = (gate * jax.nn.sigmoid(gate) * dot(u, wu_buf[slot])).astype(BF16)
+        acc_ref[...] += dot(hidden, wd_buf[slot])
+
+        @pl.when(step + 2 < mlp_steps)
+        def _():
+            start(mlp_copies(step + 2, slot))
+
+        return carry
+
+    lax.fori_loop(0, mlp_steps, mlp_step, 0)
+    send_ref[...] = acc_ref[:half, :]
+    keep_ref[...] = mid_ref[own, :] + acc_ref[half:, :]
+
+
+def chunk_layer(x, chunk, attn_mine, attn_peer, wo_mine, wo_pieces, gain, w_gate, w_up, w_down):
     rows, depth = attn_mine.shape
     dim, ff = w_gate.shape
-    block = 512
-    out_steps, mlp_steps = dim // block, ff // FF_BLOCK
-    heads = 4
-    resident = lambda a, b: pl.BlockSpec((a, b), lambda i, m: (0, 0))
-    early = lambda i: jnp.minimum(i, out_steps - 1)
-    late = lambda i: jnp.maximum(i - out_steps, 0)
-    mine_specs = [pl.BlockSpec((depth // heads, block), lambda i, m, p=p: (p ^ m[0], early(i))) for p in range(heads)]
-    peer_specs = [pl.BlockSpec((w.shape[0], block), lambda i, m: (0, early(i))) for w in wo_pieces]
-    return pl.pallas_call(
-        functools.partial(chunk_kernel, heads, len(wo_pieces), out_steps), name="chunk_layer",
-        grid_spec=pltpu.PrefetchScalarGridSpec(
-            num_scalar_prefetch=1, grid=(out_steps + mlp_steps,),
-            in_specs=[pl.BlockSpec((rows, block), lambda i, m: (chunk, early(i))), resident(rows, depth), resident(rows, depth),
-                      resident(1, dim)] + mine_specs + peer_specs
-                     + [pl.BlockSpec((dim, FF_BLOCK), lambda i, m: (0, late(i))), pl.BlockSpec((dim, FF_BLOCK), lambda i, m: (0, late(i))),
-                        pl.BlockSpec((FF_BLOCK, dim), lambda i, m: (late(i), 0))],
-            out_specs=[resident(rows // 2, dim)] * 2,
-            scratch_shapes=[pltpu.VMEM((rows, dim), F32), pltpu.VMEM((rows, dim), BF16), pltpu.VMEM((rows, dim), F32),
-                            pltpu.VMEM((depth, block), BF16), pltpu.VMEM((depth, block), BF16)]),
+    width = 512
+    whole = lambda a, b: pl.BlockSpec((a, b), lambda i: (0, 0))
+    raw = pl.BlockSpec(memory_space=pltpu.HBM)
+    pieces = len(wo_pieces)
+    return pl.pallas_call(
+        functools.partial(chunk_kernel, pieces), name="chunk_layer", grid=(1,),
+        in_specs=[pl.BlockSpec((rows, dim), lambda i: (chunk, 0)), whole(rows, depth), whole(rows, depth), whole(1, dim)] + [raw] * (pieces + 4),
+        out_specs=[whole(rows // 2, dim)] * 2,
+        scratch_shapes=[pltpu.VMEM((rows, dim), F32), pltpu.VMEM((rows, dim), BF16), pltpu.VMEM((rows, dim), F32),
+                        pltpu.VMEM((2, depth, width), BF16), pltpu.VMEM((2, depth, width), BF16),
+                        pltpu.VMEM((2, dim, FF_BLOCK), BF16), pltpu.VMEM((2, dim, FF_BLOCK), BF16), pltpu.VMEM((2, FF_BLOCK, dim), BF16),
+                        pltpu.SemaphoreType.DMA((2, HEAD_GROUPS + pieces)), pltpu.SemaphoreType.DMA((2, 3))],
         out_shape=[jax.ShapeDtypeStruct((rows // 2, dim), F32)] * 2,
         compiler_params=params(("arbitrary",), 60),
         cost_estimate=pl.CostEstimate(flops=4 * rows * depth * dim + 6 * rows * dim * ff, bytes_accessed=6 * dim * ff, transcendentals=0),
-    )(meta, x, attn_mine, attn_peer, gain, *([wo_mine] * heads), *wo_pieces, w_gate, w_up, w_down)
+    )(x, attn_mine, attn_peer, gain, wo_mine, *wo_pieces, w_gate, w_up, w_down)
 
 
 def unwritten(shape, dtype):
@@ -332,8 +369,8 @@
         quarter = depth // sp_size
         half_q = quarter // 2
 
-        def wo_rows(index, second):
-            return lax.dynamic_slice(w_o, (index * quarter + second * half_q, 0), (half_q, dim))
+        def wo_rows(index, second, weights=w_o):
+            return lax.dynamic_slice(weights, (index * quarter + second * half_q, 0), (half_q, dim))
 
         wo_a = lax.ppermute(wo_rows(sp_idx, 0), "tp", tp_swap)
 
@@ -349,10 +386,11 @@
         kv_core = lax.ppermute(kv_own, "sp", core_swap)
         kv_diag = lax.ppermute(kv_chip, "sp", core_swap)
         kv_parts = (kv_own, kv_core, kv_chip, kv_diag)
+
+        late_w_o, u = lax.optimization_barrier((w_o, u))
+        wo_b = lax.ppermute(wo_rows(sp_idx, 1, late_w_o), "tp", tp_swap)
+        wo_far = lax.ppermute(wo_rows(sp_idx ^ 2, 1, late_w_o), "tp", tp_swap)
         q_rot = project_q(u, w_q, cos_t, sin_t)
-
-        wo_b = lax.ppermute(wo_rows(sp_idx, 1), "tp", tp_swap)
-        wo_far = lax.ppermute(wo_rows(sp_idx ^ 2, 1), "tp", tp_swap)
         wo_near = lax.ppermute(wo_a, "sp", chip_swap)
         wo_core = [lax.ppermute(piece, "sp", core_swap) for piece in
                    (wo_a, wo_b, wo_near, wo_far)]
@@ -384,7 +422,7 @@
 
         kept, sent = [], []
         for c in range(CHUNKS):
-            p_peer, p_own = chunk_layer(meta, x_in, c, attn_mine[c], attn_peer[c], w_o, wo_pieces, gain_m,
+            p_peer, p_own = chunk_layer(x_in, c, attn_mine[c], attn_peer[c], w_o, wo_pieces, gain_m,
                                    w_gate, w_up, w_down)
             sent.append(lax.ppermute(p_peer, "tp", tp_swap))
             kept.append(p_own)

time: 492 us -> 469 us (0.953)
  Pallas kernels: 313 us -> 288 us
    pallas_call x4, Pallas kernels: 174 us -> 148 us  [chunk_layer(): pl.pallas_call(functools.partial(chunk_kernel, pieces), name='chunk_layer...]
    ppermute x4, waiting for transfers between devices: 36 us -> 41.7 us  [layer(): y_peer.append(lax.ppermute(y_own, 'tp', tp_swap))]
  transfers between devices with their start and end apart: 25 -> 25, of which waited for: 6 -> 6; matrix products, arithmetic and copies ran while one was open for 2% -> 2% of each run, Pallas kernels for 61% -> 59%
where the time goes in v4:
time: 469 us; the launch traced here: 460 us
  Pallas kernels  288 us (61%)
  waiting for transfers between devices  101 us (22%)
  starting transfers between devices  52.8 us (11%)
  other arithmetic  8.67 us (2%)
  local copies, waits for them, and re-layouts  7.47 us (2%)
    pallas_call x4, Pallas kernels, chunk_layer(): pl.pallas_call(functools.partial(chunk_kernel, pieces), name='chunk_layer...  148 us
    pallas_call x5, Pallas kernels, attention(): pl.pallas_call(functools.partial(attn_kernel, group, row_base, parts, k_b...  92.5 us
    ppermute x4, waiting for transfers between devices, layer(): y_peer.append(lax.ppermute(y_own, 'tp', tp_swap))  41.7 us
    ppermute x1, starting transfers between devices, layer(): cut = (zeros + lax.ppermute(zeros, 'sp', chip_swap))[0]  35.3 us
    ppermute x4, waiting for transfers between devices, layer(): sent.append(lax.ppermute(p_peer, 'tp', tp_swap))  24.4 us
    ppermute x1, waiting for transfers between devices, layer(): wo_b = lax.ppermute(wo_rows(sp_idx, 1, late_w_o), 'tp', tp_swap)  24.1 us
    pallas_call x1, Pallas kernels, project_q(): pl.pallas_call(q_kernel, grid=(width // block,), name='project_q', in_spe...  16.1 us
    pallas_call x1, Pallas kernels, project_kv(): pl.pallas_call(kv_kernel, grid=(rows // block,), name='project_kv', in_sp...  13 us
  transfers between devices with their start and end apart: 25, of which 6 were waited for; matrix products, arithmetic and copies ran while one was open for 2% of the time, Pallas kernels for 59%

profile of v4, /device:TPU:2, one launch (start us, length us, event | category | flops | bytes accessed | tf_op | source)
XLA Modules:
  0.0 460.4 jit_solution(11256032846892253444)
XLA Ops:
  4.0 13.0 %project_kv.1 = (bf16[1024,3072]{1,0:T(8,128)(2,1)}, bf16[1024,1024]{1,0:T(8,128)(2,1)}) custom-call(bf16[1024,3072]{1,0:T(8,128)(2,1)} %x_ref.9, f32[1,3072]{1,0:T(1,128)S(1)} %bitcast.10, bf16[3072,512]{1,0:T(8,128)(2,1)} %wk_ref.1, bf16[3072,512]{1,0:T(8,128)(2,1)} %wv_ref.1, f32[1024,128]{1,0:T(8,128)S(1)} %get-tuple-element.64.cos_ref, ...), custom_call_target="tpu_custom_call" | custom-call | flops 6442450944 | bytes 18874368 | tf_op jit(solution)/shard_map/project_kv/pallas_call | solution.py:66
  17.1 2.4 constant_dynamic-slice_fusion.2
  19.5 2.0 collective-permute-start.6
  27.2 35.3 %collective-permute-start.1 = (s32[1]{0:T(128)}, s32[1]{0:T(128)}, u32[]{:S(2)}, u32[]{:S(2)}) collective-permute-start(s32[1]{0:T(128)} %add.45), channel_id=1, source_target_pairs={{0,2},{1,3},{2,0},{3,1},{4,6},{5,7},{6,4},{7,5}} | collective-permute-start | bytes 20 | tf_op jit(solution)/shard_map/ppermute | solution.py:379
  62.6 2.2 collective-permute-done.1
  66.8 7.1 %collective-permute-done.11.refs_5_ = bf16[192,3072]{1,0:T(8,128)(2,1)} collective-permute-done((bf16[192,3072]{1,0:T(8,128)(2,1)S(1)}, bf16[192,3072]{1,0:T(8,128)(2,1)}, u32[]{:S(2)}, u32[]{:S(2)}) %collective-permute-start.11) | collective-permute-done | bytes 1179680 | tf_op jit(solution)/shard_map/ppermute | solution.py:392
  73.9 24.1 %collective-permute-done.7.refs_1_ = bf16[192,3072]{1,0:T(8,128)(2,1)} collective-permute-done((bf16[192,3072]{1,0:T(8,128)(2,1)S(1)}, bf16[192,3072]{1,0:T(8,128)(2,1)}, u32[]{:S(2)}, u32[]{:S(2)}) %collective-permute-start.7) | collective-permute-done | bytes 1179680 | tf_op jit(solution)/shard_map/ppermute | solution.py:391
  98.6 16.1 %project_q.1.q_ref = bf16[1024,1536]{1,0:T(8,128)(2,1)S(1)} custom-call(bf16[1024,3072]{1,0:T(8,128)(2,1)} %get-tuple-element.27.u_ref, bf16[3072,1536]{1,0:T(8,128)(2,1)} %w_ref.1, f32[1024,128]{1,0:T(8,128)S(1)} %get-tuple-element.64.cos_ref, f32[1024,128]{1,0:T(8,128)S(1)} %get-tuple-element.63.sin_ref), custom_call_target="tpu_custom_call" | custom-call | flops 9663676416 | bytes 15728640 | tf_op jit(solution)/shard_map/project_q/pallas_call | solution.py:89
  117.1 22.6 %attention.6.a_ref = bf16[256,1536]{1,0:T(8,128)(2,1)S(1)} custom-call(s32[4]{0:T(128)S(1)} %pad_add_fusion.meta_ref, bf16[1024,1536]{1,0:T(8,128)(2,1)} %copy-done.2, bf16[1024,1024]{1,0:T(8,128)(2,1)} %get-tuple-element.28.refs_0_.refs_4_.refs_2_, bf16[1024,1024]{1,0:T(8,128)(2,1)} %collective-permute-done.2.refs_1_.refs_5_.refs_3_, ...), custom_call_target="tpu_custom_call" | custom-call | flops 1610612736 | bytes 16777216 | tf_op jit(solution)/shard_map/attention/pallas_call | solution.py:188
  141.5 13.0 %attention.7 = (f32[12,128,512]{2,1,0:T(8,128)}, f32[12,1,512]{2,1,0:T(1,128)S(1)}, f32[12,1,512]{2,1,0:T(1,128)S(1)}) custom-call(s32[4]{0:T(128)S(1)} %pad_add_fusion.meta_ref, bf16[1024,1536]{1,0:T(8,128)(2,1)} %copy-done.2, bf16[1024,1024]{1,0:T(8,128)(2,1)} %get-tuple-element.28.refs_0_.refs_4_.refs_2_, ...), custom_call_target="tpu_custom_call" | custom-call | flops 1610612736 | bytes 16777216 | tf_op jit(solution)/shard_map/attention/pallas_call | solution.py:188
  154.6 24.5 %attention.5.a_ref = bf16[256,1536]{1,0:T(8,128)(2,1)S(1)} custom-call(s32[4]{0:T(128)S(1)} %pad_add_fusion.meta_ref, bf16[1024,1536]{1,0:T(8,128)(2,1)} %copy-done.2, bf16[1024,1024]{1,0:T(8,128)(2,1)} %get-tuple-element.28.refs_0_.refs_4_.refs_2_, bf16[1024,1024]{1,0:T(8,128)(2,1)} %collective-permute-done.2.refs_1_.refs_5_.refs_3_, ...), custom_call_target="tpu_custom_call" | custom-call | flops 1610612736 | bytes 16777216 | tf_op jit(solution)/shard_map/attention/pallas_call | solution.py:188
  179.1 16.2 %attention.9.a_ref = bf16[256,1536]{1,0:T(8,128)(2,1)} custom-call(s32[4]{0:T(128)S(1)} %pad_add_fusion.meta_ref, bf16[1024,1536]{1,0:T(8,128)(2,1)} %copy-done.2, bf16[1024,1024]{1,0:T(8,128)(2,1)S(1)} %copy-done.1, bf16[1024,1024]{1,0:T(8,128)(2,1)} %collective-permute-done.4.refs_3_.refs_7_.refs_1_, bf16[1024,1024]{1,0:T(8,128)(2,1)S(1)} %copy-done.1, ...), custom_call_target="tpu_custom_call" | custom-call | flops 1610612736 | bytes 16777216 | tf_op jit(solution)/shard_map/attention/pallas_call | solution.py:188
  195.3 16.2 %attention.8.a_ref = bf16[256,1536]{1,0:T(8,128)(2,1)} custom-call(s32[4]{0:T(128)S(1)} %pad_add_fusion.meta_ref, bf16[1024,1536]{1,0:T(8,128)(2,1)} %copy-done.2, bf16[1024,1024]{1,0:T(8,128)(2,1)S(1)} %copy-done.1, bf16[1024,1024]{1,0:T(8,128)(2,1)} %collective-permute-done.4.refs_3_.refs_7_.refs_1_, bf16[1024,1024]{1,0:T(8,128)(2,1)S(1)} %copy-done.1, ...), custom_call_target="tpu_custom_call" | custom-call | flops 1610612736 | bytes 16777216 | tf_op jit(solution)/shard_map/attention/pallas_call | solution.py:188
  214.7 36.8 %chunk_layer.5 = (f32[128,3072]{1,0:T(8,128)}, f32[128,3072]{1,0:T(8,128)}) custom-call(bf16[1024,3072]{1,0:T(8,128)(2,1)} %x_ref.9, bf16[256,1536]{1,0:T(8,128)(2,1)} %copy-done.4, bf16[256,1536]{1,0:T(8,128)(2,1)} %copy-done.10, f32[1,3072]{1,0:T(1,128)} %bitcast.11, bf16[1536,3072]{1,0:T(8,128)(2,1)} %wo_ref.7, ...), custom_call_target="tpu_custom_call" | custom-call | flops 24159191040 | bytes 75497472 | tf_op jit(solution)/shard_map/chunk_layer/pallas_call | solution.py:292
  253.3 37.0 %chunk_layer.6 = (f32[128,3072]{1,0:T(8,128)}, f32[128,3072]{1,0:T(8,128)}) custom-call(bf16[1024,3072]{1,0:T(8,128)(2,1)} %x_ref.9, bf16[256,1536]{1,0:T(8,128)(2,1)} %attention.8.a_ref, bf16[256,1536]{1,0:T(8,128)(2,1)} %collective-permute-done.17.b_ref, f32[1,3072]{1,0:T(1,128)} %bitcast.12, bf16[1536,3072]{1,0:T(8,128)(2,1)} %wo_ref.7, ...), custom_call_target="tpu_custom_call" | custom-call | flops 24159191040 | bytes 75497472 | tf_op jit(solution)/shard_map/chunk_layer/pallas_call | solution.py:292
  290.6 37.0 %chunk_layer.7 = (f32[128,3072]{1,0:T(8,128)}, f32[128,3072]{1,0:T(8,128)}) custom-call(bf16[1024,3072]{1,0:T(8,128)(2,1)} %x_ref.9, bf16[256,1536]{1,0:T(8,128)(2,1)} %attention.9.a_ref, bf16[256,1536]{1,0:T(8,128)(2,1)} %collective-permute-done.19.b_ref, f32[1,3072]{1,0:T(1,128)} %bitcast.13, bf16[1536,3072]{1,0:T(8,128)(2,1)} %wo_ref.7, ...), custom_call_target="tpu_custom_call" | custom-call | flops 24159191040 | bytes 75497472 | tf_op jit(solution)/shard_map/chunk_layer/pallas_call | solution.py:292
  329.4 36.9 %chunk_layer.4 = (f32[128,3072]{1,0:T(8,128)}, f32[128,3072]{1,0:T(8,128)}) custom-call(bf16[1024,3072]{1,0:T(8,128)(2,1)} %x_ref.9, bf16[256,1536]{1,0:T(8,128)(2,1)} %copy-done.3, bf16[256,1536]{1,0:T(8,128)(2,1)} %collective-permute-done.5.b_ref, f32[1,3072]{1,0:T(1,128)} %bitcast.14, bf16[1536,3072]{1,0:T(8,128)(2,1)} %wo_ref.7, ...), custom_call_target="tpu_custom_call" | custom-call | flops 24159191040 | bytes 75497472 | tf_op jit(solution)/shard_map/chunk_layer/pallas_call | solution.py:292
  369.6 3.1 finish_rows.4
  372.7 3.1 finish_rows.5
  375.8 3.1 finish_rows.6
  378.8 24.4 %collective-permute-done.14.sent_ref = f32[128,3072]{1,0:T(8,128)} collective-permute-done((f32[128,3072]{1,0:T(8,128)}, f32[128,3072]{1,0:T(8,128)}, u32[]{:S(2)}, u32[]{:S(2)}) %collective-permute-start.14) | collective-permute-done | bytes 1572896 | tf_op jit(solution)/shard_map/ppermute | solution.py:427
  403.2 3.1 finish_rows.7
  406.3 2.0 collective-permute-start.22
  412.6 41.7 %collective-permute-done.24.piece_ref = bf16[128,3072]{1,0:T(8,128)(2,1)S(1)} collective-permute-done((bf16[128,3072]{1,0:T(8,128)(2,1)S(1)}, bf16[128,3072]{1,0:T(8,128)(2,1)S(1)}, u32[]{:S(2)}, u32[]{:S(2)}) %collective-permute-start.24) | collective-permute-done | bytes 786464 | tf_op jit(solution)/shard_map/ppermute | solution.py:432
  (84 shorter events, 34.6 us)
Async XLA Ops:
  17.1 49.8 %collective-permute-start.3 = (bf16[1024,1024]{1,0:T(8,128)(2,1)}, bf16[1024,1024]{1,0:T(8,128)(2,1)S(1)}, u32[]{:S(2)}, u32[]{:S(2)}) collective-permute-start(bf16[1024,1024]{1,0:T(8,128)(2,1)} %get-tuple-element.28.refs_0_.refs_4_.refs_2_), channel_id=1, source_target_pairs={{0,2},{1,3},{2,0},{3,1},{4,6},{5,7},{6,4},{7,5}} | collective-permute-start | bytes 6291464 | tf_op jit(solution)/shard_map/ppermute | solution.py:385
  19.5 46.8 %collective-permute-start.6 = (bf16[192,3072]{1,0:T(8,128)(2,1)}, bf16[192,3072]{1,0:T(8,128)(2,1)}, u32[]{:S(2)}, u32[]{:S(2)}) collective-permute-start(bf16[192,3072]{1,0:T(8,128)(2,1)} %constant_dynamic-slice_fusion.2), channel_id=1, source_target_pairs={{0,4},{4,0},{1,5},{5,1},{2,6},{6,2},{3,7},{7,3}} | collective-permute-start | bytes 3538952 | tf_op jit(solution)/shard_map/ppermute | solution.py:375
  21.5 76.6 %collective-permute-start.2 = (bf16[1024,1024]{1,0:T(8,128)(2,1)}, bf16[1024,1024]{1,0:T(8,128)(2,1)}, u32[]{:S(2)}, u32[]{:S(2)}) collective-permute-start(bf16[1024,1024]{1,0:T(8,128)(2,1)} %get-tuple-element.28.refs_0_.refs_4_.refs_2_), channel_id=1, source_target_pairs={{0,1},{1,0},{2,3},{3,2},{4,5},{5,4},{6,7},{7,6}} | collective-permute-start | bytes 6291464 | tf_op jit(solution)/shard_map/ppermute | solution.py:386
  24.4 49.5 %collective-permute-start.11 = (bf16[192,3072]{1,0:T(8,128)(2,1)S(1)}, bf16[192,3072]{1,0:T(8,128)(2,1)}, u32[]{:S(2)}, u32[]{:S(2)}) collective-permute-start(bf16[192,3072]{1,0:T(8,128)(2,1)S(1)} %get-tuple-element.49), channel_id=1, source_target_pairs={{0,4},{4,0},{1,5},{5,1},{2,6},{6,2},{3,7},{7,3}} | collective-permute-start | bytes 3538952 | tf_op jit(solution)/shard_map/ppermute | solution.py:392
  27.2 37.5 %collective-permute-start.1 = (s32[1]{0:T(128)}, s32[1]{0:T(128)}, u32[]{:S(2)}, u32[]{:S(2)}) collective-permute-start(s32[1]{0:T(128)} %add.45), channel_id=1, source_target_pairs={{0,2},{1,3},{2,0},{3,1},{4,6},{5,7},{6,4},{7,5}} | collective-permute-start | bytes 20 | tf_op jit(solution)/shard_map/ppermute | solution.py:379
  64.8 33.3 %collective-permute-start.7 = (bf16[192,3072]{1,0:T(8,128)(2,1)S(1)}, bf16[192,3072]{1,0:T(8,128)(2,1)}, u32[]{:S(2)}, u32[]{:S(2)}) collective-permute-start(bf16[192,3072]{1,0:T(8,128)(2,1)S(1)} %get-tuple-element.50), channel_id=1, source_target_pairs={{0,4},{4,0},{1,5},{5,1},{2,6},{6,2},{3,7},{7,3}} | collective-permute-start | bytes 3538952 | tf_op jit(solution)/shard_map/ppermute | solution.py:391
  66.3 32.3 %collective-permute-start.10 = (bf16[192,3072]{1,0:T(8,128)(2,1)}, bf16[192,3072]{1,0:T(8,128)(2,1)}, u32[]{:S(2)}, u32[]{:S(2)}) collective-permute-start(bf16[192,3072]{1,0:T(8,128)(2,1)} %collective-permute-done.6.refs_0_), channel_id=1, source_target_pairs={{0,2},{1,3},{2,0},{3,1},{4,6},{5,7},{6,4},{7,5}} | collective-permute-start | bytes 3538952 | tf_op jit(solution)/shard_map/ppermute | solution.py:394
  66.8 50.3 %collective-permute-start.4 = (bf16[1024,1024]{1,0:T(8,128)(2,1)S(1)}, bf16[1024,1024]{1,0:T(8,128)(2,1)}, u32[]{:S(2)}, u32[]{:S(2)}) collective-permute-start(bf16[1024,1024]{1,0:T(8,128)(2,1)S(1)} %collective-permute-done.3.refs_2_.refs_6_.refs_0_), channel_id=1, source_target_pairs={{0,1},{1,0},{2,3},{3,2},{4,5},{5,4},{6,7},{7,6}} | collective-permute-start | bytes 6291464 | tf_op jit(solution)/shard_map/ppermute | solution.py:387
  73.9 137.5 %collective-permute-start.8 = (bf16[192,3072]{1,0:T(8,128)(2,1)}, bf16[192,3072]{1,0:T(8,128)(2,1)}, u32[]{:S(2)}, u32[]{:S(2)}) collective-permute-start(bf16[192,3072]{1,0:T(8,128)(2,1)} %collective-permute-done.6.refs_0_), channel_id=1, source_target_pairs={{0,1},{1,0},{2,3},{3,2},{4,5},{5,4},{6,7},{7,6}} | collective-permute-start | bytes 3538952 | tf_op jit(solution)/shard_map/ppermute | solution.py:395
  98.1 113.7 %collective-permute-start.13 = (bf16[192,3072]{1,0:T(8,128)(2,1)}, bf16[192,3072]{1,0:T(8,128)(2,1)}, u32[]{:S(2)}, u32[]{:S(2)}) collective-permute-start(bf16[192,3072]{1,0:T(8,128)(2,1)} %collective-permute-done.11.refs_5_), channel_id=1, source_target_pairs={{0,1},{1,0},{2,3},{3,2},{4,5},{5,4},{6,7},{7,6}} | collective-permute-start | bytes 3538952 | tf_op jit(solution)/shard_map/ppermute | solution.py:395
  98.1 115.4 %collective-permute-start.9 = (bf16[192,3072]{1,0:T(8,128)(2,1)}, bf16[192,3072]{1,0:T(8,128)(2,1)}, u32[]{:S(2)}, u32[]{:S(2)}) collective-permute-start(bf16[192,3072]{1,0:T(8,128)(2,1)} %collective-permute-done.7.refs_1_), channel_id=1, source_target_pairs={{0,1},{1,0},{2,3},{3,2},{4,5},{5,4},{6,7},{7,6}} | collective-permute-start | bytes 3538952 | tf_op jit(solution)/shard_map/ppermute | solution.py:395
  98.6 115.2 %collective-permute-start.12 = (bf16[192,3072]{1,0:T(8,128)(2,1)}, bf16[192,3072]{1,0:T(8,128)(2,1)}, u32[]{:S(2)}, u32[]{:S(2)}) collective-permute-start(bf16[192,3072]{1,0:T(8,128)(2,1)} %collective-permute-done.10.refs_4_), channel_id=1, source_target_pairs={{0,1},{1,0},{2,3},{3,2},{4,5},{5,4},{6,7},{7,6}} | collective-permute-start | bytes 3538952 | tf_op jit(solution)/shard_map/ppermute | solution.py:395
  139.8 74.1 %collective-permute-start.15 = (bf16[256,1536]{1,0:T(8,128)(2,1)S(1)}, bf16[256,1536]{1,0:T(8,128)(2,1)S(1)}, u32[]{:S(2)}, u32[]{:S(2)}) collective-permute-start(bf16[256,1536]{1,0:T(8,128)(2,1)S(1)} %attention.6.a_ref), channel_id=1, source_target_pairs={{0,4},{4,0},{1,5},{5,1},{2,6},{6,2},{3,7},{7,3}} | collective-permute-start | bytes 2359304 | tf_op jit(solution)/shard_map/ppermute | solution.py:419
  211.5 117.9 %collective-permute-start.5 = (bf16[256,1536]{1,0:T(8,128)(2,1)S(1)}, bf16[256,1536]{1,0:T(8,128)(2,1)}, u32[]{:S(2)}, u32[]{:S(2)}) collective-permute-start(bf16[256,1536]{1,0:T(8,128)(2,1)S(1)} %attention.5.a_ref), channel_id=1, source_target_pairs={{0,4},{4,0},{1,5},{5,1},{2,6},{6,2},{3,7},{7,3}} | collective-permute-start | bytes 2359304 | tf_op jit(solution)/shard_map/ppermute | solution.py:419
  211.8 41.5 %collective-permute-start.17 = (bf16[256,1536]{1,0:T(8,128)(2,1)}, bf16[256,1536]{1,0:T(8,128)(2,1)}, u32[]{:S(2)}, u32[]{:S(2)}) collective-permute-start(bf16[256,1536]{1,0:T(8,128)(2,1)} %attention.8.a_ref), channel_id=1, source_target_pairs={{0,4},{4,0},{1,5},{5,1},{2,6},{6,2},{3,7},{7,3}} | collective-permute-start | bytes 2359304 | tf_op jit(solution)/shard_map/ppermute | solution.py:419
  213.5 77.1 %collective-permute-start.19 = (bf16[256,1536]{1,0:T(8,128)(2,1)}, bf16[256,1536]{1,0:T(8,128)(2,1)}, u32[]{:S(2)}, u32[]{:S(2)}) collective-permute-start(bf16[256,1536]{1,0:T(8,128)(2,1)} %attention.9.a_ref), channel_id=1, source_target_pairs={{0,4},{4,0},{1,5},{5,1},{2,6},{6,2},{3,7},{7,3}} | collective-permute-start | bytes 2359304 | tf_op jit(solution)/shard_map/ppermute | solution.py:419
  251.6 124.2 %collective-permute-start.16 = (f32[128,3072]{1,0:T(8,128)}, f32[128,3072]{1,0:T(8,128)}, u32[]{:S(2)}, u32[]{:S(2)}) collective-permute-start(f32[128,3072]{1,0:T(8,128)} %get-tuple-element.33), channel_id=1, source_target_pairs={{0,4},{4,0},{1,5},{5,1},{2,6},{6,2},{3,7},{7,3}} | collective-permute-start | bytes 4718600 | tf_op jit(solution)/shard_map/ppermute | solution.py:427
  290.3 82.4 %collective-permute-start.18 = (f32[128,3072]{1,0:T(8,128)}, f32[128,3072]{1,0:T(8,128)}, u32[]{:S(2)}, u32[]{:S(2)}) collective-permute-start(f32[128,3072]{1,0:T(8,128)} %get-tuple-element.38), channel_id=1, source_target_pairs={{0,4},{4,0},{1,5},{5,1},{2,6},{6,2},{3,7},{7,3}} | collective-permute-start | bytes 4718600 | tf_op jit(solution)/shard_map/ppermute | solution.py:427
  327.6 42.0 %collective-permute-start.20 = (f32[128,3072]{1,0:T(8,128)}, f32[128,3072]{1,0:T(8,128)}, u32[]{:S(2)}, u32[]{:S(2)}) collective-permute-start(f32[128,3072]{1,0:T(8,128)} %get-tuple-element.40), channel_id=1, source_target_pairs={{0,4},{4,0},{1,5},{5,1},{2,6},{6,2},{3,7},{7,3}} | collective-permute-start | bytes 4718600 | tf_op jit(solution)/shard_map/ppermute | solution.py:427
  366.3 37.0 %collective-permute-start.14 = (f32[128,3072]{1,0:T(8,128)}, f32[128,3072]{1,0:T(8,128)}, u32[]{:S(2)}, u32[]{:S(2)}) collective-permute-start(f32[128,3072]{1,0:T(8,128)} %get-tuple-element.31), channel_id=1, source_target_pairs={{0,4},{4,0},{1,5},{5,1},{2,6},{6,2},{3,7},{7,3}} | collective-permute-start | bytes 4718600 | tf_op jit(solution)/shard_map/ppermute | solution.py:427
  406.3 52.4 %collective-permute-start.21 = (bf16[128,3072]{1,0:T(8,128)(2,1)S(1)}, bf16[128,3072]{1,0:T(8,128)(2,1)S(1)}, u32[]{:S(2)}, u32[]{:S(2)}) collective-permute-start(bf16[128,3072]{1,0:T(8,128)(2,1)S(1)} %get-tuple-element.44), channel_id=1, source_target_pairs={{0,4},{4,0},{1,5},{5,1},{2,6},{6,2},{3,7},{7,3}} | collective-permute-start | bytes 2359304 | tf_op jit(solution)/shard_map/ppermute | solution.py:432
  406.3 51.0 %collective-permute-start.22 = (bf16[128,3072]{1,0:T(8,128)(2,1)S(1)}, bf16[128,3072]{1,0:T(8,128)(2,1)S(1)}, u32[]{:S(2)}, u32[]{:S(2)}) collective-permute-start(bf16[128,3072]{1,0:T(8,128)(2,1)S(1)} %get-tuple-element.45), channel_id=1, source_target_pairs={{0,4},{4,0},{1,5},{5,1},{2,6},{6,2},{3,7},{7,3}} | collective-permute-start | bytes 2359304 | tf_op jit(solution)/shard_map/ppermute | solution.py:432
  408.3 47.5 %collective-permute-start.23 = (bf16[128,3072]{1,0:T(8,128)(2,1)S(1)}, bf16[128,3072]{1,0:T(8,128)(2,1)S(1)}, u32[]{:S(2)}, u32[]{:S(2)}) collective-permute-start(bf16[128,3072]{1,0:T(8,128)(2,1)S(1)} %get-tuple-element.46), channel_id=1, source_target_pairs={{0,4},{4,0},{1,5},{5,1},{2,6},{6,2},{3,7},{7,3}} | collective-permute-start | bytes 2359304 | tf_op jit(solution)/shard_map/ppermute | solution.py:432
  408.3 46.0 %collective-permute-start.24 = (bf16[128,3072]{1,0:T(8,128)(2,1)S(1)}, bf16[128,3072]{1,0:T(8,128)(2,1)S(1)}, u32[]{:S(2)}, u32[]{:S(2)}) collective-permute-start(bf16[128,3072]{1,0:T(8,128)(2,1)S(1)} %get-tuple-element.47), channel_id=1, source_target_pairs={{0,4},{4,0},{1,5},{5,1},{2,6},{6,2},{3,7},{7,3}} | collective-permute-start | bytes 2359304 | tf_op jit(solution)/shard_map/ppermute | solution.py:432
  (13 other events, 166.5 us)

commit v5 on v4

--- a/solution.py
+++ b/solution.py
@@ -16,8 +16,8 @@
 F32 = jnp.float32
 
 CHUNKS = 4
-Q_BLOCK = 256
 FF_BLOCK = 512
+FINE_BLOCK = 512
 HEAD_GROUPS = 4
 MASKED = -1e30
 
@@ -82,14 +82,13 @@
         store_rotated(q_ref, rows, dot(u_ref[rows, :], w_ref[...]), cos_ref[rows, :], sin_ref[rows, :])
 
 
-def project_q(u, w_q, cos_t, sin_t):
-    rows, dim = u.shape
-    width = w_q.shape[1]
+def project_q(u, w_q, cos_t, sin_t, first, rows):
+    dim, width = w_q.shape
     block = 512
+    banded = lambda b: pl.BlockSpec((rows, b), lambda i: (first // rows, 0))
     return pl.pallas_call(
         q_kernel, grid=(width // block,), name="project_q",
-        in_specs=[pl.BlockSpec((rows, dim), lambda i: (0, 0)), pl.BlockSpec((dim, block), lambda i: (0, i)),
-                  pl.BlockSpec((rows, HEAD_DIM), lambda i: (0, 0)), pl.BlockSpec((rows, HEAD_DIM), lambda i: (0, 0))],
+        in_specs=[banded(dim), pl.BlockSpec((dim, block), lambda i: (0, i)), banded(HEAD_DIM), banded(HEAD_DIM)],
         out_specs=pl.BlockSpec((rows, block), lambda i: (0, i)),
         out_shape=jax.ShapeDtypeStruct((rows, width), BF16),
         compiler_params=params(("arbitrary",), 48),
@@ -131,17 +130,20 @@
         l_ref[...] = jnp.zeros_like(l_ref)
         acc_ref[...] = jnp.zeros_like(acc_ref)
 
+    fine = min(k_block, FINE_BLOCK)
+
     def step(masked, kb, carry):
-        start = kb * k_block
-        rows = pl.ds(pl.multiple_of(start - base, k_block), k_block)
+        size = fine if masked else k_block
+        start = kb * size
+        rows = pl.ds(pl.multiple_of(start - base, size), size)
         k_blk = k_all[rows, :]
         v_blk = v_all[:, rows]
         scores = [dot(k_blk, q_t[head]) for head in range(group)]
         m_old = [m_ref[head] for head in range(group)]
         l_old = [l_ref[head] for head in range(group)]
         if masked:
-            k_idx = start + lax.broadcasted_iota(jnp.int32, (k_block, block), 0)
-            r_idx = first + lax.broadcasted_iota(jnp.int32, (k_block, block), 1)
+            k_idx = start + lax.broadcasted_iota(jnp.int32, (size, block), 0)
+            r_idx = first + lax.broadcasted_iota(jnp.int32, (size, block), 1)
             allowed = (k_idx <= r_idx) & ((k_idx >= cut) | (r_idx < cut))
             scores = [jnp.where(allowed, s, MASKED) for s in scores]
         news = []
@@ -163,10 +165,14 @@
     clear = (seg_high + k_block - 1) // k_block
     edge_a = jnp.maximum(low, jnp.minimum(clear, high))
     edge_b = jnp.maximum(edge_a, jnp.minimum((first + 1) // k_block, high))
-    head_count = edge_a - low
     lax.fori_loop(edge_a, edge_b, functools.partial(step, False), 0)
-    lax.fori_loop(0, head_count + jnp.maximum(high - edge_b, 0),
-                  lambda i, carry: step(True, jnp.where(i < head_count, low + i, edge_b + i - head_count), carry), 0)
+    ratio = k_block // fine
+    fine_low = jnp.maximum(seg_low, base) // fine
+    fine_high = chip_base // fine if load else last // fine + 1
+    head_count = jnp.maximum(jnp.minimum(edge_a * ratio, fine_high) - fine_low, 0)
+    fine_rest = jnp.maximum(edge_b * ratio, fine_low)
+    lax.fori_loop(0, head_count + jnp.maximum(fine_high - fine_rest, 0),
+                  lambda i, carry: step(True, jnp.where(i < head_count, fine_low + i, fine_rest + i - head_count), carry), 0)
     if finish:
         for head in range(group):
             o_ref[:, head * HEAD_DIM:(head + 1) * HEAD_DIM] = (acc_ref[head] / l_ref[head]).T.astype(BF16)
@@ -174,27 +180,27 @@
         acc_out[...], m_out[...], l_out[...] = acc_ref[...], m_ref[...], l_ref[...]
 
 
-def attention(meta, q_rot, kv_parts, row_base, rows, k_block, flops, finish=True, partial_sums=None):
+def attention(meta, q_rot, q_base, kv_parts, row_base, rows, q_block, k_block, flops, finish=True, partial_sums=None):
     kv_rows, kv_width = kv_parts[0].shape
     kv_heads = kv_width // (2 * HEAD_DIM)
     group = q_rot.shape[1] // HEAD_DIM // kv_heads
     width = group * HEAD_DIM
-    base = row_base // Q_BLOCK
+    base = row_base // q_block
     parts, load = len(kv_parts), partial_sums is not None
     k_spec = pl.BlockSpec((kv_rows, HEAD_DIM), lambda h, i, m: (0, h))
     v_spec = pl.BlockSpec((kv_rows, HEAD_DIM), lambda h, i, m: (0, kv_heads + h))
-    sums_specs = [pl.BlockSpec((group, depth, Q_BLOCK), lambda h, i, m: (h, 0, base + i)) for depth in (HEAD_DIM, 1, 1)]
+    sums_specs = [pl.BlockSpec((group, depth, q_block), lambda h, i, m: (h, 0, base + i)) for depth in (HEAD_DIM, 1, 1)]
     sums_shapes = [jax.ShapeDtypeStruct((kv_heads * group, depth, rows), F32) for depth in (HEAD_DIM, 1, 1)]
     return pl.pallas_call(
         functools.partial(attn_kernel, group, row_base, parts, k_block, load, finish), name="attention",
         grid_spec=pltpu.PrefetchScalarGridSpec(
-            num_scalar_prefetch=1, grid=(kv_heads, rows // Q_BLOCK),
-            in_specs=[pl.BlockSpec((Q_BLOCK, width), lambda h, i, m: (base + i, h))] + [k_spec] * parts + [v_spec] * parts
+            num_scalar_prefetch=1, grid=(kv_heads, rows // q_block),
+            in_specs=[pl.BlockSpec((q_block, width), lambda h, i, m: (q_base // q_block + i, h))] + [k_spec] * parts + [v_spec] * parts
                      + (sums_specs if load else []),
-            out_specs=pl.BlockSpec((Q_BLOCK, width), lambda h, i, m: (i, h ^ m[0])) if finish else sums_specs,
+            out_specs=pl.BlockSpec((q_block, width), lambda h, i, m: (i, h ^ m[0])) if finish else sums_specs,
             scratch_shapes=[pltpu.VMEM((parts * kv_rows, HEAD_DIM), BF16), pltpu.VMEM((HEAD_DIM, parts * kv_rows), BF16),
-                            pltpu.VMEM((group, HEAD_DIM, Q_BLOCK), BF16), pltpu.VMEM((group, 1, Q_BLOCK), F32),
-                            pltpu.VMEM((group, 1, Q_BLOCK), F32), pltpu.VMEM((group, HEAD_DIM, Q_BLOCK), F32)]),
+                            pltpu.VMEM((group, HEAD_DIM, q_block), BF16), pltpu.VMEM((group, 1, q_block), F32),
+                            pltpu.VMEM((group, 1, q_block), F32), pltpu.VMEM((group, HEAD_DIM, q_block), F32)]),
         out_shape=jax.ShapeDtypeStruct((rows, kv_heads * width), BF16) if finish else sums_shapes,
         compiler_params=params(("arbitrary", "arbitrary"), 48),
         cost_estimate=pl.CostEstimate(flops=flops, bytes_accessed=16 << 20, transcendentals=0),
@@ -203,11 +209,9 @@
 
 def chunk_kernel(pieces, x_ref, a_ref, b_ref, gain_ref, wo_ref, *refs):
     piece_refs, (wg_ref, wu_ref, wd_ref, send_ref, keep_ref) = refs[:pieces], refs[pieces:pieces + 5]
-    mid_ref, u_ref, acc_ref, wa_buf, wb_buf, wg_buf, wu_buf, wd_buf, wo_sem, mlp_sem = refs[pieces + 5:]
+    mid_ref, u_ref, wa_buf, wb_buf, wg_buf, wu_buf, wd_buf, wo_sem, mlp_sem = refs[pieces + 5:]
     tp_idx, sp_idx = lax.axis_index("tp"), lax.axis_index("sp")
     half = send_ref.shape[0]
-    own = pl.ds(pl.multiple_of(tp_idx * half, half), half)
-    other = pl.ds(pl.multiple_of((1 - tp_idx) * half, half), half)
     depth, width = wa_buf.shape[1:]
     quarter = depth // HEAD_GROUPS
     out_steps = wo_ref.shape[1] // width
@@ -240,7 +244,7 @@
 
     start(wo_copies(0, 0))
     start(wo_copies(1, 1))
-    acc_ref[...] = jnp.zeros_like(acc_ref)
+    send_ref[...] = jnp.zeros_like(send_ref)
 
     def out_step(step, carry):
         slot = step % 2
@@ -260,8 +264,13 @@
 
     lax.fori_loop(0, out_steps, out_step, 0)
     start(mlp_copies(1, 1))
-    u_ref[:half, :] = normed(mid_ref[other, :], gain_ref[...])
-    u_ref[half:, :] = normed(mid_ref[own, :], gain_ref[...])
+
+    keep_ref[...] = mid_ref[pl.ds(pl.multiple_of(tp_idx * half, half), half), :]
+
+    @pl.loop(0, 2)
+    def _(i):
+        u_ref[pl.ds(pl.multiple_of(i * half, half), half), :] = normed(
+            mid_ref[pl.ds(pl.multiple_of((tp_idx ^ i ^ 1) * half, half), half), :], gain_ref[...])
 
     def mlp_step(step, carry):
         slot = step % 2
@@ -269,7 +278,9 @@
         u = u_ref[...]
         gate = dot(u, wg_buf[slot])
         hidden = (gate * jax.nn.sigmoid(gate) * dot(u, wu_buf[slot])).astype(BF16)
-        acc_ref[...] += dot(hidden, wd_buf[slot])
+        added = dot(hidden, wd_buf[slot])
+        send_ref[...] += added[:half, :]
+        keep_ref[...] += added[half:, :]
 
         @pl.when(step + 2 < mlp_steps)
         def _():
@@ -278,8 +289,6 @@
         return carry
 
     lax.fori_loop(0, mlp_steps, mlp_step, 0)
-    send_ref[...] = acc_ref[:half, :]
-    keep_ref[...] = mid_ref[own, :] + acc_ref[half:, :]
 
 
 def chunk_layer(x, chunk, attn_mine, attn_peer, wo_mine, wo_pieces, gain, w_gate, w_up, w_down):
@@ -293,7 +302,7 @@
         functools.partial(chunk_kernel, pieces), name="chunk_layer", grid=(1,),
         in_specs=[pl.BlockSpec((rows, dim), lambda i: (chunk, 0)), whole(rows, depth), whole(rows, depth), whole(1, dim)] + [raw] * (pieces + 4),
         out_specs=[whole(rows // 2, dim)] * 2,
-        scratch_shapes=[pltpu.VMEM((rows, dim), F32), pltpu.VMEM((rows, dim), BF16), pltpu.VMEM((rows, dim), F32),
+        scratch_shapes=[pltpu.VMEM((rows, dim), F32), pltpu.VMEM((rows, dim), BF16),
                         pltpu.VMEM((2, depth, width), BF16), pltpu.VMEM((2, depth, width), BF16),
                         pltpu.VMEM((2, dim, FF_BLOCK), BF16), pltpu.VMEM((2, dim, FF_BLOCK), BF16), pltpu.VMEM((2, FF_BLOCK, dim), BF16),
                         pltpu.SemaphoreType.DMA((2, HEAD_GROUPS + pieces)), pltpu.SemaphoreType.DMA((2, 3))],
@@ -390,7 +399,8 @@
         late_w_o, u = lax.optimization_barrier((w_o, u))
         wo_b = lax.ppermute(wo_rows(sp_idx, 1, late_w_o), "tp", tp_swap)
         wo_far = lax.ppermute(wo_rows(sp_idx ^ 2, 1, late_w_o), "tp", tp_swap)
-        q_rot = project_q(u, w_q, cos_t, sin_t)
+        chunk_rows = rows_local // CHUNKS
+        q_rot = project_q(u, w_q, cos_t, sin_t, 0, rows_local)
         wo_near = lax.ppermute(wo_a, "sp", chip_swap)
         wo_core = [lax.ppermute(piece, "sp", core_swap) for piece in
                    (wo_a, wo_b, wo_near, wo_far)]
@@ -405,17 +415,16 @@
             cols = [lax.dynamic_slice(part, (0, offset + sp_idx * HEAD_DIM), (rows_local, HEAD_DIM)) for part in kv_parts]
             return ordered(*cols).reshape(sp_size * rows_local, 1, HEAD_DIM)
 
-        chunk_rows = rows_local // CHUNKS
         attn_flops = 4 * chunk_rows * sp_size * rows_local * w_q.shape[1] // 4
         split = CHUNKS // 2
-        partial_sums = attention(meta, q_rot, kv_parts[:2], 0, split * chunk_rows, 512, attn_flops, False)
+        partial_sums = attention(meta, q_rot, 0, kv_parts[:2], 0, split * chunk_rows, split * chunk_rows, 512, attn_flops, False)
         attn_mine, attn_peer = [], []
         for c in range(CHUNKS):
             if c < split:
-                rest = (kv_parts[2:], c * chunk_rows, chunk_rows, 1024, attn_flops, True, partial_sums)
+                rest = (kv_parts[2:], c * chunk_rows, chunk_rows, chunk_rows, 1024, attn_flops, True, partial_sums)
             else:
-                rest = (kv_parts, c * chunk_rows, chunk_rows, 1024, attn_flops)
-            attn_mine.append(attention(meta, q_rot, *rest))
+                rest = (kv_parts, c * chunk_rows, chunk_rows, chunk_rows, 1024, attn_flops)
+            attn_mine.append(attention(meta, q_rot, c * chunk_rows, *rest))
             attn_peer.append(lax.ppermute(attn_mine[c], "tp", tp_swap))
         k_cache, v_cache = cache(0), cache(w_k.shape[1])
         y_out = unwritten((rows_local, dim), BF16)

time: 469 us -> 466 us (level); the launches traced: 460 us -> 466 us
  Pallas kernels: 288 us -> 293 us
where the time goes in v5:
time: 466 us
  Pallas kernels  293 us (63%)
  waiting for transfers between devices  101 us (22%)
  starting transfers between devices  52.8 us (11%)
  other arithmetic  8.67 us (2%)
  local copies, waits for them, and re-layouts  7.47 us (2%)
    pallas_call x4, Pallas kernels, chunk_layer(): pl.pallas_call(functools.partial(chunk_kernel, pieces), name='chunk_layer...  152 us
    pallas_call x5, Pallas kernels, attention(): pl.pallas_call(functools.partial(attn_kernel, group, row_base, parts, k_b...  94.5 us
    ppermute x4, waiting for transfers between devices, layer(): y_peer.append(lax.ppermute(y_own, 'tp', tp_swap))  40.7 us
    ppermute x1, starting transfers between devices, layer(): cut = (zeros + lax.ppermute(zeros, 'sp', chip_swap))[0]  35.3 us
    ppermute x4, waiting for transfers between devices, layer(): sent.append(lax.ppermute(p_peer, 'tp', tp_swap))  25 us
    ppermute x1, waiting for transfers between devices, layer(): wo_b = lax.ppermute(wo_rows(sp_idx, 1, late_w_o), 'tp', tp_swap)  24.1 us
    pallas_call x1, Pallas kernels, project_q(): pl.pallas_call(q_kernel, grid=(width // block,), name='project_q', in_spe...  16.1 us
    pallas_call x1, Pallas kernels, project_kv(): pl.pallas_call(kv_kernel, grid=(rows // block,), name='project_kv', in_sp...  13 us
  transfers between devices with their start and end apart: 25, of which 6 were waited for; matrix products, arithmetic and copies ran while one was open for 2% of the time, Pallas kernels for 59%

profile of v5, /device:TPU:2, one launch (start us, length us, event | category | flops | bytes accessed | tf_op | source)
XLA Modules:
  0.0 465.8 jit_solution(2608118037898682106)
XLA Ops:
  4.0 13.0 %project_kv.1 = (bf16[1024,3072]{1,0:T(8,128)(2,1)}, bf16[1024,1024]{1,0:T(8,128)(2,1)}) custom-call(bf16[1024,3072]{1,0:T(8,128)(2,1)} %x_ref.9, f32[1,3072]{1,0:T(1,128)S(1)} %bitcast.10, bf16[3072,512]{1,0:T(8,128)(2,1)} %wk_ref.1, bf16[3072,512]{1,0:T(8,128)(2,1)} %wv_ref.1, f32[1024,128]{1,0:T(8,128)S(1)} %get-tuple-element.64.cos_ref, ...), custom_call_target="tpu_custom_call" | custom-call | flops 6442450944 | bytes 18874368 | tf_op jit(solution)/shard_map/project_kv/pallas_call | solution.py:66
  17.1 2.4 constant_dynamic-slice_fusion.2
  19.5 2.0 collective-permute-start.6
  27.2 35.3 %collective-permute-start.1 = (s32[1]{0:T(128)}, s32[1]{0:T(128)}, u32[]{:S(2)}, u32[]{:S(2)}) collective-permute-start(s32[1]{0:T(128)} %add.45), channel_id=1, source_target_pairs={{0,2},{1,3},{2,0},{3,1},{4,6},{5,7},{6,4},{7,5}} | collective-permute-start | bytes 20 | tf_op jit(solution)/shard_map/ppermute | solution.py:388
  62.6 2.2 collective-permute-done.1
  66.8 7.1 %collective-permute-done.11.refs_5_ = bf16[192,3072]{1,0:T(8,128)(2,1)} collective-permute-done((bf16[192,3072]{1,0:T(8,128)(2,1)S(1)}, bf16[192,3072]{1,0:T(8,128)(2,1)}, u32[]{:S(2)}, u32[]{:S(2)}) %collective-permute-start.11) | collective-permute-done | bytes 1179680 | tf_op jit(solution)/shard_map/ppermute | solution.py:401
  73.9 24.1 %collective-permute-done.7.refs_1_ = bf16[192,3072]{1,0:T(8,128)(2,1)} collective-permute-done((bf16[192,3072]{1,0:T(8,128)(2,1)S(1)}, bf16[192,3072]{1,0:T(8,128)(2,1)}, u32[]{:S(2)}, u32[]{:S(2)}) %collective-permute-start.7) | collective-permute-done | bytes 1179680 | tf_op jit(solution)/shard_map/ppermute | solution.py:400
  98.6 16.1 %project_q.1.q_ref = bf16[1024,1536]{1,0:T(8,128)(2,1)S(1)} custom-call(bf16[1024,3072]{1,0:T(8,128)(2,1)} %get-tuple-element.27.u_ref, bf16[3072,1536]{1,0:T(8,128)(2,1)} %w_ref.1, f32[1024,128]{1,0:T(8,128)S(1)} %get-tuple-element.64.cos_ref, f32[1024,128]{1,0:T(8,128)S(1)} %get-tuple-element.63.sin_ref), custom_call_target="tpu_custom_call" | custom-call | flops 9663676416 | bytes 15728640 | tf_op jit(solution)/shard_map/project_q/pallas_call | solution.py:89
  117.1 23.6 %attention.6.a_ref = bf16[256,1536]{1,0:T(8,128)(2,1)S(1)} custom-call(s32[4]{0:T(128)S(1)} %pad_add_fusion.meta_ref, bf16[1024,1536]{1,0:T(8,128)(2,1)} %copy-done.2, bf16[1024,1024]{1,0:T(8,128)(2,1)} %get-tuple-element.28.refs_0_.refs_4_.refs_2_, bf16[1024,1024]{1,0:T(8,128)(2,1)} %collective-permute-done.2.refs_1_.refs_5_.refs_3_, ...), custom_call_target="tpu_custom_call" | custom-call | flops 1610612736 | bytes 16777216 | tf_op jit(solution)/shard_map/attention/pallas_call | solution.py:194
  142.5 11.5 %attention.7 = (f32[12,128,512]{2,1,0:T(8,128)}, f32[12,1,512]{2,1,0:T(1,128)S(1)}, f32[12,1,512]{2,1,0:T(1,128)S(1)}) custom-call(s32[4]{0:T(128)S(1)} %pad_add_fusion.meta_ref, bf16[1024,1536]{1,0:T(8,128)(2,1)} %copy-done.2, bf16[1024,1024]{1,0:T(8,128)(2,1)} %get-tuple-element.28.refs_0_.refs_4_.refs_2_, ...), custom_call_target="tpu_custom_call" | custom-call | flops 1610612736 | bytes 16777216 | tf_op jit(solution)/shard_map/attention/pallas_call | solution.py:194
  154.0 27.0 %attention.5.a_ref = bf16[256,1536]{1,0:T(8,128)(2,1)S(1)} custom-call(s32[4]{0:T(128)S(1)} %pad_add_fusion.meta_ref, bf16[1024,1536]{1,0:T(8,128)(2,1)} %copy-done.2, bf16[1024,1024]{1,0:T(8,128)(2,1)} %get-tuple-element.28.refs_0_.refs_4_.refs_2_, bf16[1024,1024]{1,0:T(8,128)(2,1)} %collective-permute-done.2.refs_1_.refs_5_.refs_3_, ...), custom_call_target="tpu_custom_call" | custom-call | flops 1610612736 | bytes 16777216 | tf_op jit(solution)/shard_map/attention/pallas_call | solution.py:194
  181.0 16.2 %attention.9.a_ref = bf16[256,1536]{1,0:T(8,128)(2,1)} custom-call(s32[4]{0:T(128)S(1)} %pad_add_fusion.meta_ref, bf16[1024,1536]{1,0:T(8,128)(2,1)} %copy-done.2, bf16[1024,1024]{1,0:T(8,128)(2,1)S(1)} %copy-done.1, bf16[1024,1024]{1,0:T(8,128)(2,1)} %collective-permute-done.4.refs_3_.refs_7_.refs_1_, bf16[1024,1024]{1,0:T(8,128)(2,1)S(1)} %copy-done.1, ...), custom_call_target="tpu_custom_call" | custom-call | flops 1610612736 | bytes 16777216 | tf_op jit(solution)/shard_map/attention/pallas_call | solution.py:194
  197.3 16.2 %attention.8.a_ref = bf16[256,1536]{1,0:T(8,128)(2,1)} custom-call(s32[4]{0:T(128)S(1)} %pad_add_fusion.meta_ref, bf16[1024,1536]{1,0:T(8,128)(2,1)} %copy-done.2, bf16[1024,1024]{1,0:T(8,128)(2,1)S(1)} %copy-done.1, bf16[1024,1024]{1,0:T(8,128)(2,1)} %collective-permute-done.4.refs_3_.refs_7_.refs_1_, bf16[1024,1024]{1,0:T(8,128)(2,1)S(1)} %copy-done.1, ...), custom_call_target="tpu_custom_call" | custom-call | flops 1610612736 | bytes 16777216 | tf_op jit(solution)/shard_map/attention/pallas_call | solution.py:194
  216.7 37.8 %chunk_layer.5 = (f32[128,3072]{1,0:T(8,128)}, f32[128,3072]{1,0:T(8,128)}) custom-call(bf16[1024,3072]{1,0:T(8,128)(2,1)} %x_ref.9, bf16[256,1536]{1,0:T(8,128)(2,1)} %copy-done.4, bf16[256,1536]{1,0:T(8,128)(2,1)} %copy-done.10, f32[1,3072]{1,0:T(1,128)} %bitcast.11, bf16[1536,3072]{1,0:T(8,128)(2,1)} %wo_ref.7, ...), custom_call_target="tpu_custom_call" | custom-call | flops 24159191040 | bytes 75497472 | tf_op jit(solution)/shard_map/chunk_layer/pallas_call | solution.py:301
  256.3 37.9 %chunk_layer.6 = (f32[128,3072]{1,0:T(8,128)}, f32[128,3072]{1,0:T(8,128)}) custom-call(bf16[1024,3072]{1,0:T(8,128)(2,1)} %x_ref.9, bf16[256,1536]{1,0:T(8,128)(2,1)} %attention.8.a_ref, bf16[256,1536]{1,0:T(8,128)(2,1)} %collective-permute-done.17.b_ref, f32[1,3072]{1,0:T(1,128)} %bitcast.12, bf16[1536,3072]{1,0:T(8,128)(2,1)} %wo_ref.7, ...), custom_call_target="tpu_custom_call" | custom-call | flops 24159191040 | bytes 75497472 | tf_op jit(solution)/shard_map/chunk_layer/pallas_call | solution.py:301
  294.5 38.0 %chunk_layer.7 = (f32[128,3072]{1,0:T(8,128)}, f32[128,3072]{1,0:T(8,128)}) custom-call(bf16[1024,3072]{1,0:T(8,128)(2,1)} %x_ref.9, bf16[256,1536]{1,0:T(8,128)(2,1)} %attention.9.a_ref, bf16[256,1536]{1,0:T(8,128)(2,1)} %collective-permute-done.19.b_ref, f32[1,3072]{1,0:T(1,128)} %bitcast.13, bf16[1536,3072]{1,0:T(8,128)(2,1)} %wo_ref.7, ...), custom_call_target="tpu_custom_call" | custom-call | flops 24159191040 | bytes 75497472 | tf_op jit(solution)/shard_map/chunk_layer/pallas_call | solution.py:301
  334.3 37.9 %chunk_layer.4 = (f32[128,3072]{1,0:T(8,128)}, f32[128,3072]{1,0:T(8,128)}) custom-call(bf16[1024,3072]{1,0:T(8,128)(2,1)} %x_ref.9, bf16[256,1536]{1,0:T(8,128)(2,1)} %copy-done.3, bf16[256,1536]{1,0:T(8,128)(2,1)} %collective-permute-done.5.b_ref, f32[1,3072]{1,0:T(1,128)} %bitcast.14, bf16[1536,3072]{1,0:T(8,128)(2,1)} %wo_ref.7, ...), custom_call_target="tpu_custom_call" | custom-call | flops 24159191040 | bytes 75497472 | tf_op jit(solution)/shard_map/chunk_layer/pallas_call | solution.py:301
  375.5 3.1 finish_rows.4
  378.6 3.1 finish_rows.5
  381.7 3.1 finish_rows.6
  384.7 25.0 %collective-permute-done.14.sent_ref = f32[128,3072]{1,0:T(8,128)} collective-permute-done((f32[128,3072]{1,0:T(8,128)}, f32[128,3072]{1,0:T(8,128)}, u32[]{:S(2)}, u32[]{:S(2)}) %collective-permute-start.14) | collective-permute-done | bytes 1572896 | tf_op jit(solution)/shard_map/ppermute | solution.py:436
  409.8 3.1 finish_rows.7
  412.8 2.0 collective-permute-start.22
  419.2 40.7 %collective-permute-done.24.piece_ref = bf16[128,3072]{1,0:T(8,128)(2,1)S(1)} collective-permute-done((bf16[128,3072]{1,0:T(8,128)(2,1)S(1)}, bf16[128,3072]{1,0:T(8,128)(2,1)S(1)}, u32[]{:S(2)}, u32[]{:S(2)}) %collective-permute-start.24) | collective-permute-done | bytes 786464 | tf_op jit(solution)/shard_map/ppermute | solution.py:441
  (84 shorter events, 34.6 us)
Async XLA Ops:
  17.1 49.8 %collective-permute-start.3 = (bf16[1024,1024]{1,0:T(8,128)(2,1)}, bf16[1024,1024]{1,0:T(8,128)(2,1)S(1)}, u32[]{:S(2)}, u32[]{:S(2)}) collective-permute-start(bf16[1024,1024]{1,0:T(8,128)(2,1)} %get-tuple-element.28.refs_0_.refs_4_.refs_2_), channel_id=1, source_target_pairs={{0,2},{1,3},{2,0},{3,1},{4,6},{5,7},{6,4},{7,5}} | collective-permute-start | bytes 6291464 | tf_op jit(solution)/shard_map/ppermute | solution.py:394
  19.5 46.8 %collective-permute-start.6 = (bf16[192,3072]{1,0:T(8,128)(2,1)}, bf16[192,3072]{1,0:T(8,128)(2,1)}, u32[]{:S(2)}, u32[]{:S(2)}) collective-permute-start(bf16[192,3072]{1,0:T(8,128)(2,1)} %constant_dynamic-slice_fusion.2), channel_id=1, source_target_pairs={{0,4},{4,0},{1,5},{5,1},{2,6},{6,2},{3,7},{7,3}} | collective-permute-start | bytes 3538952 | tf_op jit(solution)/shard_map/ppermute | solution.py:384
  21.5 76.6 %collective-permute-start.2 = (bf16[1024,1024]{1,0:T(8,128)(2,1)}, bf16[1024,1024]{1,0:T(8,128)(2,1)}, u32[]{:S(2)}, u32[]{:S(2)}) collective-permute-start(bf16[1024,1024]{1,0:T(8,128)(2,1)} %get-tuple-element.28.refs_0_.refs_4_.refs_2_), channel_id=1, source_target_pairs={{0,1},{1,0},{2,3},{3,2},{4,5},{5,4},{6,7},{7,6}} | collective-permute-start | bytes 6291464 | tf_op jit(solution)/shard_map/ppermute | solution.py:395
  24.4 49.5 %collective-permute-start.11 = (bf16[192,3072]{1,0:T(8,128)(2,1)S(1)}, bf16[192,3072]{1,0:T(8,128)(2,1)}, u32[]{:S(2)}, u32[]{:S(2)}) collective-permute-start(bf16[192,3072]{1,0:T(8,128)(2,1)S(1)} %get-tuple-element.49), channel_id=1, source_target_pairs={{0,4},{4,0},{1,5},{5,1},{2,6},{6,2},{3,7},{7,3}} | collective-permute-start | bytes 3538952 | tf_op jit(solution)/shard_map/ppermute | solution.py:401
  27.2 37.5 %collective-permute-start.1 = (s32[1]{0:T(128)}, s32[1]{0:T(128)}, u32[]{:S(2)}, u32[]{:S(2)}) collective-permute-start(s32[1]{0:T(128)} %add.45), channel_id=1, source_target_pairs={{0,2},{1,3},{2,0},{3,1},{4,6},{5,7},{6,4},{7,5}} | collective-permute-start | bytes 20 | tf_op jit(solution)/shard_map/ppermute | solution.py:388
  64.8 33.3 %collective-permute-start.7 = (bf16[192,3072]{1,0:T(8,128)(2,1)S(1)}, bf16[192,3072]{1,0:T(8,128)(2,1)}, u32[]{:S(2)}, u32[]{:S(2)}) collective-permute-start(bf16[192,3072]{1,0:T(8,128)(2,1)S(1)} %get-tuple-element.50), channel_id=1, source_target_pairs={{0,4},{4,0},{1,5},{5,1},{2,6},{6,2},{3,7},{7,3}} | collective-permute-start | bytes 3538952 | tf_op jit(solution)/shard_map/ppermute | solution.py:400
  66.3 32.3 %collective-permute-start.10 = (bf16[192,3072]{1,0:T(8,128)(2,1)}, bf16[192,3072]{1,0:T(8,128)(2,1)}, u32[]{:S(2)}, u32[]{:S(2)}) collective-permute-start(bf16[192,3072]{1,0:T(8,128)(2,1)} %collective-permute-done.6.refs_0_), channel_id=1, source_target_pairs={{0,2},{1,3},{2,0},{3,1},{4,6},{5,7},{6,4},{7,5}} | collective-permute-start | bytes 3538952 | tf_op jit(solution)/shard_map/ppermute | solution.py:404
  66.8 50.3 %collective-permute-start.4 = (bf16[1024,1024]{1,0:T(8,128)(2,1)S(1)}, bf16[1024,1024]{1,0:T(8,128)(2,1)}, u32[]{:S(2)}, u32[]{:S(2)}) collective-permute-start(bf16[1024,1024]{1,0:T(8,128)(2,1)S(1)} %collective-permute-done.3.refs_2_.refs_6_.refs_0_), channel_id=1, source_target_pairs={{0,1},{1,0},{2,3},{3,2},{4,5},{5,4},{6,7},{7,6}} | collective-permute-start | bytes 6291464 | tf_op jit(solution)/shard_map/ppermute | solution.py:396
  73.9 139.5 %collective-permute-start.8 = (bf16[192,3072]{1,0:T(8,128)(2,1)}, bf16[192,3072]{1,0:T(8,128)(2,1)}, u32[]{:S(2)}, u32[]{:S(2)}) collective-permute-start(bf16[192,3072]{1,0:T(8,128)(2,1)} %collective-permute-done.6.refs_0_), channel_id=1, source_target_pairs={{0,1},{1,0},{2,3},{3,2},{4,5},{5,4},{6,7},{7,6}} | collective-permute-start | bytes 3538952 | tf_op jit(solution)/shard_map/ppermute | solution.py:405
  98.1 115.7 %collective-permute-start.13 = (bf16[192,3072]{1,0:T(8,128)(2,1)}, bf16[192,3072]{1,0:T(8,128)(2,1)}, u32[]{:S(2)}, u32[]{:S(2)}) collective-permute-start(bf16[192,3072]{1,0:T(8,128)(2,1)} %collective-permute-done.11.refs_5_), channel_id=1, source_target_pairs={{0,1},{1,0},{2,3},{3,2},{4,5},{5,4},{6,7},{7,6}} | collective-permute-start | bytes 3538952 | tf_op jit(solution)/shard_map/ppermute | solution.py:405
  98.1 117.4 %collective-permute-start.9 = (bf16[192,3072]{1,0:T(8,128)(2,1)}, bf16[192,3072]{1,0:T(8,128)(2,1)}, u32[]{:S(2)}, u32[]{:S(2)}) collective-permute-start(bf16[192,3072]{1,0:T(8,128)(2,1)} %collective-permute-done.7.refs_1_), channel_id=1, source_target_pairs={{0,1},{1,0},{2,3},{3,2},{4,5},{5,4},{6,7},{7,6}} | collective-permute-start | bytes 3538952 | tf_op jit(solution)/shard_map/ppermute | solution.py:405
  98.6 117.2 %collective-permute-start.12 = (bf16[192,3072]{1,0:T(8,128)(2,1)}, bf16[192,3072]{1,0:T(8,128)(2,1)}, u32[]{:S(2)}, u32[]{:S(2)}) collective-permute-start(bf16[192,3072]{1,0:T(8,128)(2,1)} %collective-permute-done.10.refs_4_), channel_id=1, source_target_pairs={{0,1},{1,0},{2,3},{3,2},{4,5},{5,4},{6,7},{7,6}} | collective-permute-start | bytes 3538952 | tf_op jit(solution)/shard_map/ppermute | solution.py:405
  140.7 75.1 %collective-permute-start.15 = (bf16[256,1536]{1,0:T(8,128)(2,1)S(1)}, bf16[256,1536]{1,0:T(8,128)(2,1)S(1)}, u32[]{:S(2)}, u32[]{:S(2)}) collective-permute-start(bf16[256,1536]{1,0:T(8,128)(2,1)S(1)} %attention.6.a_ref), channel_id=1, source_target_pairs={{0,4},{4,0},{1,5},{5,1},{2,6},{6,2},{3,7},{7,3}} | collective-permute-start | bytes 2359304 | tf_op jit(solution)/shard_map/ppermute | solution.py:428
  213.4 120.8 %collective-permute-start.5 = (bf16[256,1536]{1,0:T(8,128)(2,1)S(1)}, bf16[256,1536]{1,0:T(8,128)(2,1)}, u32[]{:S(2)}, u32[]{:S(2)}) collective-permute-start(bf16[256,1536]{1,0:T(8,128)(2,1)S(1)} %attention.5.a_ref), channel_id=1, source_target_pairs={{0,4},{4,0},{1,5},{5,1},{2,6},{6,2},{3,7},{7,3}} | collective-permute-start | bytes 2359304 | tf_op jit(solution)/shard_map/ppermute | solution.py:428
  213.8 42.5 %collective-permute-start.17 = (bf16[256,1536]{1,0:T(8,128)(2,1)}, bf16[256,1536]{1,0:T(8,128)(2,1)}, u32[]{:S(2)}, u32[]{:S(2)}) collective-permute-start(bf16[256,1536]{1,0:T(8,128)(2,1)} %attention.8.a_ref), channel_id=1, source_target_pairs={{0,4},{4,0},{1,5},{5,1},{2,6},{6,2},{3,7},{7,3}} | collective-permute-start | bytes 2359304 | tf_op jit(solution)/shard_map/ppermute | solution.py:428
  215.5 79.0 %collective-permute-start.19 = (bf16[256,1536]{1,0:T(8,128)(2,1)}, bf16[256,1536]{1,0:T(8,128)(2,1)}, u32[]{:S(2)}, u32[]{:S(2)}) collective-permute-start(bf16[256,1536]{1,0:T(8,128)(2,1)} %attention.9.a_ref), channel_id=1, source_target_pairs={{0,4},{4,0},{1,5},{5,1},{2,6},{6,2},{3,7},{7,3}} | collective-permute-start | bytes 2359304 | tf_op jit(solution)/shard_map/ppermute | solution.py:428
  254.5 127.2 %collective-permute-start.16 = (f32[128,3072]{1,0:T(8,128)}, f32[128,3072]{1,0:T(8,128)}, u32[]{:S(2)}, u32[]{:S(2)}) collective-permute-start(f32[128,3072]{1,0:T(8,128)} %get-tuple-element.33), channel_id=1, source_target_pairs={{0,4},{4,0},{1,5},{5,1},{2,6},{6,2},{3,7},{7,3}} | collective-permute-start | bytes 4718600 | tf_op jit(solution)/shard_map/ppermute | solution.py:436
  294.2 84.4 %collective-permute-start.18 = (f32[128,3072]{1,0:T(8,128)}, f32[128,3072]{1,0:T(8,128)}, u32[]{:S(2)}, u32[]{:S(2)}) collective-permute-start(f32[128,3072]{1,0:T(8,128)} %get-tuple-element.38), channel_id=1, source_target_pairs={{0,4},{4,0},{1,5},{5,1},{2,6},{6,2},{3,7},{7,3}} | collective-permute-start | bytes 4718600 | tf_op jit(solution)/shard_map/ppermute | solution.py:436
  332.5 43.0 %collective-permute-start.20 = (f32[128,3072]{1,0:T(8,128)}, f32[128,3072]{1,0:T(8,128)}, u32[]{:S(2)}, u32[]{:S(2)}) collective-permute-start(f32[128,3072]{1,0:T(8,128)} %get-tuple-element.40), channel_id=1, source_target_pairs={{0,4},{4,0},{1,5},{5,1},{2,6},{6,2},{3,7},{7,3}} | collective-permute-start | bytes 4718600 | tf_op jit(solution)/shard_map/ppermute | solution.py:436
  372.2 37.6 %collective-permute-start.14 = (f32[128,3072]{1,0:T(8,128)}, f32[128,3072]{1,0:T(8,128)}, u32[]{:S(2)}, u32[]{:S(2)}) collective-permute-start(f32[128,3072]{1,0:T(8,128)} %get-tuple-element.31), channel_id=1, source_target_pairs={{0,4},{4,0},{1,5},{5,1},{2,6},{6,2},{3,7},{7,3}} | collective-permute-start | bytes 4718600 | tf_op jit(solution)/shard_map/ppermute | solution.py:436
  412.8 51.5 %collective-permute-start.21 = (bf16[128,3072]{1,0:T(8,128)(2,1)S(1)}, bf16[128,3072]{1,0:T(8,128)(2,1)S(1)}, u32[]{:S(2)}, u32[]{:S(2)}) collective-permute-start(bf16[128,3072]{1,0:T(8,128)(2,1)S(1)} %get-tuple-element.44), channel_id=1, source_target_pairs={{0,4},{4,0},{1,5},{5,1},{2,6},{6,2},{3,7},{7,3}} | collective-permute-start | bytes 2359304 | tf_op jit(solution)/shard_map/ppermute | solution.py:441
  412.8 50.0 %collective-permute-start.22 = (bf16[128,3072]{1,0:T(8,128)(2,1)S(1)}, bf16[128,3072]{1,0:T(8,128)(2,1)S(1)}, u32[]{:S(2)}, u32[]{:S(2)}) collective-permute-start(bf16[128,3072]{1,0:T(8,128)(2,1)S(1)} %get-tuple-element.45), channel_id=1, source_target_pairs={{0,4},{4,0},{1,5},{5,1},{2,6},{6,2},{3,7},{7,3}} | collective-permute-start | bytes 2359304 | tf_op jit(solution)/shard_map/ppermute | solution.py:441
  414.9 46.5 %collective-permute-start.23 = (bf16[128,3072]{1,0:T(8,128)(2,1)S(1)}, bf16[128,3072]{1,0:T(8,128)(2,1)S(1)}, u32[]{:S(2)}, u32[]{:S(2)}) collective-permute-start(bf16[128,3072]{1,0:T(8,128)(2,1)S(1)} %get-tuple-element.46), channel_id=1, source_target_pairs={{0,4},{4,0},{1,5},{5,1},{2,6},{6,2},{3,7},{7,3}} | collective-permute-start | bytes 2359304 | tf_op jit(solution)/shard_map/ppermute | solution.py:441
  414.9 45.0 %collective-permute-start.24 = (bf16[128,3072]{1,0:T(8,128)(2,1)S(1)}, bf16[128,3072]{1,0:T(8,128)(2,1)S(1)}, u32[]{:S(2)}, u32[]{:S(2)}) collective-permute-start(bf16[128,3072]{1,0:T(8,128)(2,1)S(1)} %get-tuple-element.47), channel_id=1, source_target_pairs={{0,4},{4,0},{1,5},{5,1},{2,6},{6,2},{3,7},{7,3}} | collective-permute-start | bytes 2359304 | tf_op jit(solution)/shard_map/ppermute | solution.py:441
  (13 other events, 168.2 us)
